TPU v7x, 16 devices: a 4x2x1 block of a 4x4x8 slice. The times are simulated.
16 devices in a mesh: rep: 2 (over y, z), dp: 8 (over x, core).
Axes of the slice: x: 4, y: 2, z: 1, core: 2. Of those that a mesh axis runs over, the one named last changes fastest.
The devices are a block of a 4x4x8 slice.
Arguments:
- x: bfloat16 [16, 2048, 640], P(('rep', 'dp')), parts along dimension 0
- dy: bfloat16 [16, 2048, 640], P(('rep', 'dp')), parts along dimension 0
- w_gate: bfloat16 [2, 640, 3200], replicated
- w_up: bfloat16 [2, 640, 3200], replicated
- w_down: bfloat16 [2, 3200, 640], replicated
- m_w_gate: float32 [2, 640, 3200], P(None, 'dp')
- m_w_up: float32 [2, 640, 3200], P(None, 'dp')
- m_w_down: float32 [2, 3200, 640], P(None, 'dp')
- v_w_gate: float32 [2, 640, 3200], P(None, 'dp')
- v_w_up: float32 [2, 640, 3200], P(None, 'dp')
- v_w_down: float32 [2, 3200, 640], P(None, 'dp')
Outputs:
- output 1: bfloat16 [4, 640, 3200], P('rep'), parts along dimension 0
- output 2: bfloat16 [4, 640, 3200], P('rep'), parts along dimension 0
- output 3: bfloat16 [4, 3200, 640], P('rep'), parts along dimension 0
- output 4: float32 [4, 640, 3200], P('rep', 'dp'), parts along dimension 0
- output 5: float32 [4, 640, 3200], P('rep', 'dp'), parts along dimension 0
- output 6: float32 [4, 3200, 640], P('rep', 'dp'), parts along dimension 0
- output 7: float32 [4, 640, 3200], P('rep', 'dp'), parts along dimension 0
- output 8: float32 [4, 640, 3200], P('rep', 'dp'), parts along dimension 0
- output 9: float32 [4, 3200, 640], P('rep', 'dp'), parts along dimension 0
There are 2 independent parts. A program takes and returns all parts, laid end to end along the dimension named above; an argument that names none is the same for every part.
All inputs are finite; a program needn't handle non-finite values.
Results may differ from a plain program's by a relative error of at most 0.022.
Values are sent between devices in bfloat16 or wider.
A program may use at most 768 MiB of HBM per device.

v0:
```python
import jax
import jax.numpy as jnp
from jax import lax

NAMES = ("w_gate", "w_up", "w_down")


def matmul(a, w):
    return jnp.dot(a, w, preferred_element_type=jnp.float32).astype(jnp.bfloat16)


def normed(h):
    wide = h.astype(jnp.float32)
    scale = lax.rsqrt(jnp.mean(wide**2, -1, keepdims=True) + 1e-6)
    return (wide * scale).astype(jnp.bfloat16)


def layer(h, w):
    a = normed(h)
    gate = jnp.dot(a, w["w_gate"], preferred_element_type=jnp.float32)
    up = jnp.dot(a, w["w_up"], preferred_element_type=jnp.float32)
    return h + matmul((jax.nn.silu(gate) * up).astype(jnp.bfloat16), w["w_down"])


def adamw(w, m, v, g):
    m = 0.9 * m + 0.1 * g
    v = 0.95 * v + 0.05 * g * g
    step = m * lax.rsqrt(v + 1e-8) + 0.1 * w
    return (w - 0.02 * step).astype(jnp.bfloat16), m, v


def clipped(gradients, sum_of_squares, count):
    factor = jnp.minimum(1.0, 0.5 * lax.rsqrt(sum_of_squares / count + 1e-30))
    return [g * factor for g in gradients]


def stack(weights, h):
    for number in range(weights["w_gate"].shape[0]):
        h = layer(h, {name: w[number] for name, w in weights.items()})
    return h


def solution(mesh):
    groups = mesh.shape["rep"]

    def step(x, dy, *arrays):
        weights, m, v = (arrays[i : i + 3] for i in (0, 3, 6))
        x, dy = (t.reshape(groups, -1, *t.shape[1:]) for t in (x, dy))

        def of_a_group(x, dy):
            _, back = jax.vjp(lambda w: stack(w, x), dict(zip(NAMES, weights, strict=True)))
            by_weights = back(dy)[0]
            gradients = [by_weights[name].astype(jnp.float32) for name in NAMES]
            gradients = clipped(gradients, sum(jnp.sum(g * g) for g in gradients), sum(g.size for g in gradients))
            new = [adamw(w.astype(jnp.float32), m, v, g) for w, m, v, g in zip(weights, m, v, gradients, strict=True)]
            return tuple(one[which] for which in range(3) for one in new)

        return tuple(t.reshape(-1, *t.shape[2:]) for t in jax.vmap(of_a_group)(x, dy))

    return step
```

profile of v0, /device:TPU:113, one launch (start us, length us, event | category | flops | bytes accessed | tf_op | source)
XLA Modules:
  0.0 705.9 jit_solution(16295779651773664061)
XLA Ops:
  14.2 16.7 %fusion.67 = f32[2048,3200]{1,0:T(8,128)} fusion(bf16[2,640,3200]{2,1,0:T(8,128)(2,1)} %param, bf16[1,2048,640]{2,1,0:T(8,128)(2,1)S(1)} %copy-done, f32[2048]{0:T(1024)S(1)} %add_rsqrt_fusion), kind=kOutput, calls=%fused_computation.79 | convolution fusion | flops 8392540160 | bytes 32940032 | tf_op jit(solution)/vmap(jvp())/dot_general | solution.py:20
  30.9 16.6 %fusion.65 = f32[2048,3200]{1,0:T(8,128)} fusion(bf16[2,640,3200]{2,1,0:T(8,128)(2,1)} %param.3, bf16[1,2048,640]{2,1,0:T(8,128)(2,1)S(1)} %copy-done, f32[2048]{0:T(1024)S(1)} %add_rsqrt_fusion), kind=kOutput, calls=%fused_computation.77 | convolution fusion | flops 8392540160 | bytes 32940032 | tf_op jit(solution)/vmap(jvp())/dot_general | solution.py:21
  47.5 23.1 %fusion.26 = bf16[2048,3200]{1,0:T(8,128)(2,1)} fusion(f32[2048,3200]{1,0:T(8,128)} %fusion.65, f32[2048,3200]{1,0:T(8,128)} %fusion.67), kind=kLoop, calls=%fused_computation.37 | loop fusion | flops 39321600 | bytes 65536000
  70.7 13.6 %fusion.51 = (f32[2048]{0:T(1024)S(1)}, bf16[1,1,2048,640]{2,3,1,0:T(8,128)(2,1)S(1)}) fusion(bf16[2048,3200]{1,0:T(8,128)(2,1)} %fusion.26, bf16[2,3200,640]{2,1,0:T(8,128)(2,1)} %param.4, bf16[1,2048,640]{1,2,0:T(8,128)(2,1)S(1)} %copy-done.7), kind=kOutput, calls=%fused_computation.62 | convolution fusion | flops 8395159552 | bytes 22454272 | tf_op jit(solution)/vmap(jvp())/dot_general | solution.py:9
  84.4 17.2 %fusion.54 = f32[2048,3200]{1,0:T(8,128)} fusion(bf16[2,640,3200]{2,1,0:T(8,128)(2,1)} %param, bf16[1,1,2048,640]{2,3,1,0:T(8,128)(2,1)S(1)} %get-tuple-element.10, f32[2048]{0:T(1024)S(1)} %bitcast.376), kind=kOutput, calls=%fused_computation.66 | convolution fusion | flops 8392540160 | bytes 32940032 | tf_op jit(solution)/vmap(jvp())/dot_general | solution.py:20
  101.6 16.5 %fusion.58 = f32[2048,3200]{1,0:T(8,128)} fusion(bf16[2,640,3200]{2,1,0:T(8,128)(2,1)} %param.3, bf16[1,1,2048,640]{2,3,1,0:T(8,128)(2,1)S(1)} %get-tuple-element.10, f32[2048]{0:T(1024)S(1)} %bitcast.377), kind=kOutput, calls=%fused_computation.70 | convolution fusion | flops 8392540160 | bytes 32940032 | tf_op jit(solution)/vmap(jvp())/dot_general | solution.py:21
  118.0 15.5 %convolution_convert_fusion.1 = bf16[2048,3200]{1,0:T(8,128)(2,1)} fusion(bf16[2,3200,640]{2,1,0:T(8,128)(2,1)} %param.4, bf16[1,2048,640]{2,1,0:T(8,128)(2,1)S(1)} %copy-done.5), kind=kOutput, calls=%fused_computation.36 | convolution fusion | flops 8395161600 | bytes 19824640 | tf_op jit(solution)/vmap(transpose(jvp()))/dot_general | solution.py:9
  136.5 26.9 %fusion.6 = bf16[2048,3200]{1,0:T(8,128)(2,1)} fusion(f32[2048,3200]{1,0:T(8,128)} %fusion.54, f32[2048,3200]{1,0:T(8,128)} %fusion.58, bf16[2048,3200]{1,0:T(8,128)(2,1)} %convolution_convert_fusion.1), kind=kLoop, calls=%fused_computation.11 | loop fusion | flops 78643200 | bytes 78643200
  163.4 14.9 %fusion.81 = bf16[2048,640]{0,1:T(8,128)(2,1)} fusion(bf16[2048,3200]{1,0:T(8,128)(2,1)} %fusion.6, bf16[2,640,3200]{2,1,0:T(8,128)(2,1)} %param), kind=kOutput, calls=%fused_computation.91 | convolution fusion | flops 8388608000 | bytes 19824640 | tf_op jit(solution)/vmap(transpose(jvp()))/dot_general | solution.py:20
  178.3 21.4 %fusion.53 = (f32[2048]{0:T(1024)S(1)}, bf16[1,1,2048,640]{2,3,1,0:T(8,128)(2,1)}) fusion(bf16[1,1,2048,640]{2,3,1,0:T(8,128)(2,1)} %copy-done.1, bf16[2048,640]{0,1:T(8,128)(2,1)} %fusion.81, bf16[2,640,3200]{2,1,0:T(8,128)(2,1)} %param.3, bf16[2048,3200]{1,0:T(8,128)(2,1)} %convolution_convert_fusion.1, f32[2048,3200]{1,0:T(8,128)} %fusion.54), kind=kOutput, calls=%fused_computation.64 | convolution fusion | flops 8435791872 | bytes 51290112 | tf_op jit(solution)/vmap(transpose(jvp()))/dot_general | solution.py:21
  220.2 23.1 %fusion.41 = f32[1,3200,640]{2,1,0:T(8,128)} fusion(f32[2048,3200]{1,0:T(8,128)} %fusion.58, f32[2048,3200]{1,0:T(8,128)} %fusion.54, bf16[1,2048,640]{2,1,0:T(8,128)(2,1)S(1)} %copy-done.6), kind=kOutput, calls=%fused_computation.53 | convolution fusion | flops 8427929600 | bytes 63242240 | tf_op jit(solution)/vmap(transpose(jvp()))/dot_general | solution.py:9
  245.0 15.3 %convolution_convert_fusion = bf16[2048,3200]{1,0:T(8,128)(2,1)} fusion(bf16[2048,640]{0,1:T(8,128)(2,1)S(1)} %copy-done.4, bf16[2,3200,640]{2,1,0:T(8,128)(2,1)} %param.4), kind=kOutput, calls=%fused_computation.35 | convolution fusion | flops 8395161600 | bytes 19824640 | tf_op jit(solution)/vmap(transpose(jvp()))/dot_general | solution.py:9
  260.3 20.4 %fusion.38 = f32[1,640,3200]{2,1,0:T(8,128)} fusion(bf16[2048,3200]{1,0:T(8,128)(2,1)} %convolution_convert_fusion, f32[2048,3200]{1,0:T(8,128)} %fusion.67, bf16[1,2048,640]{1,2,0:T(8,128)(2,1)} %copy, f32[2048]{0:T(1024)S(1)} %copy-done.9), kind=kOutput, calls=%fused_computation.50 | convolution fusion | flops 8431861760 | bytes 50143232 | tf_op jit(solution)/vmap(transpose(jvp()))/dot_general | solution.py:21
  282.5 19.7 %fusion.35 = f32[1,640,3200]{2,1,0:T(8,128)} fusion(bf16[2048,3200]{1,0:T(8,128)(2,1)} %convolution_convert_fusion.1, f32[2048,3200]{1,0:T(8,128)} %fusion.54, bf16[1,1,2048,640]{2,3,1,0:T(8,128)(2,1)S(1)} %copy-done.2, f32[2048]{0:T(1024)S(1)} %bitcast.379), kind=kOutput, calls=%fused_computation.49 | convolution fusion | flops 8431861760 | bytes 50143232 | tf_op jit(solution)/vmap(transpose(jvp()))/dot_general | solution.py:21
  302.3 29.5 %fusion.44 = f32[1,640,3200]{2,1,0:T(8,128)} fusion(f32[2048,3200]{1,0:T(8,128)} %fusion.67, f32[2048,3200]{1,0:T(8,128)} %fusion.65, bf16[2048,3200]{1,0:T(8,128)(2,1)} %convolution_convert_fusion, bf16[1,2048,640]{1,2,0:T(8,128)(2,1)} %copy, f32[2048]{0:T(1024)S(1)} %copy-done.9), kind=kOutput, calls=%fused_computation.54 | convolution fusion | flops 8464629760 | bytes 76357632 | tf_op jit(solution)/vmap(transpose(jvp()))/dot_general | solution.py:20
  332.0 14.7 %convolution_bitcast_fusion.1 = f32[1,640,3200]{2,1,0:T(8,128)} fusion(bf16[2048,3200]{1,0:T(8,128)(2,1)} %fusion.6, bf16[1,1,2048,640]{2,3,1,0:T(8,128)(2,1)S(1)} %copy-done.2, f32[2048]{0:T(1024)S(1)} %bitcast.380), kind=kOutput, calls=%fused_computation.52 | convolution fusion | flops 8392540160 | bytes 23928832 | tf_op jit(solution)/vmap(transpose(jvp()))/dot_general | solution.py:20
  352.3 15.9 %reduce-scatter.25.cloned.1.call-done = f32[1,80,3200]{2,1,0:T(8,128)} async-done(((f32[1,640,3200]{2,1,0:T(8,128)}), f32[1,80,3200]{2,1,0:T(8,128)}) %reduce-scatter.25.cloned.1.call-update) | async-done | bytes 1024016
  369.4 48.1 %reduce-scatter.23.cloned.1.call-done = f32[1,80,3200]{2,1,0:T(8,128)} async-done(((f32[1,640,3200]{2,1,0:T(8,128)}), f32[1,80,3200]{2,1,0:T(8,128)}) %reduce-scatter.23.cloned.1.call-update) | async-done | bytes 1024016
  419.9 47.5 %reduce-scatter.21.cloned.1.call-done = f32[1,80,3200]{2,1,0:T(8,128)} async-done(((f32[1,640,3200]{2,1,0:T(8,128)}), f32[1,80,3200]{2,1,0:T(8,128)}) %reduce-scatter.21.cloned.1.call-update) | async-done | bytes 1024016
  468.7 48.6 %reduce-scatter.19.cloned.1.call-done = f32[1,80,3200]{2,1,0:T(8,128)} async-done(((f32[1,640,3200]{2,1,0:T(8,128)}), f32[1,80,3200]{2,1,0:T(8,128)}) %reduce-scatter.19.cloned.1.call-update) | async-done | bytes 1024016
  521.7 14.0 %all-reduce.16 = f32[1]{0:T(128)} all-reduce(f32[1]{0:T(128)} %bitcast.50), channel_id=5, replica_groups=mesh['rep'=2,'dp'=8] {'dp'}, use_global_device_ids=true, to_apply=%region_3.4.clone | all-reduce | flops 1 | bytes 8 | tf_op jit(solution)/vmap()/reduce_sum | solution.py:54
  554.6 32.3 %all-gather.14.cloned.1.call-done = bf16[1,2,3200,640]{3,2,1,0:T(8,128)(2,1)} async-done(((bf16[1,2,400,640]{3,2,1,0:T(8,128)(2,1)}), bf16[1,2,3200,640]{3,2,1,0:T(8,128)(2,1)}) %all-gather.14.cloned.1.call-update) | async-done | bytes 8192016 | tf_op jit(solution)/reshape | solution.py:58
  586.9 47.0 %all-gather.12.cloned.1.call-done = bf16[1,2,640,3200]{3,2,1,0:T(8,128)(2,1)} async-done(((bf16[1,2,80,3200]{3,2,1,0:T(8,128)(2,1)}), bf16[1,2,640,3200]{3,2,1,0:T(8,128)(2,1)}) %all-gather.12.cloned.1.call-update) | async-done | bytes 8192016 | tf_op jit(solution)/reshape | solution.py:58
  633.9 47.0 %all-gather.10.cloned.1.call-done = bf16[1,2,640,3200]{3,2,1,0:T(8,128)(2,1)} async-done(((bf16[1,2,80,3200]{3,2,1,0:T(8,128)(2,1)}), bf16[1,2,640,3200]{3,2,1,0:T(8,128)(2,1)}) %all-gather.10.cloned.1.call-update) | async-done | bytes 8192016 | tf_op jit(solution)/reshape | solution.py:58
  (81 shorter events, 82.4 us)
Async XLA Ops:
  7.2 6.9 copy-start
  7.2 341.4 %reduce-scatter.29.cloned.1.call-start = ((), (), s32[]{:S(2)}) async-start(), calls=%async_computation.14 | async-start | bytes 9216000
  14.1 16.8 %copy-start.8 = (f32[2048]{0:T(1024)}, f32[2048]{0:T(1024)S(1)}, u32[]{:S(2)}) copy-start(f32[2048]{0:T(1024)S(1)} %add_rsqrt_fusion) | copy-start | bytes 24580
  47.5 23.1 %copy-start.7 = (bf16[1,2048,640]{1,2,0:T(8,128)(2,1)S(1)}, bf16[1,2048,640]{1,2,0:T(8,128)(2,1)}, u32[]{:S(2)}) copy-start(bf16[1,2048,640]{1,2,0:T(8,128)(2,1)} %copy) | copy-start | bytes 7864324
  84.3 17.3 %copy-start.1 = (bf16[1,1,2048,640]{2,3,1,0:T(8,128)(2,1)}, bf16[1,1,2048,640]{2,3,1,0:T(8,128)(2,1)S(1)}, u32[]{:S(2)}) copy-start(bf16[1,1,2048,640]{2,3,1,0:T(8,128)(2,1)S(1)} %get-tuple-element.10) | copy-start | bytes 7864324
  101.6 16.5 %copy-start.5 = (bf16[1,2048,640]{2,1,0:T(8,128)(2,1)S(1)}, bf16[1,2048,640]{2,1,0:T(8,128)(2,1)}, u32[]{:S(2)}) copy-start(bf16[1,2048,640]{2,1,0:T(8,128)(2,1)} %param.5) | copy-start | bytes 7864324
  163.4 42.2 %slice-start = ((s8[13107200]{0:T(1024)(128)(4,1)}), s8[4194304]{0:T(1024)(128)(4,1)S(1)}, s32[]{:S(2)}) async-start(s8[13107200]{0:T(1024)(128)(4,1)} %bitcast.366), calls=%async_computation.15 | async-start | bytes 8388608
  178.3 27.3 %slice-start.1 = ((s8[13107200]{0:T(1024)(128)(4,1)}), s8[4194304]{0:T(1024)(128)(4,1)S(1)}, s32[]{:S(2)}) async-start(s8[13107200]{0:T(1024)(128)(4,1)} %bitcast.366), calls=%async_computation.16 | async-start | bytes 8388608
  178.3 27.3 %slice-start.2 = ((s8[13107200]{0:T(1024)(128)(4,1)}), s8[4194304]{0:T(1024)(128)(4,1)S(1)}, s32[]{:S(2)}) async-start(s8[13107200]{0:T(1024)(128)(4,1)} %bitcast.366), calls=%async_computation.17 | async-start | bytes 8388608
  178.3 27.3 %slice-start.3 = ((s8[13107200]{0:T(1024)(128)(4,1)}), s8[524288]{0:T(1024)(128)(4,1)S(1)}, s32[]{:S(2)}) async-start(s8[13107200]{0:T(1024)(128)(4,1)} %bitcast.366), calls=%async_computation.18 | async-start | bytes 1048576
  218.4 1.7 copy-start.6
  218.5 131.4 %reduce-scatter.27.cloned.1.call-start = ((), (), s32[]{:S(2)}) async-start(), calls=%async_computation.13 | async-start | bytes 9216000
  243.3 1.7 copy-start.4
  243.4 17.0 %copy-start.9 = (f32[2048]{0:T(1024)S(1)}, f32[2048]{0:T(1024)}, u32[]{:S(2)}) copy-start(f32[2048]{0:T(1024)} %copy-done.8) | copy-start | bytes 24580
  243.4 124.8 %reduce-scatter.25.cloned.1.call-start = ((), (), s32[]{:S(2)}) async-start(), calls=%async_computation.12 | async-start | bytes 9216000
  280.7 1.7 copy-start.2
  280.8 136.7 %reduce-scatter.23.cloned.1.call-start = ((), (), s32[]{:S(2)}) async-start(), calls=%async_computation.11 | async-start | bytes 9216000
  302.2 165.2 %reduce-scatter.21.cloned.1.call-start = ((), (), s32[]{:S(2)}) async-start(), calls=%async_computation.10 | async-start | bytes 9216000
  331.9 185.5 %reduce-scatter.19.cloned.1.call-start = ((), (), s32[]{:S(2)}) async-start(), calls=%async_computation.9 | async-start | bytes 9216000
  346.7 240.1 %all-gather.14.cloned.1.call-start = ((), (), s32[]{:S(2)}) async-start(), calls=%async_computation.8 | async-start | bytes 9216000 | tf_op jit(solution)/reshape | solution.py:58
  542.4 91.4 %all-gather.12.cloned.1.call-start = ((), (), s32[]{:S(2)}) async-start(), calls=%async_computation.7 | async-start | bytes 9216000 | tf_op jit(solution)/reshape | solution.py:58
  548.5 132.3 %all-gather.10.cloned.1.call-start = ((), (), s32[]{:S(2)}) async-start(), calls=%async_computation.6 | async-start | bytes 9216000 | tf_op jit(solution)/reshape | solution.py:58
  680.9 14.7 %slice-start.4 = ((s8[8192000]{0:T(1024)(128)(4,1)}), s8[4194304]{0:T(1024)(128)(4,1)S(1)}, s32[]{:S(2)}) async-start(s8[8192000]{0:T(1024)(128)(4,1)} %bitcast.368), calls=%async_computation.19 | async-start | bytes 8388608
  688.2 7.4 %slice-start.5 = ((s8[8192000]{0:T(1024)(128)(4,1)}), s8[3997696]{0:T(1024)(128)(4,1)S(1)}, s32[]{:S(2)}) async-start(s8[8192000]{0:T(1024)(128)(4,1)} %bitcast.368), calls=%async_computation.20 | async-start | bytes 7995392
  (2 other events, 2.1 us)
Sparse Core Ops, SparseCore 0:
  218.6 49.9 reduce-scatter.28
  270.9 47.1 reduce-scatter.26
  321.0 47.1 reduce-scatter.24
  370.3 47.1 reduce-scatter.22
  420.2 47.1 reduce-scatter.20
  470.2 47.1 reduce-scatter.18
  542.6 44.2 all-gather.13
  589.0 44.7 all-gather.11
  636.0 44.7 all-gather.9
where the time goes:
time: 715 us; the launch traced here: 706 us
  waiting for transfers between devices  287 us (40%)
  matrix products  268 us (37%)
  other arithmetic  85.7 us (12%)
  local copies, waits for them, and re-layouts  32.6 us (5%)
  between operations  17.8 us (2%)
  blocking collectives  14 us (2%)
    unnamed x15, waiting for transfers between devices  161 us
    reshape x3, waiting for transfers between devices, step(): t.reshape(-1, *t.shape[2:])  126 us
    dot_general x5, matrix products, layer(): up = jnp.dot(a, w['w_up'], preferred_element_type=jnp.float32)  94.6 us
    dot_general x5, matrix products, layer(): gate = jnp.dot(a, w['w_gate'], preferred_element_type=jnp.float32)  93.1 us
    dot_general x5, matrix products, matmul(): jnp.dot(a, w, preferred_element_type=jnp.float32).astype(jnp.bfloat16)  80.4 us
    unnamed x5, other arithmetic  54.3 us
    unnamed x39, local copies, waits for them, and re-layouts  32 us
    reshape x3, other arithmetic, step(): t.reshape(-1, *t.shape[2:])  17.8 us
  transfers between devices with their start and end apart: 9, of which 7 were waited for; matrix products, arithmetic and copies ran while one was open for 20% of the time, Pallas kernels for 0%

commit v1 on v0

v1 whole, which is shorter than its diff:
```python
import jax
import jax.numpy as jnp
from jax import lax
from jax.sharding import PartitionSpec as P

NAMES = ("w_gate", "w_up", "w_down")


def matmul(a, w):
    return jnp.dot(a, w, preferred_element_type=jnp.float32).astype(jnp.bfloat16)


def normed(h):
    wide = h.astype(jnp.float32)
    scale = lax.rsqrt(jnp.mean(wide**2, -1, keepdims=True) + 1e-6)
    return (wide * scale).astype(jnp.bfloat16)


def layer(h, w):
    a = normed(h)
    gate = jnp.dot(a, w[0], preferred_element_type=jnp.float32)
    up = jnp.dot(a, w[1], preferred_element_type=jnp.float32)
    return h + matmul((jax.nn.silu(gate) * up).astype(jnp.bfloat16), w[2])


def adamw(w, m, v, g):
    m = 0.9 * m + 0.1 * g
    v = 0.95 * v + 0.05 * g * g
    step = m * lax.rsqrt(v + 1e-8) + 0.1 * w
    return (w - 0.02 * step).astype(jnp.bfloat16), m, v


def solution(mesh):
    dp = mesh.shape["dp"]

    def step(x, dy, *arrays):
        weights, m, v = (arrays[i : i + 3] for i in (0, 3, 6))
        layers = weights[0].shape[0]
        per_layer = [tuple(w[i] for w in weights) for i in range(layers)]

        def stack(per_layer, h):
            for w in per_layer:
                h = layer(h, w)
            return h

        _, back = jax.vjp(lambda w: stack(w, x[0]), per_layer)
        grads = back(dy[0])[0]
        me = lax.axis_index("dp")
        g = [[None] * layers for _ in weights]
        for i in reversed(range(layers)):
            for j in (2, 0, 1):
                g[j][i] = lax.psum_scatter(grads[i][j], "dp", scatter_dimension=0, tiled=True).astype(jnp.float32)
        total = lax.psum(sum(jnp.sum(t * t) for row in g for t in row), "dp")
        count = sum(w.size for w in weights)
        factor = jnp.minimum(1.0, 0.5 * lax.rsqrt(total / count + 1e-30))
        new_w, new_m, new_v = [], [], []
        for j, w in enumerate(weights):
            rows = m[j].shape[1]
            mine = lax.dynamic_slice_in_dim(w, me * rows, rows, 1).astype(jnp.float32)
            nw, nm, nv = adamw(mine, m[j], v[j], jnp.stack(g[j]) * factor)
            new_w.append(lax.all_gather(nw, "dp", axis=1, tiled=True))
            new_m.append(nm)
            new_v.append(nv)
        return (*new_w, *new_m, *new_v)

    whole, split = P(None, None, None), P(None, "dp", None)
    return jax.shard_map(
        step,
        mesh=mesh,
        in_specs=(P(("rep", "dp")),) * 2 + (whole,) * 3 + (split,) * 6,
        out_specs=(P("rep", None, None),) * 3 + (P("rep", "dp", None),) * 6,
        check_vma=False,
    )
```

time: 715 us -> 604 us (0.84)
  waiting for transfers between devices: 287 us -> 209 us
  other arithmetic: 85.7 us -> 31 us
  matrix products: 268 us -> 294 us
    unnamed x15 -> x9, waiting for transfers between devices: 161 us -> 0.48 us
    reshape x3 -> x0, waiting for transfers between devices: 126 us -> none  [step(): t.reshape(-1, *t.shape[2:])]
    all_gather x0 -> x3, waiting for transfers between devices: none -> 126 us  [step(): new_w.append(lax.all_gather(nw, 'dp', axis=1, tiled=True))]
    reduce_scatter x0 -> x6, waiting for transfers between devices: none -> 82.7 us  [step(): lax.psum_scatter(grads[i][j], 'dp', scatter_dimension=0, tiled=True)]
    unnamed x5 -> x1, other arithmetic: 54.3 us -> 0.01 us
    dot_general x10, matrix products: 188 us -> 208 us  [the longest x5 108 us: layer(): gate = jnp.dot(a, w[0], preferred_element_type=jnp.float32)]
    reshape x3 -> x0, other arithmetic: 17.8 us -> none  [step(): t.reshape(-1, *t.shape[2:])]
    psum x0 -> x1, blocking collectives: none -> 15.9 us  [step(): total = lax.psum(sum((jnp.sum(t * t) for row in g for t in row)), 'dp')]
  transfers between devices with their start and end apart: 9 -> 9, of which waited for: 7 -> 6; matrix products, arithmetic and copies ran while one was open for 20% -> 30% of each run, Pallas kernels for 0% -> 0%
where the time goes in v1:
time: 604 us; the launch traced here: 596 us
  matrix products  294 us (49%)
  waiting for transfers between devices  209 us (35%)
  other arithmetic  31 us (5%)
  local copies, waits for them, and re-layouts  26.8 us (4%)
  between operations  19.3 us (3%)
  blocking collectives  15.9 us (3%)
    all_gather x3, waiting for transfers between devices, step(): new_w.append(lax.all_gather(nw, 'dp', axis=1, tiled=True))  126 us
    dot_general x5, matrix products, layer(): gate = jnp.dot(a, w[0], preferred_element_type=jnp.float32)  108 us
    dot_general x5, matrix products, layer(): up = jnp.dot(a, w[1], preferred_element_type=jnp.float32)  101 us
    dot_general x5, matrix products, matmul(): jnp.dot(a, w, preferred_element_type=jnp.float32).astype(jnp.bfloat16)  85.1 us
    reduce_scatter x6, waiting for transfers between devices, step(): lax.psum_scatter(grads[i][j], 'dp', scatter_dimension=0, tiled=True)  82.7 us
    unnamed x45, local copies, waits for them, and re-layouts  26.8 us
    psum x1, blocking collectives, step(): total = lax.psum(sum((jnp.sum(t * t) for row in g for t in row)), 'dp')  15.9 us
    convert_element_type x3, other arithmetic, adamw(): return ((w - 0.02 * step).astype(jnp.bfloat16), m, v)  14.6 us
  transfers between devices with their start and end apart: 9, of which 6 were waited for; matrix products, arithmetic and copies ran while one was open for 30% of the time, Pallas kernels for 0%

profile of v1, /device:TPU:113, one launch (start us, length us, event | category | flops | bytes accessed | tf_op | source)
XLA Modules:
  0.0 596.3 jit_solution(4386627808660652532)
XLA Ops:
  10.8 18.6 %fusion.42 = f32[2048,3200]{1,0:T(8,128)} fusion(bf16[2,640,3200]{2,1,0:T(8,128)(2,1)} %param.13, bf16[1,2048,640]{2,1,0:T(8,128)(2,1)} %param.11, f32[2048]{0:T(1024)S(1)} %add_rsqrt_fusion), kind=kOutput, calls=%fused_computation.60 | convolution fusion | flops 8392540160 | bytes 32940032 | tf_op jit(solution)/shard_map/jvp()/dot_general | solution.py:21
  29.4 28.0 %multiply_convert_fusion.1 = (bf16[2048,3200]{1,0:T(8,128)(2,1)}, f32[2048,3200]{1,0:T(8,128)}) fusion(f32[2048,3200]{1,0:T(8,128)} %fusion.42, bf16[2,640,3200]{2,1,0:T(8,128)(2,1)} %param.14, bf16[1,2048,640]{2,1,0:T(8,128)(2,1)} %param.11, f32[2048]{0:T(1024)S(1)} %add_rsqrt_fusion), kind=kOutput, calls=%fused_computation.17 | convolution fusion | flops 8431861760 | bytes 72261632 | tf_op jit(solution)/shard_map/jvp()/dot_general | solution.py:22
  57.4 13.9 %fusion.25 = (f32[2048]{0:T(1024)S(1)}, bf16[2048,640]{0,1:T(8,128)(2,1)S(1)}) fusion(bf16[2048,3200]{1,0:T(8,128)(2,1)} %get-tuple-element.18, bf16[2,3200,640]{2,1,0:T(8,128)(2,1)} %param.15, bf16[1,2048,640]{1,2,0:T(8,128)(2,1)S(1)} %copy.20), kind=kOutput, calls=%fused_computation.43 | convolution fusion | flops 8395159552 | bytes 22454272 | tf_op jit(solution)/shard_map/jvp()/dot_general | solution.py:10
  71.4 16.5 %convolution_convert_fusion.1 = bf16[2048,3200]{1,0:T(8,128)(2,1)} fusion(bf16[2,3200,640]{2,1,0:T(8,128)(2,1)} %param.15, bf16[1,2048,640]{2,1,0:T(8,128)(2,1)S(1)} %copy-done.6), kind=kOutput, calls=%fused_computation.23 | convolution fusion | flops 8395161600 | bytes 19824640 | tf_op jit(solution)/shard_map/transpose(jvp())/dot_general | solution.py:10
  87.8 16.4 %fusion.29 = f32[2048,3200]{1,0:T(8,128)} fusion(bf16[2,640,3200]{2,1,0:T(8,128)(2,1)} %param.14, bf16[2048,640]{0,1:T(8,128)(2,1)S(1)} %get-tuple-element.21, f32[2048]{0:T(1024)S(1)} %fusion.98), kind=kOutput, calls=%fused_computation.47 | convolution fusion | flops 8392540160 | bytes 32940032 | tf_op jit(solution)/shard_map/jvp()/dot_general | solution.py:22
  104.3 34.1 %fusion.2 = (bf16[2048,3200]{1,0:T(8,128)(2,1)}, f32[2048,3200]{1,0:T(8,128)}) fusion(f32[2048,3200]{1,0:T(8,128)} %fusion.29, bf16[2048,3200]{1,0:T(8,128)(2,1)} %convolution_convert_fusion.1, bf16[2,640,3200]{2,1,0:T(8,128)(2,1)} %param.13, bf16[2048,640]{0,1:T(8,128)(2,1)S(1)} %get-tuple-element.21, f32[2048]{0:T(1024)S(1)} %fusion.98), kind=kOutput, calls=%fused_computation.8 | convolution fusion | flops 8471183360 | bytes 85368832 | tf_op jit(solution)/shard_map/jvp()/dot_general | solution.py:21
  138.4 14.1 %convolution_convert_fusion.2 = bf16[640,3200]{1,0:T(8,128)(2,1)} fusion(bf16[2048,3200]{1,0:T(8,128)(2,1)} %get-tuple-element.22, bf16[2048,640]{0,1:T(8,128)(2,1)S(1)} %get-tuple-element.21, f32[2048]{0:T(1024)S(1)} %fusion.98), kind=kOutput, calls=%fused_computation.33 | convolution fusion | flops 8392540160 | bytes 19832832 | tf_op jit(solution)/shard_map/transpose(jvp())/dot_general | solution.py:21
  156.0 17.0 %fusion.59 = bf16[2048,640]{0,1:T(8,128)(2,1)S(1)} fusion(bf16[2,640,3200]{2,1,0:T(8,128)(2,1)} %param.14, bf16[2048,3200]{1,0:T(8,128)(2,1)} %convolution_convert_fusion.1, f32[2048,3200]{1,0:T(8,128)} %get-tuple-element.23), kind=kOutput, calls=%fused_computation.73 | convolution fusion | flops 8429240320 | bytes 46039040 | tf_op jit(solution)/shard_map/transpose(jvp())/dot_general | solution.py:22
  173.1 13.5 %fusion.27 = (f32[2048]{0:T(1024)S(1)}, bf16[2048,640]{0,1:T(8,128)(2,1)S(1)}) fusion(bf16[2048,640]{0,1:T(8,128)(2,1)S(1)} %copy-done.3, bf16[2048,640]{0,1:T(8,128)(2,1)S(1)} %fusion.59, bf16[2048,3200]{1,0:T(8,128)(2,1)} %get-tuple-element.22, bf16[2,640,3200]{2,1,0:T(8,128)(2,1)} %param.13), kind=kOutput, calls=%fused_computation.45 | convolution fusion | flops 8395159552 | bytes 25075712 | tf_op jit(solution)/shard_map/transpose(jvp())/dot_general | solution.py:21
  188.5 16.3 %convolution_convert_fusion = bf16[2048,3200]{1,0:T(8,128)(2,1)} fusion(bf16[2048,640]{0,1:T(8,128)(2,1)S(1)} %fusion.69, bf16[2,3200,640]{2,1,0:T(8,128)(2,1)} %param.15), kind=kOutput, calls=%fused_computation.22 | convolution fusion | flops 8395161600 | bytes 19824640 | tf_op jit(solution)/shard_map/transpose(jvp())/dot_general | solution.py:10
  204.9 27.5 %fusion.17 = bf16[640,3200]{1,0:T(8,128)(2,1)} fusion(f32[2048,3200]{1,0:T(8,128)} %fusion.42, f32[2048,3200]{1,0:T(8,128)} %get-tuple-element.19, bf16[2048,3200]{1,0:T(8,128)(2,1)} %convolution_convert_fusion, bf16[1,2048,640]{1,2,0:T(8,128)(2,1)S(1)} %copy-done.1, f32[2048]{0:T(1024)S(1)} %copy-done.17), kind=kOutput, calls=%fused_computation.36 | convolution fusion | flops 8466677760 | bytes 72261632 | tf_op jit(solution)/shard_map/transpose(jvp())/dot_general | solution.py:21
  232.5 18.9 %fusion.20 = bf16[640,3200]{1,0:T(8,128)(2,1)} fusion(bf16[2048,3200]{1,0:T(8,128)(2,1)} %convolution_convert_fusion, f32[2048,3200]{1,0:T(8,128)} %fusion.42, bf16[1,2048,640]{1,2,0:T(8,128)(2,1)S(1)} %copy-done.1, f32[2048]{0:T(1024)S(1)} %copy-done.17), kind=kOutput, calls=%fused_computation.37 | convolution fusion | flops 8433909760 | bytes 46047232 | tf_op jit(solution)/shard_map/transpose(jvp())/dot_general | solution.py:22
  251.5 20.3 %fusion.16 = bf16[640,3200]{1,0:T(8,128)(2,1)} fusion(bf16[2048,3200]{1,0:T(8,128)(2,1)} %convolution_convert_fusion.1, bf16[2048,640]{0,1:T(8,128)(2,1)} %copy-done.2, f32[2048]{0:T(1024)S(1)} %fusion.98, f32[2048,3200]{1,0:T(8,128)} %get-tuple-element.23), kind=kOutput, calls=%fused_computation.35 | convolution fusion | flops 8433909760 | bytes 46047232 | tf_op jit(solution)/shard_map/transpose(jvp())/dot_general | solution.py:22
  272.0 15.3 %convolution_convert_fusion.3 = bf16[3200,640]{1,0:T(8,128)(2,1)} fusion(bf16[2048,3200]{1,0:T(8,128)(2,1)} %get-tuple-element.18, bf16[2048,640]{0,1:T(8,128)(2,1)S(1)} %copy-done.5), kind=kOutput, calls=%fused_computation.38 | convolution fusion | flops 8390656000 | bytes 19824640 | tf_op jit(solution)/shard_map/transpose(jvp())/dot_general | solution.py:10
  287.4 23.1 %fusion.15 = bf16[3200,640]{1,0:T(8,128)(2,1)} fusion(f32[2048,3200]{1,0:T(8,128)} %fusion.29, bf16[1,2048,640]{2,1,0:T(8,128)(2,1)} %param.12, f32[2048,3200]{1,0:T(8,128)} %get-tuple-element.23), kind=kOutput, calls=%fused_computation.34 | convolution fusion | flops 8429977600 | bytes 59146240 | tf_op jit(solution)/shard_map/transpose(jvp())/dot_general | solution.py:10
  318.5 18.2 %reduce-scatter.13.cloned.1.call-done = bf16[80,3200]{1,0:T(8,128)(2,1)} async-done(((bf16[640,3200]{1,0:T(8,128)(2,1)}), bf16[80,3200]{1,0:T(8,128)(2,1)}) %reduce-scatter.13.cloned.1.call-update) | async-done | bytes 512016 | tf_op jit(solution)/shard_map/reduce_scatter | solution.py:52
  339.3 32.2 %reduce-scatter.15.cloned.1.call-done = bf16[400,640]{1,0:T(8,128)(2,1)} async-done(((bf16[3200,640]{1,0:T(8,128)(2,1)}), bf16[400,640]{1,0:T(8,128)(2,1)}) %reduce-scatter.15.cloned.1.call-update) | async-done | bytes 512016 | tf_op jit(solution)/shard_map/reduce_scatter | solution.py:52
  374.1 32.2 %reduce-scatter.17.cloned.1.call-done = bf16[400,640]{1,0:T(8,128)(2,1)} async-done(((bf16[3200,640]{1,0:T(8,128)(2,1)}), bf16[400,640]{1,0:T(8,128)(2,1)}) %reduce-scatter.17.cloned.1.call-update) | async-done | bytes 512016 | tf_op jit(solution)/shard_map/reduce_scatter | solution.py:52
  408.9 15.9 %psum.7 = f32[]{:T(128)} all-reduce(f32[]{:T(128)S(6)} %add.116), channel_id=1, replica_groups=mesh['rep'=2,'dp'=8] {'dp'}, use_global_device_ids=true, to_apply=%region_15.16 | all-reduce | flops 1 | bytes 8 | tf_op jit(solution)/shard_map/psum | solution.py:53
  445.5 31.7 %all-gather.8.cloned.1.call-done = bf16[2,3200,640]{2,1,0:T(8,128)(2,1)} async-done(((bf16[2,400,640]{2,1,0:T(8,128)(2,1)}), bf16[2,3200,640]{2,1,0:T(8,128)(2,1)}) %all-gather.8.cloned.1.call-update) | async-done | bytes 8192016 | tf_op jit(solution)/shard_map/all_gather | solution.py:61
  477.2 47.0 %all-gather.6.cloned.1.call-done = bf16[2,640,3200]{2,1,0:T(8,128)(2,1)} async-done(((bf16[2,80,3200]{2,1,0:T(8,128)(2,1)}), bf16[2,640,3200]{2,1,0:T(8,128)(2,1)}) %all-gather.6.cloned.1.call-update) | async-done | bytes 8192016 | tf_op jit(solution)/shard_map/all_gather | solution.py:61
  524.2 47.0 %all-gather.4.cloned.1.call-done = bf16[2,640,3200]{2,1,0:T(8,128)(2,1)} async-done(((bf16[2,80,3200]{2,1,0:T(8,128)(2,1)}), bf16[2,640,3200]{2,1,0:T(8,128)(2,1)}) %all-gather.4.cloned.1.call-update) | async-done | bytes 8192016 | tf_op jit(solution)/shard_map/all_gather | solution.py:61
  571.2 7.4 %copy.25 = bf16[2,640,3200]{2,1,0:T(8,128)(2,1)} copy(bf16[2,640,3200]{2,1,0:T(8,128)(2,1)} %all-gather.4.cloned.1.call-done) | data formatting | bytes 16384000
  578.6 7.4 %copy.26 = bf16[2,640,3200]{2,1,0:T(8,128)(2,1)} copy(bf16[2,640,3200]{2,1,0:T(8,128)(2,1)} %all-gather.6.cloned.1.call-done) | data formatting | bytes 16384000
  (85 shorter events, 44.4 us)
Async XLA Ops:
  7.2 303.5 %reduce-scatter.9.cloned.1.call-start = ((), (), s32[]{:S(2)}) async-start(), calls=%async_computation.7 | async-start | bytes 4608000 | tf_op jit(solution)/shard_map/reduce_scatter | solution.py:52
  10.3 47.2 %copy-start = (bf16[1,2048,640]{1,2,0:T(8,128)(2,1)}, bf16[1,2048,640]{1,2,0:T(8,128)(2,1)S(1)}, u32[]{:S(2)}) copy-start(bf16[1,2048,640]{1,2,0:T(8,128)(2,1)S(1)} %copy.20) | copy-start | bytes 7864324
  10.8 18.6 %copy-start.16 = (f32[2048]{0:T(1024)}, f32[2048]{0:T(1024)S(1)}, u32[]{:S(2)}) copy-start(f32[2048]{0:T(1024)S(1)} %add_rsqrt_fusion) | copy-start | bytes 24580
  57.4 13.9 %copy-start.6 = (bf16[1,2048,640]{2,1,0:T(8,128)(2,1)S(1)}, bf16[1,2048,640]{2,1,0:T(8,128)(2,1)}, u32[]{:S(2)}) copy-start(bf16[1,2048,640]{2,1,0:T(8,128)(2,1)} %param.12) | copy-start | bytes 7864324
  71.3 16.5 %copy-start.14 = (f32[2048]{0:T(1024)}, f32[2048]{0:T(1024)S(1)}, u32[]{:S(2)}) copy-start(f32[2048]{0:T(1024)S(1)} %get-tuple-element.20) | copy-start | bytes 24580
  71.3 67.1 %copy-start.2 = (bf16[2048,640]{0,1:T(8,128)(2,1)}, bf16[2048,640]{0,1:T(8,128)(2,1)S(1)}, u32[]{:S(2)}) copy-start(bf16[2048,640]{0,1:T(8,128)(2,1)S(1)} %get-tuple-element.21) | copy-start | bytes 7864324
  152.5 160.2 %reduce-scatter.7.cloned.1.call-start = ((), (), s32[]{:S(2)}) async-start(), calls=%async_computation.6 | async-start | bytes 4608000 | tf_op jit(solution)/shard_map/reduce_scatter | solution.py:52
  156.0 17.1 %copy-start.3 = (bf16[2048,640]{0,1:T(8,128)(2,1)S(1)}, bf16[2048,640]{0,1:T(8,128)(2,1)}, u32[]{:S(2)}) copy-start(bf16[2048,640]{0,1:T(8,128)(2,1)} %copy-done.2) | copy-start | bytes 7864324
  173.1 13.5 %copy-start.15 = (f32[2048]{0:T(1024)S(1)}, f32[2048]{0:T(1024)}, u32[]{:S(2)}) copy-start(f32[2048]{0:T(1024)} %copy-done.14) | copy-start | bytes 24580
  188.5 16.4 %copy-start.4 = (bf16[2048,640]{0,1:T(8,128)(2,1)}, bf16[2048,640]{0,1:T(8,128)(2,1)S(1)}, u32[]{:S(2)}) copy-start(bf16[2048,640]{0,1:T(8,128)(2,1)S(1)} %fusion.69) | copy-start | bytes 7864324
  188.5 16.4 %copy-start.1 = (bf16[1,2048,640]{1,2,0:T(8,128)(2,1)S(1)}, bf16[1,2048,640]{1,2,0:T(8,128)(2,1)}, u32[]{:S(2)}) copy-start(bf16[1,2048,640]{1,2,0:T(8,128)(2,1)} %copy-done) | copy-start | bytes 7864324
  188.5 16.4 %copy-start.17 = (f32[2048]{0:T(1024)S(1)}, f32[2048]{0:T(1024)}, u32[]{:S(2)}) copy-start(f32[2048]{0:T(1024)} %copy-done.16) | copy-start | bytes 24580
  232.4 83.6 %reduce-scatter.11.cloned.1.call-start = ((), (), s32[]{:S(2)}) async-start(), calls=%async_computation.8 | async-start | bytes 4608000 | tf_op jit(solution)/shard_map/reduce_scatter | solution.py:52
  251.5 20.5 %copy-start.5 = (bf16[2048,640]{0,1:T(8,128)(2,1)S(1)}, bf16[2048,640]{0,1:T(8,128)(2,1)}, u32[]{:S(2)}) copy-start(bf16[2048,640]{0,1:T(8,128)(2,1)} %copy-done.4) | copy-start | bytes 7864324
  251.5 85.3 %reduce-scatter.13.cloned.1.call-start = ((), (), s32[]{:S(2)}) async-start(), calls=%async_computation.9 | async-start | bytes 4608000 | tf_op jit(solution)/shard_map/reduce_scatter | solution.py:52
  271.9 99.6 %reduce-scatter.15.cloned.1.call-start = ((), (), s32[]{:S(2)}) async-start(), calls=%async_computation.10 | async-start | bytes 4608000 | tf_op jit(solution)/shard_map/reduce_scatter | solution.py:52
  287.3 119.0 %reduce-scatter.17.cloned.1.call-start = ((), (), s32[]{:S(2)}) async-start(), calls=%async_computation.11 | async-start | bytes 4608000 | tf_op jit(solution)/shard_map/reduce_scatter | solution.py:52
  310.6 117.1 %copy-start.7 = (f32[2,400,640]{2,1,0:T(8,128)S(1)}, f32[2,400,640]{2,1,0:T(8,128)}, u32[]{:S(2)}) copy-start(f32[2,400,640]{2,1,0:T(8,128)} %param.21) | copy-start | bytes 6144004
  310.6 166.6 %all-gather.8.cloned.1.call-start = ((), (), s32[]{:S(2)}) async-start(), calls=%async_computation.14 | async-start | bytes 9216000 | tf_op jit(solution)/shard_map/all_gather | solution.py:61
  432.7 91.5 %all-gather.6.cloned.1.call-start = ((), (), s32[]{:S(2)}) async-start(), calls=%async_computation.13 | async-start | bytes 9216000 | tf_op jit(solution)/shard_map/all_gather | solution.py:61
  434.2 5.4 copy-start.11
  439.1 132.1 %all-gather.4.cloned.1.call-start = ((), (), s32[]{:S(2)}) async-start(), calls=%async_computation.12 | async-start | bytes 9216000 | tf_op jit(solution)/shard_map/all_gather | solution.py:61
  571.2 14.7 %slice-start = ((s8[8192000]{0:T(1024)(128)(4,1)}), s8[4194304]{0:T(1024)(128)(4,1)S(1)}, s32[]{:S(2)}) async-start(s8[8192000]{0:T(1024)(128)(4,1)} %bitcast.80), calls=%async_computation.15 | async-start | bytes 8388608
  578.6 7.4 %slice-start.1 = ((s8[8192000]{0:T(1024)(128)(4,1)}), s8[3997696]{0:T(1024)(128)(4,1)S(1)}, s32[]{:S(2)}) async-start(s8[8192000]{0:T(1024)(128)(4,1)} %bitcast.80), calls=%async_computation.16 | async-start | bytes 7995392
  (5 other events, 18.7 us)
Sparse Core Ops, SparseCore 0:
  152.7 33.7 reduce-scatter.8
  232.5 33.7 reduce-scatter.6
  269.2 32.5 reduce-scatter.10
  304.0 32.6 reduce-scatter.12
  338.9 32.5 reduce-scatter.14
  373.7 32.5 reduce-scatter.16
  432.8 44.3 all-gather.7
  479.4 44.7 all-gather.5
  526.4 44.7 all-gather.3

commit v2 on v1

v2 whole, which is shorter than its diff:
```python
import functools

import jax
import jax.numpy as jnp
from jax import lax
from jax.experimental import pallas as pl
from jax.experimental.pallas import tpu as pltpu
from jax.sharding import PartitionSpec as P

F32, BF16 = jnp.float32, jnp.bfloat16
MESH = pl.DeviceIdType.MESH
EPS = 1e-6
VMEM_LIMIT = 67043328


def dot(a, b):
    return jnp.dot(a, b, preferred_element_type=F32)


def dot_nt(a, b):
    return lax.dot_general(a, b, (((1,), (1,)), ((), ())), preferred_element_type=F32)


def sigmoid(g):
    return 0.5 * jnp.tanh(0.5 * g) + 0.5


def scale_of(h):
    return lax.rsqrt(jnp.mean(h * h, -1, keepdims=True) + EPS)


def forward_kernel(z, x_ref, wg_ref, wu_ref, wd_ref, h1_ref, aT_ref, save_ref, a, wgu, wd, hid, *bufs):
    W, CH, NT, NC, T = z.W, z.CH, z.NT, z.NC, z.T
    gus, (wsem, dsem, osem) = bufs[:NC], bufs[NC:]

    def wcopy(t, slot):
        return (
            pltpu.make_async_copy(wg_ref.at[0, :, pl.ds(t * W, W)], wgu.at[slot, :, pl.ds(0, W)], wsem.at[slot, 0]),
            pltpu.make_async_copy(wu_ref.at[0, :, pl.ds(t * W, W)], wgu.at[slot, :, pl.ds(W, W)], wsem.at[slot, 1]),
        )

    for c in wcopy(0, 0):
        c.start()
    dcopy = pltpu.make_async_copy(wd_ref.at[0], wd, dsem)
    dcopy.start()
    for i in range(T // 256):
        r = pl.ds(i * 256, 256)
        h = x_ref[0, r, :].astype(F32)
        n = (h * scale_of(h)).astype(BF16)
        a[r, :] = n
        aT_ref[:, r] = n.T

    def out(t, c):
        return pltpu.make_async_copy(gus[c], save_ref.at[t, c], osem.at[c])

    def A(t, c):
        gu = dot(a[pl.ds(c * CH, CH), :], wgu[t % 2])
        gus[c][0] = gu[:, :W]
        gus[c][1] = gu[:, W:]

    def E(t, c):
        g, u = gus[c][0], gus[c][1]
        hid[pl.ds(c * CH, CH), pl.ds(pl.multiple_of(t * W, 128), W)] = (g * sigmoid(g) * u).astype(BF16)

    def tile(t, first):
        for c in wcopy(t, t % 2):
            c.wait()
        if first:
            for c in wcopy(t + 1, (t + 1) % 2):
                c.start()
        else:
            @pl.when(t + 1 < NT)
            def _():
                for c in wcopy(t + 1, (t + 1) % 2):
                    c.start()
        for p in range(0, NC, 2):
            if not first:
                out(t, p).wait()
                out(t, p + 1).wait()
            A(t, p)
            if p:
                E(t, p - 1)
            A(t, p + 1)
            E(t, p)
            if p:
                out(t, p - 2).start()
                out(t, p - 1).start()
        E(t, NC - 1)
        out(t, NC - 2).start()
        out(t, NC - 1).start()

    tile(0, True)

    @pl.loop(1, NT)
    def _(t):
        tile(t, False)

    dcopy.wait()

    @pl.loop(0, T // 512)
    def _(i):
        r = pl.ds(pl.multiple_of(i * 512, 512), 512)
        h1_ref[r, :] = x_ref[0, r, :] + dot(hid[r, :], wd[...]).astype(BF16)

    for c in range(NC):
        out(0, c).wait()


def backward_kernel(z, h1_ref, dy_ref, wg_ref, wu_ref, wd_ref, aT0_ref, save_ref,
                    gg_ref, gup_ref, gd_ref, fac_ref, dwd_ref,
                    a, aT, dyT, wgu, wd, gu0, gu1, gu2, gu3, dh0, dh1, hid, dgu, sd,
                    G, PB, OB, B1, B2, ssacc, ssall,
                    wsem, gsem, tsem, dsem, usem, sP, rP, sO, rO, s1, r1, s2, r2, sS, rS):
    W, CH, NT, NC, T, D = z.W, z.CH, z.NT, z.NC, z.T, z.D
    R = z.R
    NA, NB = 8, z.NS
    gus, dhs = (gu0, gu1, gu2, gu3), (dh0, dh1)
    da = None
    rep, me = lax.axis_index("rep"), lax.axis_index("dp")
    c, k = me // 2, me % 2
    partner = c * 2 + (1 - k)

    def dev(t):
        return (rep, t)

    def chip(j):
        return lax.rem(c + j + 4, 4)

    bar = pltpu.get_barrier_semaphore()
    for j in range(1, 8):
        pl.semaphore_signal(bar, inc=1, device_id=dev(lax.rem(me + j, 8)), device_id_type=MESH)

    def copyP(slot):
        return pltpu.make_async_remote_copy(src_ref=G.at[slot, :, 1 - k], dst_ref=PB.at[slot], send_sem=sP.at[slot], recv_sem=rP.at[slot],
                                            device_id=dev(partner), device_id_type=MESH)

    def copyO(slot, d):
        return pltpu.make_async_remote_copy(src_ref=G.at[slot, chip(2), k], dst_ref=OB.at[slot], send_sem=sO.at[slot], recv_sem=rO.at[slot],
                                            device_id=dev(chip(d) * 2 + k), device_id_type=MESH)

    def copy1(slot, d):
        return pltpu.make_async_remote_copy(src_ref=G.at[slot, chip(-d), k], dst_ref=B1.at[slot], send_sem=s1.at[slot], recv_sem=r1.at[slot],
                                            device_id=dev(chip(-d) * 2 + k), device_id_type=MESH)

    def copy2(slot, d):
        return pltpu.make_async_remote_copy(src_ref=G.at[slot, chip(d), k], dst_ref=B2.at[slot], send_sem=s2.at[slot], recv_sem=r2.at[slot],
                                            device_id=dev(chip(d) * 2 + k), device_id_type=MESH)

    def stage0(slot):
        copyP(slot).start()

    def stage1(slot, d):
        copyP(slot).wait_recv()
        for j, copy in ((2, copyO), (-d, copy1)):
            q = chip(j)
            G[slot, q, k] = (G[slot, q, k].astype(F32) + PB[slot, q].astype(F32)).astype(BF16)
            copy(slot, d).start()

    def stage2(slot, d):
        copyO(slot, d).wait_recv()
        q = chip(d)
        G[slot, q, k] = (G[slot, q, k].astype(F32) + PB[slot, q].astype(F32) + OB[slot].astype(F32)).astype(BF16)
        copy2(slot, d).start()

    def stage3(slot, d, put):
        copy1(slot, d).wait_recv()
        copy2(slot, d).wait_recv()
        s = (G[slot, c, k].astype(F32) + PB[slot, c].astype(F32)) + (B1[slot].astype(F32) + B2[slot].astype(F32))
        g = s.astype(BF16)
        put(g)
        w = g.astype(F32)
        ssacc[...] += jnp.sum((w * w).reshape(R // 8, 8, W), 0)
        copyP(slot).wait_send()
        copyO(slot, d).wait_send()
        copy1(slot, d).wait_send()
        copy2(slot, d).wait_send()

    def aslot(r, e):
        return lax.rem(r * 2 + e, NA)

    def when(p, f):
        if isinstance(p, bool):
            if p:
                f()
        else:
            pl.when(p)(f)

    DIR = (1, -1)

    def a_put(r, e):
        ref = (gg_ref, gup_ref)[e]
        layer = 1 - r // NT

        def put(g):
            ref[layer, :, pl.ds(pl.multiple_of(lax.rem(r, NT) * W, 128), W)] = g
        return put

    def round_a(r, s0=True, s1_=True, s2_=True, s3_=True):
        if s1_:
            def f1():
                for e in range(2):
                    stage1(aslot(r - 1, e), DIR[e])
            when(r >= 1 if not isinstance(r, int) else bool(r >= 1), f1)
        if s3_:
            def f3():
                for e in range(2):
                    stage3(aslot(r - 3, e), DIR[e], a_put(r - 3, e))
            when(r >= 3 if not isinstance(r, int) else bool(r >= 3), f3)
        if s2_:
            def f2():
                for e in range(2):
                    stage2(aslot(r - 2, e), DIR[e])
            when(r >= 2 if not isinstance(r, int) else bool(r >= 2), f2)
        if s0:
            for e in range(2):
                stage0(aslot(r, e))

    def bslot(i):
        return NA + i

    def bdir(layer, i):
        return 1 if (i + layer) % 2 else -1

    def b_load(layer, i):
        return pltpu.make_async_copy(dwd_ref.at[layer, :, :, i], G.at[bslot(i)], usem.at[i])

    def batch_b(layer, stage):
        for i in range(NB):
            if stage == 0:
                b_load(layer, i).wait()
                stage0(bslot(i))
            elif stage == 1:
                stage1(bslot(i), bdir(layer, i))
            elif stage == 2:
                stage2(bslot(i), bdir(layer, i))
            else:
                def put(g, i=i):
                    gd_ref[layer, pl.ds(i * R, R), :] = g
                stage3(bslot(i), bdir(layer, i), put)

    def wcopies(t, slot):
        return (
            pltpu.make_async_copy(wg_ref.at[1, :, pl.ds(t * W, W)], wgu.at[slot, :, pl.ds(0, W)], wsem.at[slot, 0]),
            pltpu.make_async_copy(wu_ref.at[1, :, pl.ds(t * W, W)], wgu.at[slot, :, pl.ds(W, W)], wsem.at[slot, 1]),
        )

    def dcopy(layer, t, slot):
        return pltpu.make_async_copy(wd_ref.at[layer, pl.ds(t * W, W), :], wd.at[slot], wsem.at[slot, 2])

    def sdcopy(layer, t, slot, b):
        B = t * 8 + b
        return pltpu.make_async_copy(sd.at[slot, pl.ds(b * R, R)], dwd_ref.at[layer, B // (2 * NB), lax.rem(B // NB, 2), lax.rem(B, NB)], dsem.at[slot, b])

    for cp in wcopies(0, 0) + (dcopy(1, 0, 0),):
        cp.start()
    hcopy = pltpu.make_async_copy(h1_ref, dgu.at[:, pl.ds(0, W)], tsem)
    hcopy.start()
    ssacc[...] = jnp.zeros_like(ssacc)
    hcopy.wait()

    @pl.loop(0, T // 128)
    def _(i):
        r = pl.ds(pl.multiple_of(i * 128, 128), 128)
        h = dgu[r, :W].astype(F32)
        n = (h * scale_of(h)).astype(BF16)
        a[r, :] = n
        aT[:, r] = n.T
        dyT[:, r] = dy_ref[0, r, :].T

    def da_at(ci):
        ref = gus[2 + ci // 2]
        return ref, ci % 2

    for ci in range(NC):
        ref, half = da_at(ci)
        ref[half] = jnp.zeros((CH, D), F32)

    pl.semaphore_wait(bar, 7)

    def back_elem(ci, gu, dh):
        r = pl.ds(ci * CH, CH)
        g, u, dh = gu[0], gu[1], dh[...].astype(F32)
        s = sigmoid(g)
        silu = g * s
        hid[r, :] = (silu * u).astype(BF16)
        dgu[r, :W] = (dh * u * (s + silu * (1.0 - s))).astype(BF16)
        dgu[r, W:] = (dh * silu).astype(BF16)

    def weight_grads(r, slot):
        for j in range(0, W, 256):
            n = min(256, W - j)
            sd[slot, j : j + n] = dot(dyT[...], hid[:, j : j + n]).astype(BF16).T
        for j in range(0, 2 * W, 256):
            gw = dot(aT[...], dgu[:, j : j + 256]).astype(BF16)
            for i in range(0, 256, 128):
                e, q = divmod(j + i, W)
                G[aslot(r, e), :, :, :, q : q + 128] = gw[:, i : i + 128].reshape(4, 2, R, 128)

    @pl.loop(0, NT)
    def _(t):
        slot = lax.rem(t, 2)
        for cp in wcopies(t, slot) + (dcopy(1, t, slot),):
            cp.wait()

        @pl.when(t + 1 < NT)
        def _():
            for cp in wcopies(t + 1, 1 - slot) + (dcopy(1, t + 1, 1 - slot),):
                cp.start()

        @pl.when(t >= 2)
        def _():
            for b in range(8):
                sdcopy(1, t - 2, slot, b).wait()

        def A(ci):
            r = pl.ds(ci * CH, CH)
            gu = dot(a[r, :], wgu[slot])
            gus[ci % 2][0] = gu[:, :W]
            gus[ci % 2][1] = gu[:, W:]
            dhs[ci % 2][...] = dot_nt(dy_ref[0, r, :], wd[slot]).astype(BF16)

        def DA(ci):
            ref, half = da_at(ci)
            ref[half] = ref[half] + dot_nt(dgu[pl.ds(ci * CH, CH), :], wgu[slot])

        for ci in range(NC):
            A(ci)
            if ci:
                back_elem(ci - 1, gus[(ci - 1) % 2], dhs[(ci - 1) % 2])
        for ci in range(NC - 1):
            DA(ci)
        back_elem(NC - 1, gus[(NC - 1) % 2], dhs[(NC - 1) % 2])
        weight_grads(t, slot)
        DA(NC - 1)
        for b in range(8):
            sdcopy(1, t, slot, b).start()
        round_a(t)

    hcopy.start()
    hcopy.wait()
    tcopy = pltpu.make_async_copy(aT0_ref, aT, tsem)
    tcopy.start()
    dcopy(0, 0, 0).start()

    def gcopy(t, ci):
        return pltpu.make_async_copy(save_ref.at[t, ci], gus[ci], gsem.at[ci])

    gcopy(0, 0).start()
    gcopy(0, 1).start()
    for ci in range(NC):
        ref, half = da_at(ci)
        @pl.loop(0, CH // 128)
        def _(j):
            r = pl.ds(pl.multiple_of(ci * CH + j * 128, 128), 128)
            h = dgu[r, :W].astype(F32)
            s = scale_of(h)
            d = ref[half, pl.ds(pl.multiple_of(j * 128, 128), 128), :].astype(BF16).astype(F32)
            kk = jnp.sum(d * h, -1, keepdims=True) * (s * s * s * (1.0 / D))
            n = dy_ref[0, r, :] + (d * s - h * kk).astype(BF16)
            a[r, :] = n
            dyT[:, r] = n.T
        if ci % 2:
            gcopy(0, 2 + ci // 2).start()
    for t in (NT - 2, NT - 1):
        for b in range(8):
            sdcopy(1, t, t % 2, b).wait()
    for i in range(NB):
        b_load(1, i).start()
    tcopy.wait()
    batch_b(1, 0)

    @pl.loop(0, NT)
    def _(t):
        slot = lax.rem(t, 2)
        dcopy(0, t, slot).wait()

        @pl.when(t + 1 < NT)
        def _():
            dcopy(0, t + 1, 1 - slot).start()

        @pl.when(t >= 2)
        def _():
            for b in range(8):
                sdcopy(0, t - 2, slot, b).wait()

        def A(ci):
            dhs[ci % 2][...] = dot_nt(a[pl.ds(ci * CH, CH), :], wd[slot]).astype(BF16)

        for ci in range(NC):
            A(ci)
            if ci:
                gcopy(t, ci - 1).wait()
                back_elem(ci - 1, gus[ci - 1], dhs[(ci - 1) % 2])
        gcopy(t, NC - 1).wait()
        back_elem(NC - 1, gus[NC - 1], dhs[(NC - 1) % 2])

        @pl.when(t + 1 < NT)
        def _():
            for ci in range(NC):
                gcopy(t + 1, ci).start()

        weight_grads(t + NT, slot)
        for b in range(8):
            sdcopy(0, t, slot, b).start()
        round_a(t + NT)
        for n in range(3):
            @pl.when(t == n)
            def _():
                batch_b(1, n + 1)

    for t in (NT - 2, NT - 1):
        for b in range(8):
            sdcopy(0, t, t % 2, b).wait()
    for i in range(NB):
        b_load(0, i).start()
    batch_b(0, 0)
    round_a(2 * NT, s0=False)
    batch_b(0, 1)
    round_a(2 * NT + 1, s0=False, s1_=False)
    batch_b(0, 2)
    round_a(2 * NT + 2, s0=False, s1_=False, s2_=False)
    batch_b(0, 3)

    acc = ssacc[...]
    part = acc[:, :128]
    for j in range(1, W // 128):
        part = part + acc[:, j * 128 : (j + 1) * 128]
    ssall[me] = part
    copies = []
    for j in range(1, 8):
        to = lax.rem(me + j, 8)
        cp = pltpu.make_async_remote_copy(src_ref=ssall.at[me], dst_ref=ssall.at[me], send_sem=sS.at[j - 1], recv_sem=rS.at[j - 1],
                                          device_id=dev(to), device_id_type=MESH)
        cp.start()
        copies.append(cp)
    for cp in copies:
        cp.wait()
    total = ssall[0]
    for j in range(1, 8):
        total = total + ssall[j]
    total = jnp.sum(jnp.sum(total, 0, keepdims=True), 1, keepdims=True)
    fac = jnp.minimum(1.0, 0.5 * lax.rsqrt(total / z.count + 1e-30))
    fac_ref[...] = jnp.broadcast_to(fac, fac_ref.shape)


class Sizes:
    pass


def solution(mesh):
    def step(x, dy, *arrays):
        weights, m, v = (arrays[i : i + 3] for i in (0, 3, 6))
        wg, wu, wd = weights
        z = Sizes()
        z.T, z.D = x.shape[1:]
        layers, _, z.FF = wg.shape
        z.W = z.D
        z.NT = z.FF // z.W
        z.CH = 512
        z.NC = z.T // z.CH
        z.R = z.D // 8
        z.NS = z.FF // 8 // z.R
        z.count = float(sum(w.size for w in weights))
        T, D, FF, W, CH, NT, NC, R, NS = z.T, z.D, z.FF, z.W, z.CH, z.NT, z.NC, z.R, z.NS
        vmem, hbm = pl.BlockSpec(memory_space=pltpu.VMEM), pl.BlockSpec(memory_space=pl.ANY)
        dma = pltpu.SemaphoreType.DMA
        h1, aT0, save = pl.pallas_call(
            functools.partial(forward_kernel, z),
            out_shape=(
                jax.ShapeDtypeStruct((T, D), BF16),
                jax.ShapeDtypeStruct((D, T), BF16),
                jax.ShapeDtypeStruct((NT, NC, 2, CH, W), F32),
            ),
            in_specs=[vmem] + [hbm] * 3,
            out_specs=(vmem, vmem, hbm),
            scratch_shapes=[
                pltpu.VMEM((T, D), BF16), pltpu.VMEM((2, D, 2 * W), BF16), pltpu.VMEM((FF, D), BF16), pltpu.VMEM((T, FF), BF16),
                *[pltpu.VMEM((2, CH, W), F32)] * NC,
                dma((2, 2)), dma, dma((NC,)),
            ],
            compiler_params=pltpu.CompilerParams(vmem_limit_bytes=VMEM_LIMIT),
            cost_estimate=pl.CostEstimate(flops=6 * T * D * FF, bytes_accessed=8 * T * FF, transcendentals=T * FF),
            name="forward0",
        )(x, wg, wu, wd)
        slots = 8 + NS
        block = pltpu.VMEM((slots, R, W), BF16)
        gg, gup, gd, fac, _ = pl.pallas_call(
            functools.partial(backward_kernel, z),
            out_shape=(
                jax.ShapeDtypeStruct((layers, R, FF), BF16),
                jax.ShapeDtypeStruct((layers, R, FF), BF16),
                jax.ShapeDtypeStruct((layers, NS * R, D), BF16),
                jax.ShapeDtypeStruct((8, 128), F32),
                jax.ShapeDtypeStruct((layers, 4, 2, NS, R, D), BF16),
            ),
            in_specs=[hbm, vmem] + [hbm] * 5,
            out_specs=(vmem, vmem, vmem, vmem, hbm),
            scratch_shapes=[
                pltpu.VMEM((T, D), BF16), pltpu.VMEM((D, T), BF16), pltpu.VMEM((D, T), BF16),
                pltpu.VMEM((2, D, 2 * W), BF16), pltpu.VMEM((2, W, D), BF16),
                *[pltpu.VMEM((2, CH, W), F32)] * NC,
                *[pltpu.VMEM((CH, W), BF16)] * 2,
                pltpu.VMEM((T, W), BF16), pltpu.VMEM((T, 2 * W), BF16), pltpu.VMEM((2, W, D), BF16),
                pltpu.VMEM((slots, 4, 2, R, W), BF16), pltpu.VMEM((slots, 4, R, W), BF16), block, block, block,
                pltpu.VMEM((8, W), F32), pltpu.VMEM((8, 8, 128), F32),
                dma((2, 3)), dma((NC,)), dma, dma((2, 8)), dma((NS,)),
                *[dma((slots,))] * 8, dma((7,)), dma((7,)),
            ],
            compiler_params=pltpu.CompilerParams(vmem_limit_bytes=VMEM_LIMIT, collective_id=0, has_side_effects=True),
            cost_estimate=pl.CostEstimate(flops=20 * T * D * FF, bytes_accessed=8 * T * FF, transcendentals=2 * T * FF),
            name="backward",
        )(h1, dy, wg, wu, wd, aT0, save)
        factor = fac[0, 0]
        me = lax.axis_index("dp")
        new_w, new_m, new_v = [], [], []
        for w, mm, vv, g in zip(weights, m, v, (gg, gup, gd), strict=True):
            rows = mm.shape[1]
            mine = lax.dynamic_slice_in_dim(w, me * rows, rows, 1).astype(F32)
            g = g.astype(F32) * factor
            nm = 0.9 * mm + 0.1 * g
            nv = 0.95 * vv + 0.05 * g * g
            nw = (mine - 0.02 * (nm * lax.rsqrt(nv + 1e-8) + 0.1 * mine)).astype(BF16)
            new_w.append(lax.all_gather(nw, "dp", axis=1, tiled=True))
            new_m.append(nm)
            new_v.append(nv)
        return (*new_w, *new_m, *new_v)

    whole, split = P(None, None, None), P(None, "dp", None)
    return jax.shard_map(
        step,
        mesh=mesh,
        in_specs=(P(("rep", "dp")),) * 2 + (whole,) * 3 + (split,) * 6,
        out_specs=(P("rep", None, None),) * 3 + (P("rep", "dp", None),) * 6,
        check_vma=False,
    )
```

time: 604 us -> 439 us (0.73)
  matrix products: 294 us -> 0 us
  Pallas kernels: 0 us -> 251 us
  waiting for transfers between devices: 209 us -> 127 us
  blocking collectives: 15.9 us -> 0 us
  other arithmetic: 31 us -> 18.3 us
  local copies, waits for them, and re-layouts: 26.8 us -> 19.4 us
    dot_general x15 -> x0, matrix products: 294 us -> none  [the longest x5 108 us: layer(): gate = jnp.dot(a, w[0], preferred_element_type=jnp.float32)]
    pallas_call x0 -> x2, Pallas kernels: none -> 251 us  [the longest x1 211 us: step(): pl.pallas_call(functools.partial(backward_kernel, z), out_shape=(jax.Shap...]
    reduce_scatter x6 -> x0, waiting for transfers between devices: 82.7 us -> none  [step(): lax.psum_scatter(grads[i][j], 'dp', scatter_dimension=0, tiled=True)]
    psum x1 -> x0, blocking collectives: 15.9 us -> none  [step(): total = lax.psum(sum((jnp.sum(t * t) for row in g for t in row)), 'dp')]
    reduce_sum x7 -> x0, other arithmetic: 12.1 us -> none  [the longest x6 11.5 us: step(): total = lax.psum(sum((jnp.sum(t * t) for row in g for t in row)), 'dp')]
    unnamed x45 -> x9, local copies, waits for them, and re-layouts: 26.8 us -> 18.2 us
  transfers between devices with their start and end apart: 9 -> 3, of which waited for: 6 -> 3; matrix products, arithmetic and copies ran while one was open for 30% -> 3% of each run, Pallas kernels for 0% -> 0%
where the time goes in v2:
time: 439 us; the launch traced here: 431 us
  Pallas kernels  251 us (57%)
  waiting for transfers between devices  127 us (29%)
  local copies, waits for them, and re-layouts  19.4 us (4%)
  other arithmetic  18.3 us (4%)
  between operations  14.3 us (3%)
    pallas_call x1, Pallas kernels, step(): pl.pallas_call(functools.partial(backward_kernel, z), out_shape=(jax.Shap...  211 us
    all_gather x3, waiting for transfers between devices, step(): new_w.append(lax.all_gather(nw, 'dp', axis=1, tiled=True))  127 us
    pallas_call x1, Pallas kernels, step(): pl.pallas_call(functools.partial(forward_kernel, z), out_shape=(jax.Shape...  40.6 us
    convert_element_type x3, other arithmetic, step(): nw = (mine - 0.02 * (nm * lax.rsqrt(nv + 1e-08) + 0.1 * mine)).astype(BF16)  18.3 us
    unnamed x9, local copies, waits for them, and re-layouts  18.2 us
  transfers between devices with their start and end apart: 3, of which 3 were waited for; matrix products, arithmetic and copies ran while one was open for 3% of the time, Pallas kernels for 0%

profile of v2, /device:TPU:113, one launch (start us, length us, event | category | flops | bytes accessed | tf_op | source)
XLA Modules:
  0.0 430.8 jit_solution(17972630485012021728)
XLA Ops:
  7.2 0.1 all-gather.6.cloned.1.call-start
  7.3 40.6 %forward0.1 = (bf16[2048,640]{1,0:T(8,128)(2,1)}, bf16[640,2048]{1,0:T(8,128)(2,1)}, f32[5,4,2,512,640]{4,3,2,1,0:T(8,128)}) custom-call(bf16[1,2048,640]{2,1,0:T(8,128)(2,1)} %x_ref.1, bf16[2,640,3200]{2,1,0:T(8,128)(2,1)} %wg_ref.3, bf16[2,640,3200]{2,1,0:T(8,128)(2,1)} %wu_ref.3, bf16[2,3200,640]{2,1,0:T(8,128)(2,1)} %wd_ref.3), custom_call_target="tpu_custom_call" | custom-call | flops 25165824000 | bytes 52428800 | tf_op jit(solution)/shard_map/forward0/pallas_call | solution.py:467
  47.9 210.6 %backward.1 = (bf16[2,80,3200]{2,1,0:T(8,128)(2,1)}, bf16[2,80,3200]{2,1,0:T(8,128)(2,1)}, bf16[2,400,640]{2,1,0:T(8,128)(2,1)}, f32[8,128]{1,0:T(8,128)}, bf16[2,4,2,5,80,640]{5,4,3,2,1,0:T(8,128)(2,1)}) custom-call(bf16[2048,640]{1,0:T(8,128)(2,1)} %get-tuple-element.16.h1_ref, bf16[1,2048,640]{2,1,0:T(8,128)(2,1)} %dy_ref.1, ...), custom_call_target="tpu_custom_call" | custom-call | flops 83886080000 | bytes 52428800 | tf_op jit(solution)/shard_map/backward/pallas_call | solution.py:487
  258.5 1.3 slice.3
  259.8 0.0 copy-start.1
  259.8 6.5 %fusion.5 = (bf16[2,80,3200]{2,1,0:T(8,128)(2,1)}, f32[2,80,3200]{2,1,0:T(8,128)}, f32[2,80,3200]{2,1,0:T(8,128)}) fusion(bf16[2,640,3200]{2,1,0:T(8,128)(2,1)} %wu_ref.3, s32[]{:T(128)S(6)} %select_n.7, f32[]{:T(128)} %bitcast, bf16[2,80,3200]{2,1,0:T(8,128)(2,1)} %get-tuple-element.21, f32[2,80,3200]{2,1,0:T(8,128)} %param.20, f32[2,80,3200]{2,1,0:T(8,128)} %param.17), kind=kLoop, calls=%fused_computation.14 | loop fusion | flops 8704000 | bytes 11264008 | tf_op jit(solution)/shard_map/convert_element_type | solution.py:522
  266.2 0.1 all-gather.6.cloned.1.call-update
  266.3 0.1 all-gather.4.cloned.1.call-start
  266.4 0.0 copy-done.1
  266.4 0.0 copy-start.2
  266.4 5.8 %fusion.2 = (bf16[2,80,3200]{2,1,0:T(8,128)(2,1)}, f32[2,80,3200]{2,1,0:T(8,128)}, f32[2,80,3200]{2,1,0:T(8,128)}) fusion(bf16[2,640,3200]{2,1,0:T(8,128)(2,1)} %wg_ref.3, s32[]{:T(128)S(6)} %select_n.7, f32[]{:T(128)} %bitcast, bf16[2,80,3200]{2,1,0:T(8,128)(2,1)} %get-tuple-element.19, f32[2,80,3200]{2,1,0:T(8,128)S(1)} %copy-done.1, f32[2,80,3200]{2,1,0:T(8,128)} %param.16), kind=kLoop, calls=%fused_computation.11 | loop fusion | flops 8704000 | bytes 11264008 | tf_op jit(solution)/shard_map/convert_element_type | solution.py:522
  272.1 0.1 all-gather.4.cloned.1.call-update
  272.2 0.1 all-gather.8.cloned.1.call-start
  272.3 0.0 copy-done.2
  272.3 6.1 %fusion.8 = (bf16[2,400,640]{2,1,0:T(8,128)(2,1)}, f32[2,400,640]{2,1,0:T(8,128)}, f32[2,400,640]{2,1,0:T(8,128)}) fusion(bf16[2,3200,640]{2,1,0:T(8,128)(2,1)} %wd_ref.3, s32[]{:T(128)S(6)} %select_n.8, f32[]{:T(128)} %bitcast, bf16[2,400,640]{2,1,0:T(8,128)(2,1)S(1)} %copy-done.2, f32[2,400,640]{2,1,0:T(8,128)} %param.21, f32[2,400,640]{2,1,0:T(8,128)} %param.18), kind=kLoop, calls=%fused_computation.17 | loop fusion | flops 8704000 | bytes 11264008 | tf_op jit(solution)/shard_map/convert_element_type | solution.py:522
  278.4 0.1 all-gather.8.cloned.1.call-update
  278.5 33.1 %all-gather.6.cloned.1.call-done = bf16[2,640,3200]{2,1,0:T(8,128)(2,1)} async-done(((bf16[2,80,3200]{2,1,0:T(8,128)(2,1)}), bf16[2,640,3200]{2,1,0:T(8,128)(2,1)}) %all-gather.6.cloned.1.call-update) | async-done | bytes 8192016 | tf_op jit(solution)/shard_map/all_gather | solution.py:523
  311.6 47.0 %all-gather.4.cloned.1.call-done = bf16[2,640,3200]{2,1,0:T(8,128)(2,1)} async-done(((bf16[2,80,3200]{2,1,0:T(8,128)(2,1)}), bf16[2,640,3200]{2,1,0:T(8,128)(2,1)}) %all-gather.4.cloned.1.call-update) | async-done | bytes 8192016 | tf_op jit(solution)/shard_map/all_gather | solution.py:523
  358.6 47.0 %all-gather.8.cloned.1.call-done = bf16[2,3200,640]{2,1,0:T(8,128)(2,1)} async-done(((bf16[2,400,640]{2,1,0:T(8,128)(2,1)}), bf16[2,3200,640]{2,1,0:T(8,128)(2,1)}) %all-gather.8.cloned.1.call-update) | async-done | bytes 8192016 | tf_op jit(solution)/shard_map/all_gather | solution.py:523
  405.6 0.0 copy-start
  405.6 7.5 %copy.23 = bf16[2,640,3200]{2,1,0:T(8,128)(2,1)} copy(bf16[2,640,3200]{2,1,0:T(8,128)(2,1)} %all-gather.4.cloned.1.call-done) | data formatting | bytes 16384000
  413.1 0.0 copy-done
  413.1 3.3 copy.24
  416.4 7.4 %copy.25 = bf16[2,3200,640]{2,1,0:T(8,128)(2,1)} copy(bf16[2,3200,640]{2,1,0:T(8,128)(2,1)} %all-gather.8.cloned.1.call-done) | data formatting | bytes 16384000
Async XLA Ops:
  7.2 304.4 %all-gather.6.cloned.1.call-start = ((), (), s32[]{:S(2)}) async-start(), calls=%async_computation.1 | async-start | bytes 9216000 | tf_op jit(solution)/shard_map/all_gather | solution.py:523
  259.8 6.6 %copy-start.1 = (f32[2,80,3200]{2,1,0:T(8,128)S(1)}, f32[2,80,3200]{2,1,0:T(8,128)}, u32[]{:S(2)}) copy-start(f32[2,80,3200]{2,1,0:T(8,128)} %param.19) | copy-start | bytes 6144004
  266.3 92.3 %all-gather.4.cloned.1.call-start = ((), (), s32[]{:S(2)}) async-start(), calls=%async_computation | async-start | bytes 9216000 | tf_op jit(solution)/shard_map/all_gather | solution.py:523
  266.4 5.9 %copy-start.2 = (bf16[2,400,640]{2,1,0:T(8,128)(2,1)S(1)}, bf16[2,400,640]{2,1,0:T(8,128)(2,1)}, u32[]{:S(2)}) copy-start(bf16[2,400,640]{2,1,0:T(8,128)(2,1)} %get-tuple-element.22) | copy-start | bytes 3072004
  272.2 133.4 %all-gather.8.cloned.1.call-start = ((), (), s32[]{:S(2)}) async-start(), calls=%async_computation.2 | async-start | bytes 9216000 | tf_op jit(solution)/shard_map/all_gather | solution.py:523
  405.6 7.5 %copy-start = (bf16[2,640,3200]{2,1,0:T(8,128)(2,1)S(1)}, bf16[2,640,3200]{2,1,0:T(8,128)(2,1)}, u32[]{:S(2)}) copy-start(bf16[2,640,3200]{2,1,0:T(8,128)(2,1)} %all-gather.6.cloned.1.call-done) | copy-start | bytes 24576004
Sparse Core Ops, SparseCore 0:
  266.4 45.1 all-gather.5
  313.7 44.7 all-gather.3
  360.8 44.7 all-gather.7

commit v3 on v0

v3 whole, which is shorter than its diff:
```python
import functools
from types import SimpleNamespace

import jax
import jax.numpy as jnp
from jax import lax
from jax.experimental import pallas as pl
from jax.experimental.pallas import tpu as pltpu
from jax.sharding import PartitionSpec as P

F32, BF16 = jnp.float32, jnp.bfloat16
VMEM_LIMIT = 67043328
NT_DIMS = (((1,), (1,)), ((), ()))
copy = pltpu.make_async_copy


def dot(a, b):
    return jnp.dot(a, b, preferred_element_type=F32)


def dot_nt(a, b):
    return lax.dot_general(a, b, NT_DIMS, preferred_element_type=F32)


def sigmoid(g):
    return 0.5 * jnp.tanh(0.5 * g) + 0.5


def scale_of(h):
    return lax.rsqrt(jnp.mean(h * h, -1, keepdims=True) + 1e-6)


def span(i, n):
    return pl.ds(pl.multiple_of(i * n, n), n)


def start(*copies):
    for c in copies:
        c.start()


def wait(*copies):
    for c in copies:
        c.wait()


def gate_up_tiles(z, layer_of, wg_ref, wu_ref, wgu, sem):
    def copies(t):
        slot = lax.rem(t, 2)
        return [
            copy(ref.at[layer_of(t), :, span(lax.rem(t, z.NT), z.W)], wgu.at[slot, :, pl.ds(e * z.W, z.W)], sem.at[slot, e])
            for e, ref in enumerate((wg_ref, wu_ref))
        ]

    return copies


def forward_kernel(z, x_ref, dy_ref, wg_ref, wu_ref, wd_ref, h1_ref, a1_ref, a1T_ref, a0_ref, a0T_ref, dyT_ref, hid_ref,
                   a, a1, aT, cT, h1, dy, dyT, wgu, wd, hid, gu0, gu1, wsem, dsem, hsem, tsem):
    W, CH, NT, NC, T = z.W, z.CH, z.NT, z.NC, z.T
    gus = (gu0, gu1)
    tiles = gate_up_tiles(z, lambda t: 0, wg_ref, wu_ref, wgu, wsem)
    later = [copy(dy_ref.at[0], dy, dsem.at[0]), copy(wd_ref.at[0], wd, dsem.at[1])]
    start(*tiles(0), *later)
    step = CH // 2
    for i in range(T // step):
        r = pl.ds(i * step, step)
        h = x_ref[0, r, :].astype(F32)
        a[r, :] = (h * scale_of(h)).astype(BF16)
    pairs = (a, a0_ref), (aT, a0T_ref), (dyT, dyT_ref)
    whole = [copy(s, d, tsem.at[0, e]) for e, (s, d) in enumerate(pairs)]
    start(whole[0])
    wait(later[0])

    def hid_out(t):
        return copy(hid.at[:, span(t, W)], hid_ref.at[0, t], hsem.at[t])

    @pl.loop(0, NT)
    def _(t):
        wait(*tiles(t))

        @pl.when(t + 1 < NT)
        def _():
            start(*tiles(t + 1))

        turned = span(jnp.minimum(t, NC - 1), CH)
        aT[:, turned] = a[turned, :].T
        dyT[:, turned] = dy[turned, :].T

        def E(c):
            g, u = gus[c % 2][0], gus[c % 2][1]
            hid[pl.ds(c * CH, CH), span(t, W)] = (g * sigmoid(g) * u).astype(BF16)

        for c in range(NC):
            gu = dot(a[pl.ds(c * CH, CH), :], wgu[lax.rem(t, 2)])
            gus[c % 2][0] = gu[:, :W]
            gus[c % 2][1] = gu[:, W:]
            if c:
                E(c - 1)
        E(NC - 1)
        start(hid_out(t))

    start(*whole[1:])
    wait(later[1])

    def project(i):
        r = span(i, CH)
        h1[r, :] = x_ref[0, r, :] + dot(hid[r, :], wd[...]).astype(BF16)

    def norm(i):
        r = span(i, CH)
        h = h1[r, :].astype(F32)
        n = (h * scale_of(h)).astype(BF16)
        a1[r, :] = n
        cT[:, r] = n.T

    def done(i):
        r = span(i, CH)
        parts = (h1.at[r], h1_ref.at[r]), (a1.at[r], a1_ref.at[r]), (cT.at[:, r], a1T_ref.at[:, r])
        return [copy(s, d, tsem.at[1 + i, e]) for e, (s, d) in enumerate(parts)]

    project(0)

    @pl.loop(1, NC)
    def _(i):
        norm(i - 1)
        project(i)
        start(*done(i - 1))

    norm(NC - 1)
    start(*done(NC - 1))
    wait(*whole, *[d for i in range(NC) for d in done(i)], *[hid_out(t) for t in range(NT)])


def backward_kernel(z, h1_ref, a1_ref, a1T_ref, a0_ref, a0T_ref, dyT_ref, dy_ref, wg_ref, wu_ref, wd_ref,
                    mg_ref, vg_ref, mu_ref, vu_ref, md_ref, vd_ref, _,
                    gg_ref, gup_ref, gd_ref, fac_ref, nd_ref, og_ref, ou_ref, hid_ref,
                    a, aT, dy, dyT, wgu, wd, gu0, gu1, gu2, gu3, dh0, dh1, hids, dgu,
                    G, PB, OB, B1, B2, ssacc, ssall,
                    wsem, dsem, tsem, hsem, sP, rP, sO, rO, s1, r1, s2, r2, sS, rS,
                    msem, nsem, lsem, sR, rR, sL, rL, sX, rX, sD, rD):
    W, CH, NT, NC, D, R, NS = z.W, z.CH, z.NT, z.NC, z.D, z.R, z.NS
    NA = 6
    peers = 2 * z.chips
    gus, dhs = (gu0, gu1, gu2, gu3), (dh0, dh1)
    rep, me = lax.axis_index("rep"), lax.axis_index("dp")
    c, k = me // 2, lax.rem(me, 2)

    def chip(j):
        return lax.rem(c + j + z.chips, z.chips)

    def remote(src, dst, send, recv, to):
        return pltpu.make_async_remote_copy(src_ref=src, dst_ref=dst, send_sem=send, recv_sem=recv, device_id=(rep, to),
                                            device_id_type=pl.DeviceIdType.MESH)

    bar = pltpu.get_barrier_semaphore()
    for j in range(1, peers):
        pl.semaphore_signal(bar, inc=1, device_id=(rep, lax.rem(me + j, peers)), device_id_type=pl.DeviceIdType.MESH)

    partner = c * 2 + 1 - k

    def copyP(s):
        return remote(G.at[s, :, 1 - k], PB.at[s], sP.at[s], rP.at[s], partner)

    def copyO(s, d):
        return remote(G.at[s, chip(2), k], OB.at[s], sO.at[s], rO.at[s], chip(d) * 2 + k)

    def copy1(s, d):
        return remote(G.at[s, chip(-d), k], B1.at[s], s1.at[s], r1.at[s], chip(-d) * 2 + k)

    def copy2(s, d):
        return remote(G.at[s, chip(d), k], B2.at[s], s2.at[s], r2.at[s], chip(d) * 2 + k)

    def both(s, q):
        return G[s, q, k].astype(F32) + PB[s, q].astype(F32)

    def stage0(each):
        each(lambda s, d, put: copyP(s).start())

    def stage1(each):
        def add(s, d, put):
            for q in (chip(2), chip(-d)):
                G[s, q, k] = both(s, q).astype(BF16)

        each(lambda s, d, put: copyP(s).wait_recv())
        each(add)
        each(lambda s, d, put: copyO(s, d).start())
        each(lambda s, d, put: copy1(s, d).start())

    def stage2(each):
        def add(s, d, put):
            q = chip(d)
            G[s, q, k] = (both(s, q) + OB[s].astype(F32)).astype(BF16)

        each(lambda s, d, put: copyO(s, d).wait_recv())
        each(add)
        each(lambda s, d, put: copy2(s, d).start())

    def stage3(each):
        def arrive(s, d, put):
            copy1(s, d).wait_recv()
            copy2(s, d).wait_recv()

        def add(s, d, put):
            g = (both(s, c) + (B1[s].astype(F32) + B2[s].astype(F32))).astype(BF16)
            put(g)
            w = g.astype(F32)
            ssacc[...] += jnp.sum((w * w).reshape(-1, *ssacc.shape), 0)

        def sent(s, d, put):
            for cp in (copyP(s), copyO(s, d), copy1(s, d), copy2(s, d)):
                cp.wait_send()

        for f in (arrive, add, sent):
            each(f)

    stages = stage0, stage1, stage2, stage3

    def a_slot(r, e):
        return lax.rem(r * 2 + e, NA)

    def a_put(r, e):
        def put(g):
            (gg_ref, gup_ref)[e][1 - r // NT, :, span(lax.rem(r, NT), W)] = g

        return put

    def stream_a(stage, r):
        stages[stage](lambda f: [f(a_slot(r, e), d, a_put(r, e)) for e, d in enumerate((1, -1))])

    def stream_b(stage, layer):
        def put(i):
            def f(g):
                gd_ref[layer, span(i, R), :] = g

            return f

        stages[stage](lambda f: pl.loop(0, NS)(lambda i: f(NA + i, lax.rem(i + layer, 2) * 2 - 1, put(i))))

    def layer_of(r):
        return 1 - r // NT

    tiles = gate_up_tiles(z, layer_of, wg_ref, wu_ref, wgu, wsem)

    def down(r):
        slot = lax.rem(r, 2)
        return copy(wd_ref.at[layer_of(r), span(lax.rem(r, NT), W), :], wd.at[slot], dsem.at[slot])

    def hid_out(t):
        return copy(hids.at[0], hid_ref.at[1, t], hsem.at[0])

    def gate_up_grads(r):
        for j in range(0, 2 * W, 256):
            gw = dot(aT[...], dgu[:, j : j + 256]).astype(BF16)
            for i in range(0, 256, 128):
                e, q = divmod(j + i, W)
                G[a_slot(r, e), :, :, :, q : q + 128] = gw[:, i : i + 128].reshape(*G.shape[1:4], 128)

    def hid_in(layer, i):
        return copy(hid_ref.at[layer, NT - 1 - i], hids.at[lax.rem(i, 2)], hsem.at[lax.rem(i, 2)])

    def turn_units(sd, i):
        for j in range(0, W, 128):
            rows = sd[:, j : j + 128].T
            for b in range(8):
                lo, hi = max(j, b * R), min(j + 128, b * R + R)
                if lo < hi:
                    B = (NT - 1 - i) * 8 + b
                    unit = G.at[NA + lax.rem(B, NS), B // (2 * NS), lax.rem(B // NS, 2)]
                    unit[lo - b * R : hi - b * R] = rows[lo - j : hi - j]

    def down_grads(layer, sd):
        @pl.loop(0, NT)
        def _(i):
            slot = lax.rem(i, 2)

            @pl.when(i + 1 > layer)
            def _():
                wait(hid_in(layer, i))

            turn_units(sd, jnp.maximum(i - 1, 0))
            for j in range(0, W, 256):
                n = min(256, W - j)
                sd[:, j : j + n] = dot(dyT[...], hids[slot, :, j : j + n]).astype(BF16)

            @pl.when(i + 2 < NT)
            def _():
                start(hid_in(layer, i + 2))

            @pl.when((i == 1) & (layer == 1))
            def _():
                stream_a(1, NT - 1)
                stream_a(3, NT - 2)

        turn_units(sd, NT - 1)

    def da_at(ci):
        return (gu2, gu3)[ci // 2].at[ci % 2]

    def output_grad(ci):
        step = CH // 2

        @pl.loop(0, 2)
        def _(j):
            r = span(ci * 2 + j, step)
            h = dgu[r, :W].astype(F32)
            s = scale_of(h)
            d = da_at(ci)[span(j, step), :].astype(BF16).astype(F32)
            n = dy[r, :] + (s * (d - h * (s * s * jnp.mean(d * h, -1, keepdims=True)))).astype(BF16)
            dy[r, :] = n
            dyT[:, r] = n.T

    swap = [copy(s, d, tsem.at[i]) for i, (s, d) in enumerate(((h1_ref, dgu.at[:, pl.ds(0, W)]), (a0_ref, a), (a0T_ref, aT)))]

    def turn():
        wait(*swap)
        output_grad(0)
        output_grad(1)
        output_grad(2)
        output_grad(3)
        stream_a(2, NT - 1)
        stream_b(1, 1)

    first = [copy(a1_ref, a, tsem.at[0]), copy(dy_ref.at[0], dy, tsem.at[1]), copy(a1T_ref, aT, tsem.at[2]), copy(dyT_ref, dyT, tsem.at[3])]
    start(first[0], *tiles(0), down(0), *first[1:])
    ssacc[...] = jnp.zeros_like(ssacc)
    for ci in range(NC):
        da_at(ci)[...] = jnp.zeros((CH, D), F32)
    pl.semaphore_wait(bar, peers - 1)
    wait(*first[:2])

    @pl.loop(0, 2 * NT)
    def _(r):
        slot = lax.rem(r, 2)

        @pl.when((r == NT) | (r == NT + 2))
        def _():
            layer = 1 - (r - NT) // 2
            down_grads(layer, wd.at[1 - slot])

            @pl.when(layer == 1)
            def _():
                stream_b(0, 1)


        pl.when(r == NT)(turn)
        wait(*tiles(r), down(r))

        @pl.when(r + 1 < 2 * NT)
        def _():
            start(*tiles(r + 1), down(r + 1))

        @pl.when((r >= 1) & (r < NT))
        def _():
            wait(hid_out(r - 1))

        def A(ci):
            rows = pl.ds(ci * CH, CH)
            gu = dot(a[rows, :], wgu[slot])
            gus[ci % 2][0] = gu[:, :W]
            gus[ci % 2][1] = gu[:, W:]
            dhs[ci % 2][...] = dot_nt(dy[rows, :], wd[slot]).astype(BF16)

        def E(ci):
            rows = pl.ds(ci * CH, CH)
            gu = gus[ci % 2]
            g, u, d = gu[0], gu[1], dhs[ci % 2][...].astype(F32)
            s = sigmoid(g)
            silu = g * s
            hids[0, rows, :] = (silu * u).astype(BF16)
            dgu[rows, :W] = (d * u * (s + silu * (1.0 - s))).astype(BF16)
            dgu[rows, W:] = (d * silu).astype(BF16)

        for ci in range(NC):
            A(ci)
            if ci:
                E(ci - 1)
        E(NC - 1)

        @pl.when(r < NT - 1)
        def _():
            start(hid_out(r))

        @pl.when((r >= 1) & (r != NT))
        def _():
            stream_a(1, r - 1)

            @pl.when(r >= 2)
            def _():
                stream_a(3, r - 2)

            @pl.when(r == NT + 1)
            def _():
                stream_b(3, 1)

            @pl.when(r == NT + 2)
            def _():
                stream_b(0, 0)

        @pl.when(r == 0)
        def _():
            wait(*first[2:])

        gate_up_grads(r)
        stream_a(0, r)

        @pl.when(r < NT)
        def _():
            @pl.loop(0, 2)
            def _(half):
                for i, ref in enumerate((gu2, gu3)):
                    ref[half] += dot_nt(dgu[span(i * 2 + half, CH), :], wgu[slot])

            @pl.when(r == NT - 1)
            def _():
                start(*swap, hid_in(1, 1))

        @pl.when((r >= 1) & (r != NT))
        def _():
            stream_a(2, r - 1)

        @pl.when(r >= NT)
        def _():
            @pl.when(r == NT)
            def _():
                stream_b(2, 1)

            @pl.when(r == NT + 1)
            def _():
                start(hid_in(0, 0), hid_in(0, 1))

            @pl.when(r == NT + 2)
            def _():
                stream_b(1, 0)

            @pl.when(r == NT + 3)
            def _():
                stream_b(2, 0)

    R2 = NS * R

    def block(ref, i, layer, t):
        return ref.at[layer, span(i, R), span(t, W)]

    def nw(e, layer, t):
        return hids.at[e, span(layer * NT + t, R)]

    @pl.loop(0, NT)
    def _(t):
        for layer in range(2):
            for i, ref in enumerate((mg_ref, vg_ref, mu_ref, vu_ref)):
                start(copy(block(ref, 0, layer, t), gus[i].at[layer, span(t, R)], msem.at[i]))
            for e, ref in enumerate((wg_ref, wu_ref)):
                start(copy(block(ref, me, layer, t), nw(e, layer, t), nsem.at[e]))

    def arrived(ref, sem):
        wait(copy(ref, ref, sem))

    own_down = [copy(wd_ref.at[layer, span(me, R2), :], a.at[pl.ds(layer * R2, R2)], nsem.at[2 + layer]) for layer in range(2)]
    start(*own_down)

    last = 2 * NT - 1
    stream_a(1, last)
    stream_a(3, last - 1)
    stream_a(2, last)
    stream_b(3, 0)
    stream_a(3, last)

    lanes = ssall.shape[-1]
    part = ssacc[:, :lanes]
    for j in range(1, W // lanes):
        part = part + ssacc[:, j * lanes : (j + 1) * lanes]
    ssall[me] = part
    parts = [remote(ssall.at[me], ssall.at[me], sS.at[j], rS.at[j], lax.rem(me + j, peers)) for j in range(1, peers)]
    start(*parts)
    wait(*parts)
    total = ssall[0]
    for j in range(1, peers):
        total = total + ssall[j]
    total = jnp.sum(jnp.sum(total, 0, keepdims=True), 1, keepdims=True)
    fac = jnp.minimum(1.0, 0.5 * lax.rsqrt(total / z.count + 1e-30))
    fac_ref[...] = jnp.broadcast_to(fac, fac_ref.shape)

    def new_weight(w, m, v, g):
        w, g = w.astype(F32), g.astype(F32) * fac
        m = 0.9 * m + 0.1 * g
        v = 0.95 * v + 0.05 * g * g
        return (w - 0.02 * (m * lax.rsqrt(v + 1e-8) + 0.1 * w)).astype(BF16)

    outs = (og_ref, ou_ref)
    chunks = [(e, layer) for e in range(2) for layer in range(2)]

    def here(q, j):
        e, layer = chunks[q]
        return outs[e].at[layer, span(chip(j) * 2 + k, R)]

    def send(q, j, send, recv, to):
        return remote(here(q, j), here(q, j), send, recv, to)

    def right_of(q):
        return send(q, 0, sR.at[q], rR.at[q], chip(1) * 2 + k)

    def left_of(q):
        return send(q, 0, sL.at[q], rL.at[q], chip(-1) * 2 + k)

    def across(q):
        j = chunks[q][0] * 2 - 1
        return send(q, j, sX.at[q], rX.at[q], chip(-j) * 2 + k)

    def over(q, i):
        return send(q, (0, -1, 1, 2)[i], sD.at[q, i], rD.at[q, i], partner)

    def leave(q):
        arrived(here(q, 0), lsem.at[q])
        start(right_of(q), left_of(q), over(q, 0))

    for q, (e, layer) in enumerate(chunks):
        if layer == 0:
            arrived(hids.at[e, pl.ds(0, 2 * NT * R)], nsem.at[e])
            for i in (2 * e, 2 * e + 1):
                arrived(gus[i].at[:, pl.ds(0, NT * R)], msem.at[i])

        @pl.loop(0, NT)
        def _(t):
            held = span(t, R)
            own = nw(e, layer, t)
            own[...] = new_weight(own[...], gus[2 * e][layer, held], gus[2 * e + 1][layer, held], (gg_ref, gup_ref)[e][layer, :, span(t, W)])
            start(copy(own, block(outs[e], me, layer, t), lsem.at[q]))

        if q:
            leave(q - 1)
    leave(len(chunks) - 1)
    moments = [copy(ref, gus[i].at[:, pl.ds(0, R2)], msem.at[i]) for i, ref in enumerate((md_ref, vd_ref))]
    start(*moments)
    wait(*own_down, *moments)

    @pl.loop(0, NS)
    def _(i):
        for layer in range(2):
            held, own = span(i, R), span(layer * NS + i, R)
            a[own, :] = new_weight(a[own, :], gus[0][layer, held], gus[1][layer, held], gd_ref[layer, held])

    new_down = [copy(a.at[pl.ds(layer * R2, R2)], nd_ref.at[layer], nsem.at[2 + layer]) for layer in range(2)]
    start(*new_down)
    for q, (e, layer) in enumerate(chunks):
        right_of(q).wait_recv()
        if e == 0:
            start(across(q))
        start(over(q, 1))
        left_of(q).wait_recv()
        if e:
            start(across(q))
        start(over(q, 2))
    for q in range(len(chunks)):
        across(q).wait_recv()
        start(over(q, 3))
    wait(*new_down)
    for q in range(len(chunks)):
        wait(*[over(q, i) for i in range(4)])
        for sent in (right_of(q), left_of(q), across(q)):
            sent.wait_send()


def copy_kernel(og_ref, ou_ref, ng_ref, nu_ref, buf, isem, osem):
    n, rows = buf.shape[:2]
    per = n // 2
    ins, outs = [], []
    for i in range(n):
        src, dst = ((og_ref, ng_ref), (ou_ref, nu_ref))[i // per]
        at = pl.ds(i % per * rows, rows)
        ins.append(copy(src.at[at], buf.at[i], isem.at[i]))
        outs.append(copy(buf.at[i], dst.at[at], osem.at[i]))
    start(*ins)
    for i in range(n):
        wait(ins[i])
        start(outs[i])
    wait(*outs)


def moments_kernel(fac_ref, *refs):
    ins, outs = refs[:9], refs[9:]
    for i in range(3):
        m, v, g = (r[0] for r in ins[3 * i : 3 * i + 3])
        g = g.astype(F32) * fac_ref[:1, :1]
        outs[2 * i][0] = 0.9 * m + 0.1 * g
        outs[2 * i + 1][0] = 0.95 * v + 0.05 * g * g


def place_kernel(firsts, at_ref, *refs):
    out, sem = refs[-2:]
    copies = []
    for i, first in enumerate(firsts):
        count, rows = refs[i].shape[:2]
        copies.append(copy(refs[i], out.at[pl.ds(first, count), pl.ds(pl.multiple_of(at_ref[i] * rows, 16), rows)], sem.at[i]))
    start(*copies)
    wait(*copies)


VMEM, HBM = pl.BlockSpec(memory_space=pltpu.VMEM), pl.BlockSpec(memory_space=pl.ANY)
dma = pltpu.SemaphoreType.DMA


def bf16(*shape):
    return pltpu.VMEM(shape, BF16)


def f32(*shape):
    return pltpu.VMEM(shape, F32)


def call(kernel, ins, out, scratch, cost, limit=VMEM_LIMIT, **params):
    flops, moved = cost
    more = {key: params.pop(key) for key in ("grid", "input_output_aliases") if key in params}
    outs = [spec for _, _, spec in out]
    shapes = [jax.ShapeDtypeStruct(shape, dtype) for shape, dtype, _ in out]
    return pl.pallas_call(
        kernel,
        out_shape=shapes,
        in_specs=ins,
        out_specs=outs,
        scratch_shapes=scratch,
        compiler_params=pltpu.CompilerParams(vmem_limit_bytes=limit, **params),
        cost_estimate=pl.CostEstimate(flops=int(flops), bytes_accessed=int(moved), transcendentals=0),
        **more,
    )


def solution(mesh):
    n = mesh.shape["dp"]
    chips = n // 2

    def ring(shift, flip=0):
        return [(i, (i // 2 + shift) % chips * 2 + (i + flip) % 2) for i in range(n)]

    def right(t):
        return lax.ppermute(t, "dp", ring(1))

    def left(t):
        return lax.ppermute(t, "dp", ring(-1))

    def partner(t):
        return lax.ppermute(t, "dp", ring(0, 1))

    def step(x, dy, *arrays):
        weights, m, v = (arrays[i : i + 3] for i in (0, 3, 6))
        wg, wu, wd = weights
        T, D = x.shape[1:]
        layers, _, FF = wg.shape
        W, CH = D, 512
        NT, NC, R = FF // W, T // CH, D // n
        NS = FF // n // R
        z = SimpleNamespace(T=T, D=D, FF=FF, W=W, CH=CH, NT=NT, NC=NC, R=R, NS=NS, chips=chips, count=float(sum(w.size for w in weights)))
        tokens, turned, hidden = ((T, D), BF16, HBM), ((D, T), BF16, HBM), ((layers, NT, T, W), BF16, HBM)
        h1, a1, a1T, a0, a0T, dyT, hid = call(
            functools.partial(forward_kernel, z), [VMEM] + [HBM] * 4,
            [tokens, tokens, turned, tokens, turned, turned, hidden],
            [*[bf16(T, D)] * 2, *[bf16(D, T)] * 2, *[bf16(T, D)] * 2, bf16(D, T), bf16(2, D, 2 * W), bf16(FF, D), bf16(T, FF), *[f32(2, CH, W)] * 2,
             dma((2, 2)), dma((2,)), dma((NT,)), dma((NC + 1, 3))],
            (6 * T * D * FF, 8 * T * FF),
        )(x, dy, wg, wu, wd)
        slots = 6 + NS
        blocks = bf16(slots, R, W)
        flat, tall, gathered = (layers, R, FF), (layers, NS * R, D), (layers, D, FF)
        gg, gup, gd, fac, nd, og, ou, _ = call(
            functools.partial(backward_kernel, z), [HBM] * 17,
            [(flat, BF16, VMEM), (flat, BF16, VMEM), (tall, BF16, VMEM), ((8, 128), F32, VMEM), (tall, BF16, HBM),
             (gathered, BF16, HBM), (gathered, BF16, HBM), hidden],
            [bf16(T, D), bf16(D, T), bf16(T, D), bf16(D, T), bf16(2, D, 2 * W), bf16(2, W, D), *[f32(2, CH, W)] * 4, *[bf16(CH, W)] * 2,
             bf16(2, T, W), bf16(T, 2 * W),
             bf16(slots, chips, 2, R, W), bf16(slots, chips, R, W), blocks, blocks, blocks, f32(8, W), f32(n, 8, 128),
             dma((2, 2)), dma((2,)), dma((4,)), dma((2,)), *[dma((slots,))] * 8, dma((n,)), dma((n,)),
             *[dma((4,))] * 9, *[dma((4, 4))] * 2],
            (24 * T * D * FF, 8 * T * FF), collective_id=0, has_side_effects=True, input_output_aliases={16: 7},
        )(h1, a1, a1T, a0, a0T, dyT, dy, wg, wu, wd, m[0], v[0], m[1], v[1], m[2], v[2], hid)

        me = lax.axis_index("dp")
        c, k = me // 2, lax.rem(me, 2)

        def place(out, pieces):
            ts = [t for t, _, _ in pieces]
            count = len(ts)
            known = () if out is None else (out,)
            return call(
                functools.partial(place_kernel, [first for _, _, first in pieces]),
                [pl.BlockSpec(memory_space=pltpu.SMEM)] + [VMEM] * count + [HBM] * len(known), [(wd.shape, BF16, HBM)], [dma((count,))],
                (2e6 * count, 4 * sum(t.size for t in ts)), 1 << 24, input_output_aliases={count + 1: 0} if known else {},
            )(jnp.stack([at for _, at, _ in pieces]).astype(jnp.int32), *ts, *known)[0]

        def spot(shift, core):
            return lax.rem(c + shift + chips, chips) * 2 + core

        from_left, from_right = right(nd), left(nd)
        p_own = partner(nd)
        rows = layers * D
        parts = [(rows, FF), BF16, HBM]
        ng, nu = call(
            copy_kernel, [HBM] * 2, [parts] * 2, [bf16(8, rows // 4, FF), dma((8,)), dma((8,))], (12e9, 8 * rows * FF),
        )(og.reshape(rows, FF), ou.reshape(rows, FF))
        wide = pl.BlockSpec((1, R, W), lambda i, j: (i, 0, j))
        high = pl.BlockSpec((1, R, W), lambda i, j: (i, j, 0))
        kinds = ((flat, wide), (flat, wide), (tall, high))
        moved = call(
            moments_kernel, [pl.BlockSpec((8, 128), lambda i, j: (0, 0))] + [spec for _, spec in kinds for _ in range(3)],
            [(shape, F32, spec) for shape, spec in kinds for _ in range(2)], [], (10e9, 54 * m[0].size), grid=(layers, NT),
        )(fac, *[t for i, g in enumerate((gg, gup, gd)) for t in (m[i], v[i], g)])
        opp = right(from_left[:1]), left(from_right[1:])
        p_left, p_right = partner(from_left), partner(from_right)
        sides = ((nd, p_own, 0), (from_left, p_left, -1), (from_right, p_right, 1))
        out = place(None, [piece for t, p, j in sides for piece in ((t, spot(j, k), 0), (p, spot(j, 1 - k), 0))])
        p_opp = [partner(t) for t in opp]
        out = place(out, [piece for i in range(2) for piece in ((opp[i], spot(2, k), i), (p_opp[i], spot(2, 1 - k), i))])
        return ng.reshape(gathered), nu.reshape(gathered), out, *moved[::2], *moved[1::2]

    whole, split = P(None, None, None), P(None, "dp", None)
    step = jax.shard_map(
        step,
        mesh=mesh,
        in_specs=(P(("rep", "dp")),) * 2 + (whole,) * 3 + (split,) * 6,
        out_specs=(P("rep", None, None),) * 3 + (P("rep", "dp", None),) * 6,
        check_vma=False,
    )
    return step
```

time: 715 us -> 389 us (0.54); the launches traced: 706 us -> 389 us
  Pallas kernels: 0 us -> 350 us
  matrix products: 268 us -> 0 us
  waiting for transfers between devices: 287 us -> 22.1 us
  other arithmetic: 85.7 us -> 0.08 us
  local copies, waits for them, and re-layouts: 32.6 us -> 7.29 us
  between operations: 17.8 us -> 0.96 us
  blocking collectives: 14 us -> 0 us
  starting transfers between devices: 0.83 us -> 8.36 us
    pallas_call x0 -> x6, Pallas kernels: none -> 350 us  [the longest x1 278 us: step(): call(functools.partial(backward_kernel, z), [HBM] * 17, [(flat, BF16, VME...]
    dot_general x15 -> x0, matrix products: 268 us -> none  [the longest x5 94.6 us: layer(): up = jnp.dot(a, w['w_up'], preferred_element_type=jnp.float32)]
    unnamed x15 -> x0, waiting for transfers between devices: 161 us -> none
    reshape x3 -> x0, waiting for transfers between devices: 126 us -> none  [step(): t.reshape(-1, *t.shape[2:])]
    unnamed x5 -> x0, other arithmetic: 54.3 us -> none
    unnamed x39 -> x10, local copies, waits for them, and re-layouts: 32 us -> 5.55 us
    ppermute x0 -> x9, waiting for transfers between devices: none -> 22.1 us  [the longest x2 22.1 us: right(): return lax.ppermute(t, 'dp', ring(1))]
    reshape x3 -> x0, other arithmetic: 17.8 us -> none  [step(): t.reshape(-1, *t.shape[2:])]
  transfers between devices with their start and end apart: 9 -> 9, of which waited for: 7 -> 1; matrix products, arithmetic and copies ran while one was open for 20% -> 0% of each run, Pallas kernels for 0% -> 7%
where the time goes in v3:
time: 389 us
  Pallas kernels  350 us (90%)
  waiting for transfers between devices  22.1 us (6%)
  starting transfers between devices  8.36 us (2%)
  local copies, waits for them, and re-layouts  7.29 us (2%)
    pallas_call x1, Pallas kernels, step(): call(functools.partial(backward_kernel, z), [HBM] * 17, [(flat, BF16, VME...  278 us
    pallas_call x1, Pallas kernels, step(): call(functools.partial(forward_kernel, z), [VMEM] + [HBM] * 4, [tokens, t...  40.1 us
    ppermute x2, waiting for transfers between devices, right(): return lax.ppermute(t, 'dp', ring(1))  22.1 us
    pallas_call x1, Pallas kernels, step(): call(moments_kernel, [pl.BlockSpec((8, 128), lambda i, j: (0, 0))] + [spe...  12.9 us
    pallas_call x1, Pallas kernels, step(): call(copy_kernel, [HBM] * 2, [parts] * 2, [bf16(8, rows // 4, FF), dma((8...  11.6 us
  transfers between devices with their start and end apart: 9, of which 1 were waited for; matrix products, arithmetic and copies ran while one was open for 0% of the time, Pallas kernels for 7%

profile of v3, /device:TPU:113, one launch (start us, length us, event | category | flops | bytes accessed | tf_op | source)
XLA Modules:
  0.0 388.5 jit_solution(8761798898828878259)
XLA Ops:
  0.6 40.1 %shard_map.178 = (bf16[2048,640]{1,0:T(8,128)(2,1)}, bf16[2048,640]{1,0:T(8,128)(2,1)}, bf16[640,2048]{1,0:T(8,128)(2,1)}, bf16[2048,640]{1,0:T(8,128)(2,1)}, bf...) custom-call(bf16[1,2048,640]{2,1,0:T(8,128)(2,1)} %x_ref.1, ...), custom_call_target="tpu_custom_call" | custom-call | flops 25165824000 | bytes 52428800 | tf_op jit(solution)/shard_map/pallas_call | solution.py:654
  40.7 277.8 %shard_map.179 = (bf16[2,80,3200]{2,1,0:T(8,128)(2,1)}, bf16[2,80,3200]{2,1,0:T(8,128)(2,1)}, bf16[2,400,640]{2,1,0:T(8,128)(2,1)}, f32[8,128]{1,0:T(8,128)}, bf...) custom-call(bf16[2048,640]{1,0:T(8,128)(2,1)} %get-tuple-element.31., ...), custom_call_target="tpu_custom_call", output_to_operand_aliasing={{7}: (16, {})} | custom-call | flops 100663296000 | bytes 52428800 | tf_op jit(solution)/shard_map/pallas_call | solution.py:664
  318.5 0.4 collective-permute-start
  318.9 2.3 collective-permute-start.3
  321.2 0.7 collective-permute-start.6
  321.9 22.1 %collective-permute-done.refs_2_ = bf16[2,400,640]{2,1,0:T(8,128)(2,1)S(1)} collective-permute-done((bf16[2,400,640]{2,1,0:T(8,128)(2,1)}, bf16[2,400,640]{2,1,0:T(8,128)(2,1)S(1)}, u32[]{:S(2)}, u32[]{:S(2)}) %collective-permute-start) | collective-permute-done | bytes 1024032 | tf_op jit(solution)/shard_map/ppermute | solution.py:636
  344.0 1.0 copy-done
  345.0 0.8 slice.8
  345.8 1.0 copy-done.2
  346.8 0.8 slice.9
  347.6 2.7 collective-permute-start.4
  350.3 11.6 %shard_map.180 = (bf16[1280,3200]{1,0:T(8,128)(2,1)}, bf16[1280,3200]{1,0:T(8,128)(2,1)}) custom-call(bf16[1280,3200]{1,0:T(8,128)(2,1)} %bitcast.14, bf16[1280,3200]{1,0:T(8,128)(2,1)} %bitcast.15), custom_call_target="tpu_custom_call" | custom-call | flops 12000000000 | bytes 32768000 | tf_op jit(solution)/shard_map/pallas_call | solution.py:696
  361.9 1.6 collective-permute-start.7
  363.5 0.1 collective-permute-start.8
  363.6 0.4 collective-permute-start.2
  364.1 0.1 collective-permute-start.5
  364.2 12.9 %shard_map.183 = (f32[2,80,3200]{2,1,0:T(8,128)}, f32[2,80,3200]{2,1,0:T(8,128)}, f32[2,80,3200]{2,1,0:T(8,128)}, f32[2,80,3200]{2,1,0:T(8,128)}, f32[2,400,640]{2,1,0:T(8,128)}, /*index=5*/f32[2,400,640]{2,1,0:T(8,128)}) custom-call(f32[8,128]{1,0:T(8,128)} %get-tuple-element.43.fac_ref, f32[2,80,3200]{2,1,0:T(8,128)} %refs_0_.1, f32[2,80,3200]{2,1,0:T(8,128)} %refs_1_.1, ...), custom_call_target="tpu_custom_call" | custom-call | flops 10000000000 | bytes 27648000 | tf_op jit(solution)/shard_map/pallas_call | solution.py:702
  377.1 0.1 stack.41.at_ref
  377.2 0.1 pad_add_fusion.at_ref
  377.3 1.2 copy-done.1
  378.5 1.2 copy-done.3
  379.7 1.2 copy-done.4
  381.0 4.5 %shard_map.181.refs_4_ = bf16[2,3200,640]{2,1,0:T(8,128)(2,1)} custom-call(s32[6]{0:T(128)S(1)} %stack.41.at_ref, bf16[2,400,640]{2,1,0:T(8,128)(2,1)S(1)} %copy-done.4, bf16[2,400,640]{2,1,0:T(8,128)(2,1)} %collective-permute-done.6.refs_1_, bf16[2,400,640]{2,1,0:T(8,128)(2,1)S(1)} %copy-done.1, bf16[2,400,640]{2,1,0:T(8,128)(2,1)} %collective-permute-done.7.refs_3_, ...), custom_call_target="tpu_custom_call" | custom-call | flops 12000000 | bytes 12288000 | tf_op jit(solution)/shard_map/pallas_call | solution.py:683
  385.5 2.8 shard_map.182
  (14 shorter events, 0.0 us)
Async XLA Ops:
  318.5 25.5 %collective-permute-start = (bf16[2,400,640]{2,1,0:T(8,128)(2,1)}, bf16[2,400,640]{2,1,0:T(8,128)(2,1)S(1)}, u32[]{:S(2)}, u32[]{:S(2)}) collective-permute-start(bf16[2,400,640]{2,1,0:T(8,128)(2,1)} %get-tuple-element.42.refs_0_), channel_id=1, source_target_pairs={{0,2},{1,3},{2,4},{3,5},{4,6},{5,7},{6,0},{7,1},{8,10},{9,11},{10,... | collective-permute-start | bytes 3072008 | tf_op jit(solution)/shard_map/ppermute | solution.py:636
  318.9 26.9 %collective-permute-start.3 = (bf16[2,400,640]{2,1,0:T(8,128)(2,1)}, bf16[2,400,640]{2,1,0:T(8,128)(2,1)S(1)}, u32[]{:S(2)}, u32[]{:S(2)}) collective-permute-start(bf16[2,400,640]{2,1,0:T(8,128)(2,1)} %get-tuple-element.42.refs_0_), channel_id=1, source_target_pairs={{0,6},{1,7},{2,0},{3,1},{4,2},{5,3},{6,4},{7,5},{8,14},{9,15},{10,... | collective-permute-start | bytes 3072008 | tf_op jit(solution)/shard_map/ppermute | solution.py:639
  321.2 56.0 %collective-permute-start.6 = (bf16[2,400,640]{2,1,0:T(8,128)(2,1)}, bf16[2,400,640]{2,1,0:T(8,128)(2,1)}, u32[]{:S(2)}, u32[]{:S(2)}) collective-permute-start(bf16[2,400,640]{2,1,0:T(8,128)(2,1)} %get-tuple-element.42.refs_0_), channel_id=1, source_target_pairs={{0,1},{1,0},{2,3},{3,2},{4,5},{5,4},{6,7},{7,6},{8,9},{9,8},{10,11... | collective-permute-start | bytes 3072008 | tf_op jit(solution)/shard_map/ppermute | solution.py:642
  344.0 1.0 copy-start
  345.8 17.8 %collective-permute-start.1 = (bf16[1,400,640]{2,1,0:T(8,128)(2,1)}, bf16[1,400,640]{2,1,0:T(8,128)(2,1)}, u32[]{:S(2)}, u32[]{:S(2)}) collective-permute-start(bf16[1,400,640]{2,1,0:T(8,128)(2,1)} %slice.8), channel_id=1, source_target_pairs={{0,2},{1,3},{2,4},{3,5},{4,6},{5,7},{6,0},{7,1},{8,10},{9,11},{10,... | collective-permute-start | bytes 1536008 | tf_op jit(solution)/shard_map/ppermute | solution.py:636
  345.8 1.0 copy-start.2
  347.6 16.4 %collective-permute-start.4 = (bf16[1,400,640]{2,1,0:T(8,128)(2,1)}, bf16[1,400,640]{2,1,0:T(8,128)(2,1)}, u32[]{:S(2)}, u32[]{:S(2)}) collective-permute-start(bf16[1,400,640]{2,1,0:T(8,128)(2,1)} %slice.9), channel_id=1, source_target_pairs={{0,6},{1,7},{2,0},{3,1},{4,2},{5,3},{6,4},{7,5},{8,14},{9,15},{10,... | collective-permute-start | bytes 1536008 | tf_op jit(solution)/shard_map/ppermute | solution.py:639
  361.9 15.4 %collective-permute-start.7 = (bf16[2,400,640]{2,1,0:T(8,128)(2,1)}, bf16[2,400,640]{2,1,0:T(8,128)(2,1)}, u32[]{:S(2)}, u32[]{:S(2)}) collective-permute-start(bf16[2,400,640]{2,1,0:T(8,128)(2,1)} %copy-done), channel_id=1, source_target_pairs={{0,1},{1,0},{2,3},{3,2},{4,5},{5,4},{6,7},{7,6},{8,9},{9,8},{10,11... | collective-permute-start | bytes 3072008 | tf_op jit(solution)/shard_map/ppermute | solution.py:642
  363.5 13.8 %collective-permute-start.8 = (bf16[2,400,640]{2,1,0:T(8,128)(2,1)}, bf16[2,400,640]{2,1,0:T(8,128)(2,1)}, u32[]{:S(2)}, u32[]{:S(2)}) collective-permute-start(bf16[2,400,640]{2,1,0:T(8,128)(2,1)} %copy-done.2), channel_id=1, source_target_pairs={{0,1},{1,0},{2,3},{3,2},{4,5},{5,4},{6,7},{7,6},{8,9},{9,8},{10,11... | collective-permute-start | bytes 3072008 | tf_op jit(solution)/shard_map/ppermute | solution.py:642
  363.6 21.9 %collective-permute-start.2 = (bf16[1,400,640]{2,1,0:T(8,128)(2,1)}, bf16[1,400,640]{2,1,0:T(8,128)(2,1)}, u32[]{:S(2)}, u32[]{:S(2)}) collective-permute-start(bf16[1,400,640]{2,1,0:T(8,128)(2,1)} %collective-permute-done.1.refs_0_), channel_id=1, source_target_pairs={{0,1},{1,0},{2,3},{3,2},{4,5},{5,4},{6,7},{7,6},{8,9},{9,8},{10,11... | collective-permute-start | bytes 1536008 | tf_op jit(solution)/shard_map/ppermute | solution.py:642
  364.1 21.5 %collective-permute-start.5 = (bf16[1,400,640]{2,1,0:T(8,128)(2,1)}, bf16[1,400,640]{2,1,0:T(8,128)(2,1)}, u32[]{:S(2)}, u32[]{:S(2)}) collective-permute-start(bf16[1,400,640]{2,1,0:T(8,128)(2,1)} %collective-permute-done.4.refs_2_), channel_id=1, source_target_pairs={{0,1},{1,0},{2,3},{3,2},{4,5},{5,4},{6,7},{7,6},{8,9},{9,8},{10,11... | collective-permute-start | bytes 1536008 | tf_op jit(solution)/shard_map/ppermute | solution.py:642
  377.3 1.2 copy-start.1
  378.5 1.2 copy-start.3
  379.7 1.2 copy-start.4

commit v4 on v3

--- a/solution.py
+++ b/solution.py
@@ -134,7 +134,7 @@
 
 def backward_kernel(z, h1_ref, a1_ref, a1T_ref, a0_ref, a0T_ref, dyT_ref, dy_ref, wg_ref, wu_ref, wd_ref,
                     mg_ref, vg_ref, mu_ref, vu_ref, md_ref, vd_ref, _,
-                    gg_ref, gup_ref, gd_ref, fac_ref, nd_ref, og_ref, ou_ref, hid_ref,
+                    gg_ref, gup_ref, gd_ref, fac_ref, nd_ref, n0_ref, n1_ref, og_ref, ou_ref, hid_ref,
                     a, aT, dy, dyT, wgu, wd, gu0, gu1, gu2, gu3, dh0, dh1, hids, dgu,
                     G, PB, OB, B1, B2, ssacc, ssall,
                     wsem, dsem, tsem, hsem, sP, rP, sO, rO, s1, r1, s2, r2, sS, rS,
@@ -256,8 +256,8 @@
                 e, q = divmod(j + i, W)
                 G[a_slot(r, e), :, :, :, q : q + 128] = gw[:, i : i + 128].reshape(*G.shape[1:4], 128)
 
-    def hid_in(layer, i):
-        return copy(hid_ref.at[layer, NT - 1 - i], hids.at[lax.rem(i, 2)], hsem.at[lax.rem(i, 2)])
+    def hid_in(layer, i, slot):
+        return copy(hid_ref.at[layer, NT - 1 - i], hids.at[lax.rem(slot, 2)], hsem.at[lax.rem(slot, 2)])
 
     def turn_units(sd, i):
         for j in range(0, W, 128):
@@ -269,30 +269,26 @@
                     unit = G.at[NA + lax.rem(B, NS), B // (2 * NS), lax.rem(B // NS, 2)]
                     unit[lo - b * R : hi - b * R] = rows[lo - j : hi - j]
 
-    def down_grads(layer, sd):
-        @pl.loop(0, NT)
-        def _(i):
-            slot = lax.rem(i, 2)
-
-            @pl.when(i + 1 > layer)
-            def _():
-                wait(hid_in(layer, i))
-
-            turn_units(sd, jnp.maximum(i - 1, 0))
+    def down_grads(r, layer, sd):
+        def product(i):
             for j in range(0, W, 256):
                 n = min(256, W - j)
-                sd[:, j : j + n] = dot(dyT[...], hids[slot, :, j : j + n]).astype(BF16)
-
-            @pl.when(i + 2 < NT)
-            def _():
-                start(hid_in(layer, i + 2))
-
-            @pl.when((i == 1) & (layer == 1))
-            def _():
-                stream_a(1, NT - 1)
-                stream_a(3, NT - 2)
+                sd[:, j : j + n] = dot(dyT[...], hids[lax.rem(i, 2), :, j : j + n]).astype(BF16)
+            start(hid_in(layer, jnp.minimum(i + 2, NT - 1), i))
+
+        product(0)
+        stream_a(1, r)
+
+        @pl.loop(1, NT)
+        def _(i):
+            wait(hid_in(layer, i, i))
+            turn_units(sd, i - 1)
+            product(i)
 
         turn_units(sd, NT - 1)
+        stream_b(0, layer)
+        stream_a(3, r - 1)
+        wait(hid_in(layer, 0, 0), hid_in(layer, 0, 1))
 
     def da_at(ci):
         return (gu2, gu3)[ci // 2].at[ci % 2]
@@ -326,24 +322,12 @@
     ssacc[...] = jnp.zeros_like(ssacc)
     for ci in range(NC):
         da_at(ci)[...] = jnp.zeros((CH, D), F32)
-    pl.semaphore_wait(bar, peers - 1)
     wait(*first[:2])
 
     @pl.loop(0, 2 * NT)
     def _(r):
         slot = lax.rem(r, 2)
 
-        @pl.when((r == NT) | (r == NT + 2))
-        def _():
-            layer = 1 - (r - NT) // 2
-            down_grads(layer, wd.at[1 - slot])
-
-            @pl.when(layer == 1)
-            def _():
-                stream_b(0, 1)
-
-
-        pl.when(r == NT)(turn)
         wait(*tiles(r), down(r))
 
         @pl.when(r + 1 < 2 * NT)
@@ -381,7 +365,14 @@
         def _():
             start(hid_out(r))
 
-        @pl.when((r >= 1) & (r != NT))
+        @pl.when(r == 0)
+        def _():
+            pl.semaphore_wait(bar, peers - 1)
+            wait(*first[2:])
+
+        usual = (r != NT) & (r != NT + 2)
+
+        @pl.when((r >= 1) & usual)
         def _():
             stream_a(1, r - 1)
 
@@ -391,51 +382,56 @@
 
             @pl.when(r == NT + 1)
             def _():
+                start(hid_in(0, 0, 0), hid_in(0, 1, 1))
                 stream_b(3, 1)
 
-            @pl.when(r == NT + 2)
-            def _():
-                stream_b(0, 0)
-
-        @pl.when(r == 0)
-        def _():
-            wait(*first[2:])
+        @pl.when(r == NT + 2)
+        def _():
+            stream_b(1, 0)
 
         gate_up_grads(r)
         stream_a(0, r)
 
         @pl.when(r < NT)
         def _():
-            @pl.loop(0, 2)
-            def _(half):
-                for i, ref in enumerate((gu2, gu3)):
-                    ref[half] += dot_nt(dgu[span(i * 2 + half, CH), :], wgu[slot])
-
-            @pl.when(r == NT - 1)
-            def _():
-                start(*swap, hid_in(1, 1))
-
-        @pl.when((r >= 1) & (r != NT))
+            for ci in range(NC):
+                da_at(ci)[...] += dot_nt(dgu[pl.ds(ci * CH, CH), :], wgu[slot])
+
+        @pl.when((r >= 1) & usual)
         def _():
             stream_a(2, r - 1)
 
-        @pl.when(r >= NT)
+        @pl.when((r >= NT - 1) & (r < NT + 4))
         def _():
             @pl.when(r == NT)
             def _():
                 stream_b(2, 1)
 
-            @pl.when(r == NT + 1)
-            def _():
-                start(hid_in(0, 0), hid_in(0, 1))
-
-            @pl.when(r == NT + 2)
-            def _():
-                stream_b(1, 0)
-
             @pl.when(r == NT + 3)
             def _():
                 stream_b(2, 0)
+
+            @pl.when((r == NT - 1) | (r == NT + 1))
+            def _():
+                layer = (NT + 1 - r) // 2
+
+                @pl.when(layer == 1)
+                def _():
+                    start(*swap, hid_in(1, 1, 1))
+
+                @pl.when(layer == 0)
+                def _():
+                    wait(hid_in(0, 0, 0))
+
+                down_grads(r, layer, wd.at[slot])
+
+                @pl.when(layer == 1)
+                def _():
+                    turn()
+
+                @pl.when(layer == 0)
+                def _():
+                    stream_a(2, r)
 
     R2 = NS * R
 
@@ -540,7 +536,8 @@
             held, own = span(i, R), span(layer * NS + i, R)
             a[own, :] = new_weight(a[own, :], gus[0][layer, held], gus[1][layer, held], gd_ref[layer, held])
 
-    new_down = [copy(a.at[pl.ds(layer * R2, R2)], nd_ref.at[layer], nsem.at[2 + layer]) for layer in range(2)]
+    places = (n0_ref.at[0], n1_ref.at[0], nd_ref.at[0], nd_ref.at[1])
+    new_down = [copy(a.at[pl.ds(i % 2 * R2, R2)], place, nsem.at[i]) for i, place in enumerate(places)]
     start(*new_down)
     for q, (e, layer) in enumerate(chunks):
         right_of(q).wait_recv()
@@ -660,17 +657,17 @@
         )(x, dy, wg, wu, wd)
         slots = 6 + NS
         blocks = bf16(slots, R, W)
-        flat, tall, gathered = (layers, R, FF), (layers, NS * R, D), (layers, D, FF)
-        gg, gup, gd, fac, nd, og, ou, _ = call(
+        flat, tall, half, gathered = (layers, R, FF), (layers, NS * R, D), (1, NS * R, D), (layers, D, FF)
+        gg, gup, gd, fac, nd, n0, n1, og, ou, _ = call(
             functools.partial(backward_kernel, z), [HBM] * 17,
-            [(flat, BF16, VMEM), (flat, BF16, VMEM), (tall, BF16, VMEM), ((8, 128), F32, VMEM), (tall, BF16, HBM),
+            [(flat, BF16, VMEM), (flat, BF16, VMEM), (tall, BF16, VMEM), ((8, 128), F32, VMEM), (tall, BF16, HBM), (half, BF16, HBM), (half, BF16, HBM),
              (gathered, BF16, HBM), (gathered, BF16, HBM), hidden],
             [bf16(T, D), bf16(D, T), bf16(T, D), bf16(D, T), bf16(2, D, 2 * W), bf16(2, W, D), *[f32(2, CH, W)] * 4, *[bf16(CH, W)] * 2,
              bf16(2, T, W), bf16(T, 2 * W),
              bf16(slots, chips, 2, R, W), bf16(slots, chips, R, W), blocks, blocks, blocks, f32(8, W), f32(n, 8, 128),
              dma((2, 2)), dma((2,)), dma((4,)), dma((2,)), *[dma((slots,))] * 8, dma((n,)), dma((n,)),
              *[dma((4,))] * 9, *[dma((4, 4))] * 2],
-            (24 * T * D * FF, 8 * T * FF), collective_id=0, has_side_effects=True, input_output_aliases={16: 7},
+            (24 * T * D * FF, 8 * T * FF), collective_id=0, has_side_effects=True, input_output_aliases={16: 9},
         )(h1, a1, a1T, a0, a0T, dyT, dy, wg, wu, wd, m[0], v[0], m[1], v[1], m[2], v[2], hid)
 
         me = lax.axis_index("dp")
@@ -689,24 +686,25 @@
         def spot(shift, core):
             return lax.rem(c + shift + chips, chips) * 2 + core
 
-        from_left, from_right = right(nd), left(nd)
+        left0, right1 = right(n0), left(n1)
+        left1, right0 = right(n1), left(n0)
         p_own = partner(nd)
         rows = layers * D
         parts = [(rows, FF), BF16, HBM]
         ng, nu = call(
             copy_kernel, [HBM] * 2, [parts] * 2, [bf16(8, rows // 4, FF), dma((8,)), dma((8,))], (12e9, 8 * rows * FF),
         )(og.reshape(rows, FF), ou.reshape(rows, FF))
-        wide = pl.BlockSpec((1, R, W), lambda i, j: (i, 0, j))
-        high = pl.BlockSpec((1, R, W), lambda i, j: (i, j, 0))
-        kinds = ((flat, wide), (flat, wide), (tall, high))
+        opp = right(left0), left(right1)
+        kinds = [(shape, pl.BlockSpec((1, *shape[1:]), lambda i: (i, 0, 0))) for shape in (flat, flat, tall)]
         moved = call(
-            moments_kernel, [pl.BlockSpec((8, 128), lambda i, j: (0, 0))] + [spec for _, spec in kinds for _ in range(3)],
-            [(shape, F32, spec) for shape, spec in kinds for _ in range(2)], [], (10e9, 54 * m[0].size), grid=(layers, NT),
+            moments_kernel, [pl.BlockSpec((8, 128), lambda i: (0, 0))] + [spec for _, spec in kinds for _ in range(3)],
+            [(shape, F32, spec) for shape, spec in kinds for _ in range(2)], [], (10e9, 54 * m[0].size), grid=(layers,),
         )(fac, *[t for i, g in enumerate((gg, gup, gd)) for t in (m[i], v[i], g)])
-        opp = right(from_left[:1]), left(from_right[1:])
-        p_left, p_right = partner(from_left), partner(from_right)
-        sides = ((nd, p_own, 0), (from_left, p_left, -1), (from_right, p_right, 1))
-        out = place(None, [piece for t, p, j in sides for piece in ((t, spot(j, k), 0), (p, spot(j, 1 - k), 0))])
+        p_sides = [partner(t) for t in (left0, right1, left1, right0)]
+        pieces = [(nd, spot(0, k), 0), (p_own, spot(0, 1 - k), 0)]
+        for t, p, (j, first) in zip((left0, right1, left1, right0), p_sides, ((-1, 0), (1, 1), (-1, 1), (1, 0)), strict=True):
+            pieces += [(t, spot(j, k), first), (p, spot(j, 1 - k), first)]
+        out = place(None, pieces)
         p_opp = [partner(t) for t in opp]
         out = place(out, [piece for i in range(2) for piece in ((opp[i], spot(2, k), i), (p_opp[i], spot(2, 1 - k), i))])
         return ng.reshape(gathered), nu.reshape(gathered), out, *moved[::2], *moved[1::2]

time: 389 us -> 372 us (0.956)
  Pallas kernels: 350 us -> 341 us
  local copies, waits for them, and re-layouts: 7.29 us -> 1.3 us
    pallas_call x1, Pallas kernels: 278 us -> 272 us  [step(): call(functools.partial(backward_kernel, z), [HBM] * 17, [(flat, BF16, VME...]
    unnamed x10 -> x2, local copies, waits for them, and re-layouts: 5.55 us -> 1.21 us
    ppermute x2 -> x3, waiting for transfers between devices: 22.1 us -> 18.5 us  [right(): return lax.ppermute(t, 'dp', ring(1))]
  transfers between devices with their start and end apart: 9 -> 13, of which waited for: 1 -> 2; matrix products, arithmetic and copies ran while one was open for 0% -> 0% of each run, Pallas kernels for 7% -> 7%
where the time goes in v4:
time: 372 us; the launch traced here: 371 us
  Pallas kernels  341 us (92%)
  waiting for transfers between devices  18.6 us (5%)
  starting transfers between devices  9.85 us (3%)
    pallas_call x1, Pallas kernels, step(): call(functools.partial(backward_kernel, z), [HBM] * 17, [(flat, BF16, VME...  272 us
    pallas_call x1, Pallas kernels, step(): call(functools.partial(forward_kernel, z), [VMEM] + [HBM] * 4, [tokens, t...  40.1 us
    ppermute x3, waiting for transfers between devices, right(): return lax.ppermute(t, 'dp', ring(1))  18.5 us
    pallas_call x1, Pallas kernels, step(): call(copy_kernel, [HBM] * 2, [parts] * 2, [bf16(8, rows // 4, FF), dma((8...  11.6 us
    pallas_call x1, Pallas kernels, step(): call(moments_kernel, [pl.BlockSpec((8, 128), lambda i: (0, 0))] + [spec f...  9.46 us
    pallas_call x2, Pallas kernels, place(): call(functools.partial(place_kernel, [first for _, _, first in pieces]),...  7.98 us
  transfers between devices with their start and end apart: 13, of which 2 were waited for; matrix products, arithmetic and copies ran while one was open for 0% of the time, Pallas kernels for 7%

profile of v4, /device:TPU:113, one launch (start us, length us, event | category | flops | bytes accessed | tf_op | source)
XLA Modules:
  0.0 371.4 jit_solution(7079970576843423433)
XLA Ops:
  0.6 40.1 %shard_map.178 = (bf16[2048,640]{1,0:T(8,128)(2,1)}, bf16[2048,640]{1,0:T(8,128)(2,1)}, bf16[640,2048]{1,0:T(8,128)(2,1)}, bf16[2048,640]{1,0:T(8,128)(2,1)}, bf...) custom-call(bf16[1,2048,640]{2,1,0:T(8,128)(2,1)} %x_ref.1, ...), custom_call_target="tpu_custom_call" | custom-call | flops 25165824000 | bytes 52428800 | tf_op jit(solution)/shard_map/pallas_call | solution.py:651
  40.7 271.5 %shard_map.179 = (bf16[2,80,3200]{2,1,0:T(8,128)(2,1)}, bf16[2,80,3200]{2,1,0:T(8,128)(2,1)}, bf16[2,400,640]{2,1,0:T(8,128)(2,1)}, f32[8,128]{1,0:T(8,128)}, bf...) custom-call(bf16[2048,640]{1,0:T(8,128)(2,1)} %get-tuple-element.33., ...), custom_call_target="tpu_custom_call", output_to_operand_aliasing={{9}: (16, {})} | custom-call | flops 100663296000 | bytes 52428800 | tf_op jit(solution)/shard_map/pallas_call | solution.py:661
  312.2 0.3 collective-permute-start
  312.5 2.4 collective-permute-start.3
  315.0 0.0 collective-permute-start.9
  315.0 2.7 collective-permute-start.11
  317.6 9.2 %collective-permute-done.refs_2_ = bf16[1,400,640]{2,1,0:T(8,128)(2,1)} collective-permute-done((bf16[1,400,640]{2,1,0:T(8,128)(2,1)}, bf16[1,400,640]{2,1,0:T(8,128)(2,1)}, u32[]{:S(2)}, u32[]{:S(2)}) %collective-permute-start) | collective-permute-done | bytes 512032 | tf_op jit(solution)/shard_map/ppermute | solution.py:633
  326.9 1.6 collective-permute-start.7
  328.5 0.0 collective-permute-start.1
  328.5 0.1 collective-permute-start.8
  328.6 9.3 %collective-permute-done.9.refs_6_ = bf16[1,400,640]{2,1,0:T(8,128)(2,1)} collective-permute-done((bf16[1,400,640]{2,1,0:T(8,128)(2,1)}, bf16[1,400,640]{2,1,0:T(8,128)(2,1)}, u32[]{:S(2)}, u32[]{:S(2)}) %collective-permute-start.9) | collective-permute-done | bytes 512032 | tf_op jit(solution)/shard_map/ppermute | solution.py:633
  337.9 11.6 %shard_map.180 = (bf16[1280,3200]{1,0:T(8,128)(2,1)}, bf16[1280,3200]{1,0:T(8,128)(2,1)}) custom-call(bf16[1280,3200]{1,0:T(8,128)(2,1)} %bitcast.14, bf16[1280,3200]{1,0:T(8,128)(2,1)} %bitcast.15), custom_call_target="tpu_custom_call" | custom-call | flops 12000000000 | bytes 32768000 | tf_op jit(solution)/shard_map/pallas_call | solution.py:694
  349.5 1.7 collective-permute-start.6
  351.2 0.1 collective-permute-start.10
  351.3 0.4 collective-permute-start.12
  351.7 0.1 collective-permute-start.2
  351.8 0.5 collective-permute-start.5
  352.3 9.5 %shard_map.183 = (f32[2,80,3200]{2,1,0:T(8,128)}, f32[2,80,3200]{2,1,0:T(8,128)}, f32[2,80,3200]{2,1,0:T(8,128)}, f32[2,80,3200]{2,1,0:T(8,128)}, f32[2,400,640]{2,1,0:T(8,128)}, /*index=5*/f32[2,400,640]{2,1,0:T(8,128)}) custom-call(f32[8,128]{1,0:T(8,128)} %get-tuple-element.47.fac_ref, f32[2,80,3200]{2,1,0:T(8,128)} %refs_0_.1, f32[2,80,3200]{2,1,0:T(8,128)} %refs_1_.1, ...), custom_call_target="tpu_custom_call" | custom-call | flops 10000000000 | bytes 27648000 | tf_op jit(solution)/shard_map/pallas_call | solution.py:699
  361.8 0.1 stack.45.at_ref
  361.9 0.1 pad_add_fusion.at_ref
  362.0 0.0 collective-permute-done.6.refs_1_
  362.0 1.2 copy-done
  363.2 5.1 %shard_map.181.refs_4_ = bf16[2,3200,640]{2,1,0:T(8,128)(2,1)} custom-call(s32[10]{0:T(128)S(1)} %stack.45.at_ref, bf16[2,400,640]{2,1,0:T(8,128)(2,1)S(1)} %copy-done, bf16[2,400,640]{2,1,0:T(8,128)(2,1)} %collective-permute-done.6.refs_1_, bf16[1,400,640]{2,1,0:T(8,128)(2,1)} %collective-permute-done.refs_2_, ...), custom_call_target="tpu_custom_call" | custom-call | flops 20000000 | bytes 12288000 | tf_op jit(solution)/shard_map/pallas_call | solution.py:680
  368.3 2.8 shard_map.182
  (12 shorter events, 0.0 us)
Async XLA Ops:
  312.2 14.7 %collective-permute-start = (bf16[1,400,640]{2,1,0:T(8,128)(2,1)}, bf16[1,400,640]{2,1,0:T(8,128)(2,1)}, u32[]{:S(2)}, u32[]{:S(2)}) collective-permute-start(bf16[1,400,640]{2,1,0:T(8,128)(2,1)} %get-tuple-element.44), channel_id=1, source_target_pairs={{0,2},{1,3},{2,4},{3,5},{4,6},{5,7},{6,0},{7,1},{8,10},{9,11},{10,... | collective-permute-start | bytes 1536008 | tf_op jit(solution)/shard_map/ppermute | solution.py:633
  312.5 16.0 %collective-permute-start.3 = (bf16[1,400,640]{2,1,0:T(8,128)(2,1)}, bf16[1,400,640]{2,1,0:T(8,128)(2,1)}, u32[]{:S(2)}, u32[]{:S(2)}) collective-permute-start(bf16[1,400,640]{2,1,0:T(8,128)(2,1)} %get-tuple-element.45), channel_id=1, source_target_pairs={{0,6},{1,7},{2,0},{3,1},{4,2},{5,3},{6,4},{7,5},{8,14},{9,15},{10,... | collective-permute-start | bytes 1536008 | tf_op jit(solution)/shard_map/ppermute | solution.py:636
  315.0 22.9 %collective-permute-start.9 = (bf16[1,400,640]{2,1,0:T(8,128)(2,1)}, bf16[1,400,640]{2,1,0:T(8,128)(2,1)}, u32[]{:S(2)}, u32[]{:S(2)}) collective-permute-start(bf16[1,400,640]{2,1,0:T(8,128)(2,1)} %get-tuple-element.45), channel_id=1, source_target_pairs={{0,2},{1,3},{2,4},{3,5},{4,6},{5,7},{6,0},{7,1},{8,10},{9,11},{10,... | collective-permute-start | bytes 1536008 | tf_op jit(solution)/shard_map/ppermute | solution.py:633
  315.0 34.5 %collective-permute-start.11 = (bf16[1,400,640]{2,1,0:T(8,128)(2,1)}, bf16[1,400,640]{2,1,0:T(8,128)(2,1)}, u32[]{:S(2)}, u32[]{:S(2)}) collective-permute-start(bf16[1,400,640]{2,1,0:T(8,128)(2,1)} %get-tuple-element.44), channel_id=1, source_target_pairs={{0,6},{1,7},{2,0},{3,1},{4,2},{5,3},{6,4},{7,5},{8,14},{9,15},{10,... | collective-permute-start | bytes 1536008 | tf_op jit(solution)/shard_map/ppermute | solution.py:636
  326.9 24.3 %collective-permute-start.7 = (bf16[1,400,640]{2,1,0:T(8,128)(2,1)}, bf16[1,400,640]{2,1,0:T(8,128)(2,1)}, u32[]{:S(2)}, u32[]{:S(2)}) collective-permute-start(bf16[1,400,640]{2,1,0:T(8,128)(2,1)} %collective-permute-done.refs_2_), channel_id=1, source_target_pairs={{0,1},{1,0},{2,3},{3,2},{4,5},{5,4},{6,7},{7,6},{8,9},{9,8},{10,11... | collective-permute-start | bytes 1536008 | tf_op jit(solution)/shard_map/ppermute | solution.py:639
  328.5 23.2 %collective-permute-start.1 = (bf16[1,400,640]{2,1,0:T(8,128)(2,1)}, bf16[1,400,640]{2,1,0:T(8,128)(2,1)}, u32[]{:S(2)}, u32[]{:S(2)}) collective-permute-start(bf16[1,400,640]{2,1,0:T(8,128)(2,1)} %collective-permute-done.refs_2_), channel_id=1, source_target_pairs={{0,2},{1,3},{2,4},{3,5},{4,6},{5,7},{6,0},{7,1},{8,10},{9,11},{10,... | collective-permute-start | bytes 1536008 | tf_op jit(solution)/shard_map/ppermute | solution.py:633
  328.5 22.8 %collective-permute-start.8 = (bf16[1,400,640]{2,1,0:T(8,128)(2,1)}, bf16[1,400,640]{2,1,0:T(8,128)(2,1)}, u32[]{:S(2)}, u32[]{:S(2)}) collective-permute-start(bf16[1,400,640]{2,1,0:T(8,128)(2,1)} %collective-permute-done.3.refs_4_), channel_id=1, source_target_pairs={{0,1},{1,0},{2,3},{3,2},{4,5},{5,4},{6,7},{7,6},{8,9},{9,8},{10,11... | collective-permute-start | bytes 1536008 | tf_op jit(solution)/shard_map/ppermute | solution.py:639
  337.9 13.9 %collective-permute-start.4 = (bf16[1,400,640]{2,1,0:T(8,128)(2,1)}, bf16[1,400,640]{2,1,0:T(8,128)(2,1)}, u32[]{:S(2)}, u32[]{:S(2)}) collective-permute-start(bf16[1,400,640]{2,1,0:T(8,128)(2,1)} %collective-permute-done.3.refs_4_), channel_id=1, source_target_pairs={{0,6},{1,7},{2,0},{3,1},{4,2},{5,3},{6,4},{7,5},{8,14},{9,15},{10,... | collective-permute-start | bytes 1536008 | tf_op jit(solution)/shard_map/ppermute | solution.py:636
  349.5 12.4 %collective-permute-start.6 = (bf16[2,400,640]{2,1,0:T(8,128)(2,1)}, bf16[2,400,640]{2,1,0:T(8,128)(2,1)}, u32[]{:S(2)}, u32[]{:S(2)}) collective-permute-start(bf16[2,400,640]{2,1,0:T(8,128)(2,1)} %get-tuple-element.46.refs_0_), channel_id=1, source_target_pairs={{0,1},{1,0},{2,3},{3,2},{4,5},{5,4},{6,7},{7,6},{8,9},{9,8},{10,11... | collective-permute-start | bytes 3072008 | tf_op jit(solution)/shard_map/ppermute | solution.py:639
  351.2 10.8 %collective-permute-start.10 = (bf16[1,400,640]{2,1,0:T(8,128)(2,1)}, bf16[1,400,640]{2,1,0:T(8,128)(2,1)}, u32[]{:S(2)}, u32[]{:S(2)}) collective-permute-start(bf16[1,400,640]{2,1,0:T(8,128)(2,1)} %collective-permute-done.9.refs_6_), channel_id=1, source_target_pairs={{0,1},{1,0},{2,3},{3,2},{4,5},{5,4},{6,7},{7,6},{8,9},{9,8},{10,11... | collective-permute-start | bytes 1536008 | tf_op jit(solution)/shard_map/ppermute | solution.py:639
  351.3 10.7 %collective-permute-start.12 = (bf16[1,400,640]{2,1,0:T(8,128)(2,1)}, bf16[1,400,640]{2,1,0:T(8,128)(2,1)}, u32[]{:S(2)}, u32[]{:S(2)}) collective-permute-start(bf16[1,400,640]{2,1,0:T(8,128)(2,1)} %collective-permute-done.11.refs_8_), channel_id=1, source_target_pairs={{0,1},{1,0},{2,3},{3,2},{4,5},{5,4},{6,7},{7,6},{8,9},{9,8},{10,11... | collective-permute-start | bytes 1536008 | tf_op jit(solution)/shard_map/ppermute | solution.py:639
  351.7 16.6 %collective-permute-start.2 = (bf16[1,400,640]{2,1,0:T(8,128)(2,1)}, bf16[1,400,640]{2,1,0:T(8,128)(2,1)}, u32[]{:S(2)}, u32[]{:S(2)}) collective-permute-start(bf16[1,400,640]{2,1,0:T(8,128)(2,1)} %collective-permute-done.1.refs_0_), channel_id=1, source_target_pairs={{0,1},{1,0},{2,3},{3,2},{4,5},{5,4},{6,7},{7,6},{8,9},{9,8},{10,11... | collective-permute-start | bytes 1536008 | tf_op jit(solution)/shard_map/ppermute | solution.py:639
  351.8 16.5 %collective-permute-start.5 = (bf16[1,400,640]{2,1,0:T(8,128)(2,1)}, bf16[1,400,640]{2,1,0:T(8,128)(2,1)}, u32[]{:S(2)}, u32[]{:S(2)}) collective-permute-start(bf16[1,400,640]{2,1,0:T(8,128)(2,1)} %collective-permute-done.4.refs_2_), channel_id=1, source_target_pairs={{0,1},{1,0},{2,3},{3,2},{4,5},{5,4},{6,7},{7,6},{8,9},{9,8},{10,11... | collective-permute-start | bytes 1536008 | tf_op jit(solution)/shard_map/ppermute | solution.py:639
  362.0 1.2 copy-start

commit v5 on v4

--- a/solution.py
+++ b/solution.py
@@ -56,21 +56,21 @@
 
 
 def forward_kernel(z, x_ref, dy_ref, wg_ref, wu_ref, wd_ref, h1_ref, a1_ref, a1T_ref, a0_ref, a0T_ref, dyT_ref, hid_ref,
-                   a, a1, aT, cT, h1, dy, dyT, wgu, wd, hid, gu0, gu1, wsem, dsem, hsem, tsem):
+                   x, a, a1, aT, cT, h1, dy, dyT, wgu, wd, hid, gu0, gu1, wsem, dsem, hsem, tsem):
     W, CH, NT, NC, T = z.W, z.CH, z.NT, z.NC, z.T
     gus = (gu0, gu1)
     tiles = gate_up_tiles(z, lambda t: 0, wg_ref, wu_ref, wgu, wsem)
-    later = [copy(dy_ref.at[0], dy, dsem.at[0]), copy(wd_ref.at[0], wd, dsem.at[1])]
-    start(*tiles(0), *later)
+    states, later, down = copy(x_ref.at[0], x, dsem.at[0]), copy(dy_ref.at[0], dy, dsem.at[1]), copy(wd_ref.at[0], wd, dsem.at[2])
+    start(states, *tiles(0), later)
+    wait(states)
     step = CH // 2
     for i in range(T // step):
         r = pl.ds(i * step, step)
-        h = x_ref[0, r, :].astype(F32)
+        h = x[r, :].astype(F32)
         a[r, :] = (h * scale_of(h)).astype(BF16)
     pairs = (a, a0_ref), (aT, a0T_ref), (dyT, dyT_ref)
     whole = [copy(s, d, tsem.at[0, e]) for e, (s, d) in enumerate(pairs)]
-    start(whole[0])
-    wait(later[0])
+    wait(later)
 
     def hid_out(t):
         return copy(hid.at[:, span(t, W)], hid_ref.at[0, t], hsem.at[t])
@@ -82,6 +82,10 @@
         @pl.when(t + 1 < NT)
         def _():
             start(*tiles(t + 1))
+
+        @pl.when(t == 1)
+        def _():
+            start(down)
 
         turned = span(jnp.minimum(t, NC - 1), CH)
         aT[:, turned] = a[turned, :].T
@@ -100,12 +104,12 @@
         E(NC - 1)
         start(hid_out(t))
 
-    start(*whole[1:])
-    wait(later[1])
+    start(*whole)
+    wait(down)
 
     def project(i):
         r = span(i, CH)
-        h1[r, :] = x_ref[0, r, :] + dot(hid[r, :], wd[...]).astype(BF16)
+        h1[r, :] = x[r, :] + dot(hid[r, :], wd[...]).astype(BF16)
 
     def norm(i):
         r = span(i, CH)
@@ -134,9 +138,9 @@
 
 def backward_kernel(z, h1_ref, a1_ref, a1T_ref, a0_ref, a0T_ref, dyT_ref, dy_ref, wg_ref, wu_ref, wd_ref,
                     mg_ref, vg_ref, mu_ref, vu_ref, md_ref, vd_ref, _,
-                    gg_ref, gup_ref, gd_ref, fac_ref, nd_ref, n0_ref, n1_ref, og_ref, ou_ref, hid_ref,
+                    gg_out, gup_out, gd_out, fac_out, nd_ref, n0_ref, n1_ref, og_ref, ou_ref, hid_ref,
                     a, aT, dy, dyT, wgu, wd, gu0, gu1, gu2, gu3, dh0, dh1, hids, dgu,
-                    G, PB, OB, B1, B2, ssacc, ssall,
+                    G, PB, OB, B1, B2, gg_ref, gup_ref, gd_ref, fac_ref, ssacc, ssall,
                     wsem, dsem, tsem, hsem, sP, rP, sO, rO, s1, r1, s2, r2, sS, rS,
                     msem, nsem, lsem, sR, rR, sL, rL, sX, rX, sD, rD):
     W, CH, NT, NC, D, R, NS = z.W, z.CH, z.NT, z.NC, z.D, z.R, z.NS
@@ -318,11 +322,12 @@
         stream_b(1, 1)
 
     first = [copy(a1_ref, a, tsem.at[0]), copy(dy_ref.at[0], dy, tsem.at[1]), copy(a1T_ref, aT, tsem.at[2]), copy(dyT_ref, dyT, tsem.at[3])]
-    start(first[0], *tiles(0), down(0), *first[1:])
+    start(first[0], *tiles(0), down(0), first[1])
     ssacc[...] = jnp.zeros_like(ssacc)
     for ci in range(NC):
         da_at(ci)[...] = jnp.zeros((CH, D), F32)
     wait(*first[:2])
+    start(*first[2:])
 
     @pl.loop(0, 2 * NT)
     def _(r):
@@ -351,7 +356,7 @@
             g, u, d = gu[0], gu[1], dhs[ci % 2][...].astype(F32)
             s = sigmoid(g)
             silu = g * s
-            hids[0, rows, :] = (silu * u).astype(BF16)
+            hids[r // NT, rows, :] = (silu * u).astype(BF16)
             dgu[rows, :W] = (d * u * (s + silu * (1.0 - s))).astype(BF16)
             dgu[rows, W:] = (d * silu).astype(BF16)
 
@@ -359,11 +364,6 @@
             A(ci)
             if ci:
                 E(ci - 1)
-        E(NC - 1)
-
-        @pl.when(r < NT - 1)
-        def _():
-            start(hid_out(r))
 
         @pl.when(r == 0)
         def _():
@@ -382,15 +382,20 @@
 
             @pl.when(r == NT + 1)
             def _():
-                start(hid_in(0, 0, 0), hid_in(0, 1, 1))
+                start(hid_in(0, 0, 0))
                 stream_b(3, 1)
 
         @pl.when(r == NT + 2)
         def _():
             stream_b(1, 0)
 
+        E(NC - 1)
         gate_up_grads(r)
         stream_a(0, r)
+
+        @pl.when(r < NT - 1)
+        def _():
+            start(hid_out(r))
 
         @pl.when(r < NT)
         def _():
@@ -421,6 +426,7 @@
 
                 @pl.when(layer == 0)
                 def _():
+                    start(hid_in(0, 1, 1))
                     wait(hid_in(0, 0, 0))
 
                 down_grads(r, layer, wd.at[slot])
@@ -476,6 +482,9 @@
     total = jnp.sum(jnp.sum(total, 0, keepdims=True), 1, keepdims=True)
     fac = jnp.minimum(1.0, 0.5 * lax.rsqrt(total / z.count + 1e-30))
     fac_ref[...] = jnp.broadcast_to(fac, fac_ref.shape)
+    pairs = (gg_ref, gg_out), (gup_ref, gup_out), (gd_ref, gd_out), (fac_ref, fac_out)
+    leaving = [copy(s, d, tsem.at[i]) for i, (s, d) in enumerate(pairs)]
+    start(*leaving)
 
     def new_weight(w, m, v, g):
         w, g = w.astype(F32), g.astype(F32) * fac
@@ -548,10 +557,10 @@
         if e:
             start(across(q))
         start(over(q, 2))
-    for q in range(len(chunks)):
+    for q in (0, 2, 1, 3):
         across(q).wait_recv()
         start(over(q, 3))
-    wait(*new_down)
+    wait(*new_down, *leaving)
     for q in range(len(chunks)):
         wait(*[over(q, i) for i in range(4)])
         for sent in (right_of(q), left_of(q), across(q)):
@@ -649,10 +658,10 @@
         z = SimpleNamespace(T=T, D=D, FF=FF, W=W, CH=CH, NT=NT, NC=NC, R=R, NS=NS, chips=chips, count=float(sum(w.size for w in weights)))
         tokens, turned, hidden = ((T, D), BF16, HBM), ((D, T), BF16, HBM), ((layers, NT, T, W), BF16, HBM)
         h1, a1, a1T, a0, a0T, dyT, hid = call(
-            functools.partial(forward_kernel, z), [VMEM] + [HBM] * 4,
+            functools.partial(forward_kernel, z), [HBM] * 5,
             [tokens, tokens, turned, tokens, turned, turned, hidden],
-            [*[bf16(T, D)] * 2, *[bf16(D, T)] * 2, *[bf16(T, D)] * 2, bf16(D, T), bf16(2, D, 2 * W), bf16(FF, D), bf16(T, FF), *[f32(2, CH, W)] * 2,
-             dma((2, 2)), dma((2,)), dma((NT,)), dma((NC + 1, 3))],
+            [*[bf16(T, D)] * 3, *[bf16(D, T)] * 2, *[bf16(T, D)] * 2, bf16(D, T), bf16(2, D, 2 * W), bf16(FF, D), bf16(T, FF), *[f32(2, CH, W)] * 2,
+             dma((2, 2)), dma((3,)), dma((NT,)), dma((NC + 1, 3))],
             (6 * T * D * FF, 8 * T * FF),
         )(x, dy, wg, wu, wd)
         slots = 6 + NS
@@ -660,11 +669,12 @@
         flat, tall, half, gathered = (layers, R, FF), (layers, NS * R, D), (1, NS * R, D), (layers, D, FF)
         gg, gup, gd, fac, nd, n0, n1, og, ou, _ = call(
             functools.partial(backward_kernel, z), [HBM] * 17,
-            [(flat, BF16, VMEM), (flat, BF16, VMEM), (tall, BF16, VMEM), ((8, 128), F32, VMEM), (tall, BF16, HBM), (half, BF16, HBM), (half, BF16, HBM),
+            [(flat, BF16, HBM), (flat, BF16, HBM), (tall, BF16, HBM), ((8, 128), F32, HBM), (tall, BF16, HBM), (half, BF16, HBM), (half, BF16, HBM),
              (gathered, BF16, HBM), (gathered, BF16, HBM), hidden],
             [bf16(T, D), bf16(D, T), bf16(T, D), bf16(D, T), bf16(2, D, 2 * W), bf16(2, W, D), *[f32(2, CH, W)] * 4, *[bf16(CH, W)] * 2,
              bf16(2, T, W), bf16(T, 2 * W),
-             bf16(slots, chips, 2, R, W), bf16(slots, chips, R, W), blocks, blocks, blocks, f32(8, W), f32(n, 8, 128),
+             bf16(slots, chips, 2, R, W), bf16(slots, chips, R, W), blocks, blocks, blocks, bf16(*flat), bf16(*flat), bf16(*tall), f32(8, 128),
+             f32(8, W), f32(n, 8, 128),
              dma((2, 2)), dma((2,)), dma((4,)), dma((2,)), *[dma((slots,))] * 8, dma((n,)), dma((n,)),
              *[dma((4,))] * 9, *[dma((4, 4))] * 2],
             (24 * T * D * FF, 8 * T * FF), collective_id=0, has_side_effects=True, input_output_aliases={16: 9},

time: 372 us -> 366 us (0.984)
  Pallas kernels: 341 us -> 335 us
    pallas_call x2, Pallas kernels: 312 us -> 306 us  [the longest x1 268 us: step(): call(functools.partial(backward_kernel, z), [HBM] * 17, [(flat, BF16, HBM...]
where the time goes in v5:
time: 366 us
  Pallas kernels  335 us (92%)
  waiting for transfers between devices  18.6 us (5%)
  starting transfers between devices  9.85 us (3%)
    pallas_call x1, Pallas kernels, step(): call(functools.partial(backward_kernel, z), [HBM] * 17, [(flat, BF16, HBM...  268 us
    pallas_call x1, Pallas kernels, step(): call(functools.partial(forward_kernel, z), [HBM] * 5, [tokens, tokens, tu...  38.2 us
    ppermute x3, waiting for transfers between devices, right(): return lax.ppermute(t, 'dp', ring(1))  18.5 us
    pallas_call x1, Pallas kernels, step(): call(copy_kernel, [HBM] * 2, [parts] * 2, [bf16(8, rows // 4, FF), dma((8...  11.6 us
    pallas_call x1, Pallas kernels, step(): call(moments_kernel, [pl.BlockSpec((8, 128), lambda i: (0, 0))] + [spec f...  9.46 us
    pallas_call x2, Pallas kernels, place(): call(functools.partial(place_kernel, [first for _, _, first in pieces]),...  7.98 us
  transfers between devices with their start and end apart: 13, of which 2 were waited for; matrix products, arithmetic and copies ran while one was open for 0% of the time, Pallas kernels for 7%

profile of v5, /device:TPU:113, one launch (start us, length us, event | category | flops | bytes accessed | tf_op | source)
XLA Modules:
  0.0 366.1 jit_solution(7351942288280175284)
XLA Ops:
  0.6 38.2 %shard_map.178 = (bf16[2048,640]{1,0:T(8,128)(2,1)}, bf16[2048,640]{1,0:T(8,128)(2,1)}, bf16[640,2048]{1,0:T(8,128)(2,1)}, bf16[2048,640]{1,0:T(8,128)(2,1)}, bf...) custom-call(bf16[1,2048,640]{2,1,0:T(8,128)(2,1)} %x_ref.1, ...), custom_call_target="tpu_custom_call" | custom-call | flops 25165824000 | bytes 52428800 | tf_op jit(solution)/shard_map/pallas_call | solution.py:660
  38.9 268.1 %shard_map.179 = (bf16[2,80,3200]{2,1,0:T(8,128)(2,1)}, bf16[2,80,3200]{2,1,0:T(8,128)(2,1)}, bf16[2,400,640]{2,1,0:T(8,128)(2,1)}, f32[8,128]{1,0:T(8,128)}, bf...) custom-call(bf16[2048,640]{1,0:T(8,128)(2,1)} %get-tuple-element.33., ...), custom_call_target="tpu_custom_call", output_to_operand_aliasing={{9}: (16, {})} | custom-call | flops 100663296000 | bytes 52428800 | tf_op jit(solution)/shard_map/pallas_call | solution.py:670
  306.9 0.4 collective-permute-start
  307.3 2.4 collective-permute-start.3
  309.7 0.0 collective-permute-start.9
  309.7 2.7 collective-permute-start.11
  312.4 9.2 %collective-permute-done.refs_2_ = bf16[1,400,640]{2,1,0:T(8,128)(2,1)} collective-permute-done((bf16[1,400,640]{2,1,0:T(8,128)(2,1)}, bf16[1,400,640]{2,1,0:T(8,128)(2,1)}, u32[]{:S(2)}, u32[]{:S(2)}) %collective-permute-start) | collective-permute-done | bytes 512032 | tf_op jit(solution)/shard_map/ppermute | solution.py:642
  321.6 1.6 collective-permute-start.7
  323.2 0.0 collective-permute-start.1
  323.2 0.1 collective-permute-start.8
  323.3 9.3 %collective-permute-done.9.refs_6_ = bf16[1,400,640]{2,1,0:T(8,128)(2,1)} collective-permute-done((bf16[1,400,640]{2,1,0:T(8,128)(2,1)}, bf16[1,400,640]{2,1,0:T(8,128)(2,1)}, u32[]{:S(2)}, u32[]{:S(2)}) %collective-permute-start.9) | collective-permute-done | bytes 512032 | tf_op jit(solution)/shard_map/ppermute | solution.py:642
  332.6 11.6 %shard_map.180 = (bf16[1280,3200]{1,0:T(8,128)(2,1)}, bf16[1280,3200]{1,0:T(8,128)(2,1)}) custom-call(bf16[1280,3200]{1,0:T(8,128)(2,1)} %bitcast.14, bf16[1280,3200]{1,0:T(8,128)(2,1)} %bitcast.15), custom_call_target="tpu_custom_call" | custom-call | flops 12000000000 | bytes 32768000 | tf_op jit(solution)/shard_map/pallas_call | solution.py:704
  344.2 1.7 collective-permute-start.6
  345.9 0.1 collective-permute-start.10
  346.0 0.4 collective-permute-start.12
  346.4 0.1 collective-permute-start.2
  346.5 0.5 collective-permute-start.5
  347.0 9.5 %shard_map.183 = (f32[2,80,3200]{2,1,0:T(8,128)}, f32[2,80,3200]{2,1,0:T(8,128)}, f32[2,80,3200]{2,1,0:T(8,128)}, f32[2,80,3200]{2,1,0:T(8,128)}, f32[2,400,640]{2,1,0:T(8,128)}, /*index=5*/f32[2,400,640]{2,1,0:T(8,128)}) custom-call(f32[8,128]{1,0:T(8,128)} %get-tuple-element.47.fac_ref, f32[2,80,3200]{2,1,0:T(8,128)} %refs_0_.1, f32[2,80,3200]{2,1,0:T(8,128)} %refs_1_.1, ...), custom_call_target="tpu_custom_call" | custom-call | flops 10000000000 | bytes 27648000 | tf_op jit(solution)/shard_map/pallas_call | solution.py:709
  356.5 0.1 stack.45.at_ref
  356.6 0.1 pad_add_fusion.at_ref
  356.7 0.0 collective-permute-done.6.refs_1_
  356.7 1.2 copy-done
  357.9 5.1 %shard_map.181.refs_4_ = bf16[2,3200,640]{2,1,0:T(8,128)(2,1)} custom-call(s32[10]{0:T(128)S(1)} %stack.45.at_ref, bf16[2,400,640]{2,1,0:T(8,128)(2,1)S(1)} %copy-done, bf16[2,400,640]{2,1,0:T(8,128)(2,1)} %collective-permute-done.6.refs_1_, bf16[1,400,640]{2,1,0:T(8,128)(2,1)} %collective-permute-done.refs_2_, ...), custom_call_target="tpu_custom_call" | custom-call | flops 20000000 | bytes 12288000 | tf_op jit(solution)/shard_map/pallas_call | solution.py:690
  363.1 2.8 shard_map.182
  (12 shorter events, 0.0 us)
Async XLA Ops:
  306.9 14.7 %collective-permute-start = (bf16[1,400,640]{2,1,0:T(8,128)(2,1)}, bf16[1,400,640]{2,1,0:T(8,128)(2,1)}, u32[]{:S(2)}, u32[]{:S(2)}) collective-permute-start(bf16[1,400,640]{2,1,0:T(8,128)(2,1)} %get-tuple-element.44), channel_id=1, source_target_pairs={{0,2},{1,3},{2,4},{3,5},{4,6},{5,7},{6,0},{7,1},{8,10},{9,11},{10,... | collective-permute-start | bytes 1536008 | tf_op jit(solution)/shard_map/ppermute | solution.py:642
  307.3 15.9 %collective-permute-start.3 = (bf16[1,400,640]{2,1,0:T(8,128)(2,1)}, bf16[1,400,640]{2,1,0:T(8,128)(2,1)}, u32[]{:S(2)}, u32[]{:S(2)}) collective-permute-start(bf16[1,400,640]{2,1,0:T(8,128)(2,1)} %get-tuple-element.45), channel_id=1, source_target_pairs={{0,6},{1,7},{2,0},{3,1},{4,2},{5,3},{6,4},{7,5},{8,14},{9,15},{10,... | collective-permute-start | bytes 1536008 | tf_op jit(solution)/shard_map/ppermute | solution.py:645
  309.7 22.9 %collective-permute-start.9 = (bf16[1,400,640]{2,1,0:T(8,128)(2,1)}, bf16[1,400,640]{2,1,0:T(8,128)(2,1)}, u32[]{:S(2)}, u32[]{:S(2)}) collective-permute-start(bf16[1,400,640]{2,1,0:T(8,128)(2,1)} %get-tuple-element.45), channel_id=1, source_target_pairs={{0,2},{1,3},{2,4},{3,5},{4,6},{5,7},{6,0},{7,1},{8,10},{9,11},{10,... | collective-permute-start | bytes 1536008 | tf_op jit(solution)/shard_map/ppermute | solution.py:642
  309.7 34.5 %collective-permute-start.11 = (bf16[1,400,640]{2,1,0:T(8,128)(2,1)}, bf16[1,400,640]{2,1,0:T(8,128)(2,1)}, u32[]{:S(2)}, u32[]{:S(2)}) collective-permute-start(bf16[1,400,640]{2,1,0:T(8,128)(2,1)} %get-tuple-element.44), channel_id=1, source_target_pairs={{0,6},{1,7},{2,0},{3,1},{4,2},{5,3},{6,4},{7,5},{8,14},{9,15},{10,... | collective-permute-start | bytes 1536008 | tf_op jit(solution)/shard_map/ppermute | solution.py:645
  321.6 24.3 %collective-permute-start.7 = (bf16[1,400,640]{2,1,0:T(8,128)(2,1)}, bf16[1,400,640]{2,1,0:T(8,128)(2,1)}, u32[]{:S(2)}, u32[]{:S(2)}) collective-permute-start(bf16[1,400,640]{2,1,0:T(8,128)(2,1)} %collective-permute-done.refs_2_), channel_id=1, source_target_pairs={{0,1},{1,0},{2,3},{3,2},{4,5},{5,4},{6,7},{7,6},{8,9},{9,8},{10,11... | collective-permute-start | bytes 1536008 | tf_op jit(solution)/shard_map/ppermute | solution.py:648
  323.2 23.2 %collective-permute-start.1 = (bf16[1,400,640]{2,1,0:T(8,128)(2,1)}, bf16[1,400,640]{2,1,0:T(8,128)(2,1)}, u32[]{:S(2)}, u32[]{:S(2)}) collective-permute-start(bf16[1,400,640]{2,1,0:T(8,128)(2,1)} %collective-permute-done.refs_2_), channel_id=1, source_target_pairs={{0,2},{1,3},{2,4},{3,5},{4,6},{5,7},{6,0},{7,1},{8,10},{9,11},{10,... | collective-permute-start | bytes 1536008 | tf_op jit(solution)/shard_map/ppermute | solution.py:642
  323.2 22.8 %collective-permute-start.8 = (bf16[1,400,640]{2,1,0:T(8,128)(2,1)}, bf16[1,400,640]{2,1,0:T(8,128)(2,1)}, u32[]{:S(2)}, u32[]{:S(2)}) collective-permute-start(bf16[1,400,640]{2,1,0:T(8,128)(2,1)} %collective-permute-done.3.refs_4_), channel_id=1, source_target_pairs={{0,1},{1,0},{2,3},{3,2},{4,5},{5,4},{6,7},{7,6},{8,9},{9,8},{10,11... | collective-permute-start | bytes 1536008 | tf_op jit(solution)/shard_map/ppermute | solution.py:648
  332.6 13.9 %collective-permute-start.4 = (bf16[1,400,640]{2,1,0:T(8,128)(2,1)}, bf16[1,400,640]{2,1,0:T(8,128)(2,1)}, u32[]{:S(2)}, u32[]{:S(2)}) collective-permute-start(bf16[1,400,640]{2,1,0:T(8,128)(2,1)} %collective-permute-done.3.refs_4_), channel_id=1, source_target_pairs={{0,6},{1,7},{2,0},{3,1},{4,2},{5,3},{6,4},{7,5},{8,14},{9,15},{10,... | collective-permute-start | bytes 1536008 | tf_op jit(solution)/shard_map/ppermute | solution.py:645
  344.2 12.4 %collective-permute-start.6 = (bf16[2,400,640]{2,1,0:T(8,128)(2,1)}, bf16[2,400,640]{2,1,0:T(8,128)(2,1)}, u32[]{:S(2)}, u32[]{:S(2)}) collective-permute-start(bf16[2,400,640]{2,1,0:T(8,128)(2,1)} %get-tuple-element.46.refs_0_), channel_id=1, source_target_pairs={{0,1},{1,0},{2,3},{3,2},{4,5},{5,4},{6,7},{7,6},{8,9},{9,8},{10,11... | collective-permute-start | bytes 3072008 | tf_op jit(solution)/shard_map/ppermute | solution.py:648
  345.9 10.8 %collective-permute-start.10 = (bf16[1,400,640]{2,1,0:T(8,128)(2,1)}, bf16[1,400,640]{2,1,0:T(8,128)(2,1)}, u32[]{:S(2)}, u32[]{:S(2)}) collective-permute-start(bf16[1,400,640]{2,1,0:T(8,128)(2,1)} %collective-permute-done.9.refs_6_), channel_id=1, source_target_pairs={{0,1},{1,0},{2,3},{3,2},{4,5},{5,4},{6,7},{7,6},{8,9},{9,8},{10,11... | collective-permute-start | bytes 1536008 | tf_op jit(solution)/shard_map/ppermute | solution.py:648
  346.0 10.7 %collective-permute-start.12 = (bf16[1,400,640]{2,1,0:T(8,128)(2,1)}, bf16[1,400,640]{2,1,0:T(8,128)(2,1)}, u32[]{:S(2)}, u32[]{:S(2)}) collective-permute-start(bf16[1,400,640]{2,1,0:T(8,128)(2,1)} %collective-permute-done.11.refs_8_), channel_id=1, source_target_pairs={{0,1},{1,0},{2,3},{3,2},{4,5},{5,4},{6,7},{7,6},{8,9},{9,8},{10,11... | collective-permute-start | bytes 1536008 | tf_op jit(solution)/shard_map/ppermute | solution.py:648
  346.4 16.6 %collective-permute-start.2 = (bf16[1,400,640]{2,1,0:T(8,128)(2,1)}, bf16[1,400,640]{2,1,0:T(8,128)(2,1)}, u32[]{:S(2)}, u32[]{:S(2)}) collective-permute-start(bf16[1,400,640]{2,1,0:T(8,128)(2,1)} %collective-permute-done.1.refs_0_), channel_id=1, source_target_pairs={{0,1},{1,0},{2,3},{3,2},{4,5},{5,4},{6,7},{7,6},{8,9},{9,8},{10,11... | collective-permute-start | bytes 1536008 | tf_op jit(solution)/shard_map/ppermute | solution.py:648
  346.5 16.5 %collective-permute-start.5 = (bf16[1,400,640]{2,1,0:T(8,128)(2,1)}, bf16[1,400,640]{2,1,0:T(8,128)(2,1)}, u32[]{:S(2)}, u32[]{:S(2)}) collective-permute-start(bf16[1,400,640]{2,1,0:T(8,128)(2,1)} %collective-permute-done.4.refs_2_), channel_id=1, source_target_pairs={{0,1},{1,0},{2,3},{3,2},{4,5},{5,4},{6,7},{7,6},{8,9},{9,8},{10,11... | collective-permute-start | bytes 1536008 | tf_op jit(solution)/shard_map/ppermute | solution.py:648
  356.7 1.2 copy-start

commit v6 on v5

--- a/solution.py
+++ b/solution.py
@@ -44,106 +44,13 @@
         c.wait()
 
 
-def gate_up_tiles(z, layer_of, wg_ref, wu_ref, wgu, sem):
-    def copies(t):
-        slot = lax.rem(t, 2)
-        return [
-            copy(ref.at[layer_of(t), :, span(lax.rem(t, z.NT), z.W)], wgu.at[slot, :, pl.ds(e * z.W, z.W)], sem.at[slot, e])
-            for e, ref in enumerate((wg_ref, wu_ref))
-        ]
-
-    return copies
-
-
-def forward_kernel(z, x_ref, dy_ref, wg_ref, wu_ref, wd_ref, h1_ref, a1_ref, a1T_ref, a0_ref, a0T_ref, dyT_ref, hid_ref,
-                   x, a, a1, aT, cT, h1, dy, dyT, wgu, wd, hid, gu0, gu1, wsem, dsem, hsem, tsem):
-    W, CH, NT, NC, T = z.W, z.CH, z.NT, z.NC, z.T
-    gus = (gu0, gu1)
-    tiles = gate_up_tiles(z, lambda t: 0, wg_ref, wu_ref, wgu, wsem)
-    states, later, down = copy(x_ref.at[0], x, dsem.at[0]), copy(dy_ref.at[0], dy, dsem.at[1]), copy(wd_ref.at[0], wd, dsem.at[2])
-    start(states, *tiles(0), later)
-    wait(states)
-    step = CH // 2
-    for i in range(T // step):
-        r = pl.ds(i * step, step)
-        h = x[r, :].astype(F32)
-        a[r, :] = (h * scale_of(h)).astype(BF16)
-    pairs = (a, a0_ref), (aT, a0T_ref), (dyT, dyT_ref)
-    whole = [copy(s, d, tsem.at[0, e]) for e, (s, d) in enumerate(pairs)]
-    wait(later)
-
-    def hid_out(t):
-        return copy(hid.at[:, span(t, W)], hid_ref.at[0, t], hsem.at[t])
-
-    @pl.loop(0, NT)
-    def _(t):
-        wait(*tiles(t))
-
-        @pl.when(t + 1 < NT)
-        def _():
-            start(*tiles(t + 1))
-
-        @pl.when(t == 1)
-        def _():
-            start(down)
-
-        turned = span(jnp.minimum(t, NC - 1), CH)
-        aT[:, turned] = a[turned, :].T
-        dyT[:, turned] = dy[turned, :].T
-
-        def E(c):
-            g, u = gus[c % 2][0], gus[c % 2][1]
-            hid[pl.ds(c * CH, CH), span(t, W)] = (g * sigmoid(g) * u).astype(BF16)
-
-        for c in range(NC):
-            gu = dot(a[pl.ds(c * CH, CH), :], wgu[lax.rem(t, 2)])
-            gus[c % 2][0] = gu[:, :W]
-            gus[c % 2][1] = gu[:, W:]
-            if c:
-                E(c - 1)
-        E(NC - 1)
-        start(hid_out(t))
-
-    start(*whole)
-    wait(down)
-
-    def project(i):
-        r = span(i, CH)
-        h1[r, :] = x[r, :] + dot(hid[r, :], wd[...]).astype(BF16)
-
-    def norm(i):
-        r = span(i, CH)
-        h = h1[r, :].astype(F32)
-        n = (h * scale_of(h)).astype(BF16)
-        a1[r, :] = n
-        cT[:, r] = n.T
-
-    def done(i):
-        r = span(i, CH)
-        parts = (h1.at[r], h1_ref.at[r]), (a1.at[r], a1_ref.at[r]), (cT.at[:, r], a1T_ref.at[:, r])
-        return [copy(s, d, tsem.at[1 + i, e]) for e, (s, d) in enumerate(parts)]
-
-    project(0)
-
-    @pl.loop(1, NC)
-    def _(i):
-        norm(i - 1)
-        project(i)
-        start(*done(i - 1))
-
-    norm(NC - 1)
-    start(*done(NC - 1))
-    wait(*whole, *[d for i in range(NC) for d in done(i)], *[hid_out(t) for t in range(NT)])
-
-
-def backward_kernel(z, h1_ref, a1_ref, a1T_ref, a0_ref, a0T_ref, dyT_ref, dy_ref, wg_ref, wu_ref, wd_ref,
-                    mg_ref, vg_ref, mu_ref, vu_ref, md_ref, vd_ref, _,
-                    gg_out, gup_out, gd_out, fac_out, nd_ref, n0_ref, n1_ref, og_ref, ou_ref, hid_ref,
+def step_kernel(z, x_ref, dy_ref, wg_ref, wu_ref, wd_ref, mg_ref, vg_ref, mu_ref, vu_ref, md_ref, vd_ref,
+                    gg_out, gup_out, gd_out, fac_out, nd_ref, n0_ref, n1_ref, og_ref, ou_ref, hid_ref, h1_ref, a0_ref, a0T_ref,
                     a, aT, dy, dyT, wgu, wd, gu0, gu1, gu2, gu3, dh0, dh1, hids, dgu,
                     G, PB, OB, B1, B2, gg_ref, gup_ref, gd_ref, fac_ref, ssacc, ssall,
                     wsem, dsem, tsem, hsem, sP, rP, sO, rO, s1, r1, s2, r2, sS, rS,
                     msem, nsem, lsem, sR, rR, sL, rL, sX, rX, sD, rD):
-    W, CH, NT, NC, D, R, NS = z.W, z.CH, z.NT, z.NC, z.D, z.R, z.NS
+    W, CH, NT, NC, T, D, R, NS = z.W, z.CH, z.NT, z.NC, z.T, z.D, z.R, z.NS
     NA = 6
     peers = 2 * z.chips
     gus, dhs = (gu0, gu1, gu2, gu3), (dh0, dh1)
@@ -241,14 +148,10 @@
 
         stages[stage](lambda f: pl.loop(0, NS)(lambda i: f(NA + i, lax.rem(i + layer, 2) * 2 - 1, put(i))))
 
-    def layer_of(r):
-        return 1 - r // NT
-
-    tiles = gate_up_tiles(z, layer_of, wg_ref, wu_ref, wgu, wsem)
-
-    def down(r):
-        slot = lax.rem(r, 2)
-        return copy(wd_ref.at[layer_of(r), span(lax.rem(r, NT), W), :], wd.at[slot], dsem.at[slot])
+    def tiles(g):
+        slot, layer, t = lax.rem(g, 2), lax.rem(g // NT, 2), lax.rem(g, NT)
+        sides = [copy(ref.at[layer, :, span(t, W)], wgu.at[slot, :, pl.ds(e * W, W)], wsem.at[slot, e]) for e, ref in enumerate((wg_ref, wu_ref))]
+        return [*sides, copy(wd_ref.at[layer, span(t, W), :], wd.at[slot], dsem.at[slot])]
 
     def hid_out(t):
         return copy(hids.at[0], hid_ref.at[1, t], hsem.at[0])
@@ -321,23 +224,84 @@
         stream_a(2, NT - 1)
         stream_b(1, 1)
 
-    first = [copy(a1_ref, a, tsem.at[0]), copy(dy_ref.at[0], dy, tsem.at[1]), copy(a1T_ref, aT, tsem.at[2]), copy(dyT_ref, dyT, tsem.at[3])]
-    start(first[0], *tiles(0), down(0), first[1])
+    ins = [copy(x_ref.at[0], dgu.at[:, pl.ds(0, W)], tsem.at[0]), copy(dy_ref.at[0], dy, tsem.at[1])]
+    start(ins[0], *tiles(0), ins[1])
     ssacc[...] = jnp.zeros_like(ssacc)
     for ci in range(NC):
         da_at(ci)[...] = jnp.zeros((CH, D), F32)
-    wait(*first[:2])
-    start(*first[2:])
+    wait(ins[0])
+    step = CH // 2
+    for i in range(T // step):
+        rows = pl.ds(i * step, step)
+        h = dgu[rows, :W].astype(F32)
+        a[rows, :] = (h * scale_of(h)).astype(BF16)
+    keep_a, keep_aT = copy(a, a0_ref, tsem.at[0]), copy(aT, a0T_ref, tsem.at[2])
+    start(keep_a)
+    wait(ins[1])
+
+    def first_out(t):
+        return copy(hids.at[lax.rem(t, 2)], hid_ref.at[0, t], hsem.at[lax.rem(t, 2)])
+
+    @pl.loop(0, NT)
+    def _(t):
+        slot = lax.rem(t, 2)
+        wait(*tiles(t))
+        start(*tiles(t + 1))
+
+        @pl.when(t >= 2)
+        def _():
+            wait(first_out(t - 2))
+
+        turned = span(jnp.minimum(t, NC - 1), CH)
+        aT[:, turned] = a[turned, :].T
+        dyT[:, turned] = dy[turned, :].T
+
+        def E(ci):
+            rows = pl.ds(ci * CH, CH)
+            g, u = gus[ci % 2][0], gus[ci % 2][1]
+            hids[slot, rows, :] = (g * sigmoid(g) * u).astype(BF16)
+            da_at(ci)[...] += dot(hids[slot, rows, :], wd[slot])
+
+        for ci in range(NC):
+            gu = dot(a[pl.ds(ci * CH, CH), :], wgu[slot])
+            gus[ci % 2][0] = gu[:, :W]
+            gus[ci % 2][1] = gu[:, W:]
+            if ci:
+                E(ci - 1)
+        E(NC - 1)
+        start(first_out(t))
+
+    start(keep_aT)
+    wait(keep_a)
+    for i, ref in enumerate((gu2, gu3)):
+        @pl.loop(0, 2)
+        def _(j):
+            rows = span(i * 2 + j, CH)
+            y = dgu[rows, :W] + ref[j].astype(BF16)
+            dgu[rows, W:] = y
+            h = y.astype(F32)
+            a[rows, :] = (h * scale_of(h)).astype(BF16)
+            ref[j] = jnp.zeros((CH, D), F32)
+
+    keep_h = copy(dgu.at[:, pl.ds(W, W)], h1_ref, tsem.at[3])
+    start(keep_h)
+    wait(keep_aT)
+
+    @pl.loop(0, NC)
+    def _(i):
+        aT[:, span(i, CH)] = a[span(i, CH), :].T
+
+    wait(keep_h, first_out(NT - 2), first_out(NT - 1))
 
     @pl.loop(0, 2 * NT)
     def _(r):
-        slot = lax.rem(r, 2)
-
-        wait(*tiles(r), down(r))
+        g = r + NT
+        slot = lax.rem(g, 2)
+        wait(*tiles(g))
 
         @pl.when(r + 1 < 2 * NT)
         def _():
-            start(*tiles(r + 1), down(r + 1))
+            start(*tiles(g + 1))
 
         @pl.when((r >= 1) & (r < NT))
         def _():
@@ -368,7 +332,6 @@
         @pl.when(r == 0)
         def _():
             pl.semaphore_wait(bar, peers - 1)
-            wait(*first[2:])
 
         usual = (r != NT) & (r != NT + 2)
 
@@ -656,29 +619,22 @@
         NT, NC, R = FF // W, T // CH, D // n
         NS = FF // n // R
         z = SimpleNamespace(T=T, D=D, FF=FF, W=W, CH=CH, NT=NT, NC=NC, R=R, NS=NS, chips=chips, count=float(sum(w.size for w in weights)))
-        tokens, turned, hidden = ((T, D), BF16, HBM), ((D, T), BF16, HBM), ((layers, NT, T, W), BF16, HBM)
-        h1, a1, a1T, a0, a0T, dyT, hid = call(
-            functools.partial(forward_kernel, z), [HBM] * 5,
-            [tokens, tokens, turned, tokens, turned, turned, hidden],
-            [*[bf16(T, D)] * 3, *[bf16(D, T)] * 2, *[bf16(T, D)] * 2, bf16(D, T), bf16(2, D, 2 * W), bf16(FF, D), bf16(T, FF), *[f32(2, CH, W)] * 2,
-             dma((2, 2)), dma((3,)), dma((NT,)), dma((NC + 1, 3))],
-            (6 * T * D * FF, 8 * T * FF),
-        )(x, dy, wg, wu, wd)
+        tokens = (T, D), BF16, HBM
         slots = 6 + NS
         blocks = bf16(slots, R, W)
         flat, tall, half, gathered = (layers, R, FF), (layers, NS * R, D), (1, NS * R, D), (layers, D, FF)
-        gg, gup, gd, fac, nd, n0, n1, og, ou, _ = call(
-            functools.partial(backward_kernel, z), [HBM] * 17,
+        gg, gup, gd, fac, nd, n0, n1, og, ou, *_ = call(
+            functools.partial(step_kernel, z), [HBM] * 11,
             [(flat, BF16, HBM), (flat, BF16, HBM), (tall, BF16, HBM), ((8, 128), F32, HBM), (tall, BF16, HBM), (half, BF16, HBM), (half, BF16, HBM),
-             (gathered, BF16, HBM), (gathered, BF16, HBM), hidden],
+             (gathered, BF16, HBM), (gathered, BF16, HBM), ((layers, NT, T, W), BF16, HBM), tokens, tokens, ((D, T), BF16, HBM)],
             [bf16(T, D), bf16(D, T), bf16(T, D), bf16(D, T), bf16(2, D, 2 * W), bf16(2, W, D), *[f32(2, CH, W)] * 4, *[bf16(CH, W)] * 2,
              bf16(2, T, W), bf16(T, 2 * W),
              bf16(slots, chips, 2, R, W), bf16(slots, chips, R, W), blocks, blocks, blocks, bf16(*flat), bf16(*flat), bf16(*tall), f32(8, 128),
              f32(8, W), f32(n, 8, 128),
              dma((2, 2)), dma((2,)), dma((4,)), dma((2,)), *[dma((slots,))] * 8, dma((n,)), dma((n,)),
              *[dma((4,))] * 9, *[dma((4, 4))] * 2],
-            (24 * T * D * FF, 8 * T * FF), collective_id=0, has_side_effects=True, input_output_aliases={16: 9},
-        )(h1, a1, a1T, a0, a0T, dyT, dy, wg, wu, wd, m[0], v[0], m[1], v[1], m[2], v[2], hid)
+            (30 * T * D * FF, 8 * T * FF), collective_id=0, has_side_effects=True,
+        )(x, dy, wg, wu, wd, m[0], v[0], m[1], v[1], m[2], v[2])
 
         me = lax.axis_index("dp")
         c, k = me // 2, lax.rem(me, 2)

time: 366 us -> 365 us (level)
    pallas_call x2 -> x1, Pallas kernels: 306 us -> 304 us  [step(): call(functools.partial(step_kernel, z), [HBM] * 11, [(flat, BF16, HBM), (...]
where the time goes in v6:
time: 365 us; the launch traced here: 364 us
  Pallas kernels  333 us (91%)
  waiting for transfers between devices  17.4 us (5%)
  starting transfers between devices  11.5 us (3%)
    pallas_call x1, Pallas kernels, step(): call(functools.partial(step_kernel, z), [HBM] * 11, [(flat, BF16, HBM), (...  304 us
    ppermute x3, waiting for transfers between devices, right(): return lax.ppermute(t, 'dp', ring(1))  17.4 us
    pallas_call x1, Pallas kernels, step(): call(copy_kernel, [HBM] * 2, [parts] * 2, [bf16(8, rows // 4, FF), dma((8...  11.6 us
    pallas_call x1, Pallas kernels, step(): call(moments_kernel, [pl.BlockSpec((8, 128), lambda i: (0, 0))] + [spec f...  9.47 us
    pallas_call x2, Pallas kernels, place(): call(functools.partial(place_kernel, [first for _, _, first in pieces]),...  7.98 us
  transfers between devices with their start and end apart: 13, of which 2 were waited for; matrix products, arithmetic and copies ran while one was open for 0% of the time, Pallas kernels for 7%

profile of v6, /device:TPU:113, one launch (start us, length us, event | category | flops | bytes accessed | tf_op | source)
XLA Modules:
  0.0 364.4 jit_solution(727742041887436534)
XLA Ops:
  0.6 304.1 %shard_map.178 = (bf16[2,80,3200]{2,1,0:T(8,128)(2,1)}, bf16[2,80,3200]{2,1,0:T(8,128)(2,1)}, bf16[2,400,640]{2,1,0:T(8,128)(2,1)}, f32[8,128]{1,0:T(8,128)}, bf...) custom-call(bf16[1,2048,640]{2,1,0:T(8,128)(2,1)} %x_ref.1, ...), custom_call_target="tpu_custom_call" | custom-call | flops 125829120000 | bytes 52428800 | tf_op jit(solution)/shard_map/pallas_call | solution.py:626
  304.7 0.4 collective-permute-start
  305.1 2.4 collective-permute-start.3
  307.5 2.7 collective-permute-start.11
  310.2 1.3 collective-permute-start.6
  311.4 8.0 %collective-permute-done.refs_2_ = bf16[1,400,640]{2,1,0:T(8,128)(2,1)} collective-permute-done((bf16[1,400,640]{2,1,0:T(8,128)(2,1)}, bf16[1,400,640]{2,1,0:T(8,128)(2,1)}, u32[]{:S(2)}, u32[]{:S(2)}) %collective-permute-start) | collective-permute-done | bytes 512032 | tf_op jit(solution)/shard_map/ppermute | solution.py:605
  319.4 1.6 collective-permute-start.7
  321.0 9.4 %collective-permute-done.9.refs_6_ = bf16[1,400,640]{2,1,0:T(8,128)(2,1)} collective-permute-done((bf16[1,400,640]{2,1,0:T(8,128)(2,1)}, bf16[1,400,640]{2,1,0:T(8,128)(2,1)}, u32[]{:S(2)}, u32[]{:S(2)}) %collective-permute-start.9) | collective-permute-done | bytes 512032 | tf_op jit(solution)/shard_map/ppermute | solution.py:605
  330.4 11.6 %shard_map.179 = (bf16[1280,3200]{1,0:T(8,128)(2,1)}, bf16[1280,3200]{1,0:T(8,128)(2,1)}) custom-call(bf16[1280,3200]{1,0:T(8,128)(2,1)} %bitcast.14, bf16[1280,3200]{1,0:T(8,128)(2,1)} %bitcast.15), custom_call_target="tpu_custom_call" | custom-call | flops 12000000000 | bytes 32768000 | tf_op jit(solution)/shard_map/pallas_call | solution.py:660
  342.0 0.0 collective-permute-done.11.refs_8_
  342.0 1.7 collective-permute-start.8
  343.7 0.0 collective-permute-done.1.refs_0_
  343.7 0.1 collective-permute-start.10
  343.8 1.0 collective-permute-start.12
  344.8 0.0 collective-permute-done.6.refs_1_
  344.8 0.0 collective-permute-start.2
  344.8 0.5 collective-permute-start.5
  345.3 9.5 %shard_map.182 = (f32[2,80,3200]{2,1,0:T(8,128)}, f32[2,80,3200]{2,1,0:T(8,128)}, f32[2,80,3200]{2,1,0:T(8,128)}, f32[2,80,3200]{2,1,0:T(8,128)}, f32[2,400,640]{2,1,0:T(8,128)}, /*index=5*/f32[2,400,640]{2,1,0:T(8,128)}) custom-call(f32[8,128]{1,0:T(8,128)} %get-tuple-element.33.fac_ref, f32[2,80,3200]{2,1,0:T(8,128)} %refs_0_.1, f32[2,80,3200]{2,1,0:T(8,128)} %refs_1_.1, ...), custom_call_target="tpu_custom_call" | custom-call | flops 10000000000 | bytes 27648000 | tf_op jit(solution)/shard_map/pallas_call | solution.py:665
  354.8 0.1 stack.45.at_ref
  354.9 0.1 pad_add_fusion.at_ref
  355.0 0.0 collective-permute-done.12.refs_9_
  355.0 1.2 copy-done
  356.2 5.1 %shard_map.180.refs_4_ = bf16[2,3200,640]{2,1,0:T(8,128)(2,1)} custom-call(s32[10]{0:T(128)S(1)} %stack.45.at_ref, bf16[2,400,640]{2,1,0:T(8,128)(2,1)S(1)} %copy-done, bf16[2,400,640]{2,1,0:T(8,128)(2,1)} %collective-permute-done.6.refs_1_, bf16[1,400,640]{2,1,0:T(8,128)(2,1)} %collective-permute-done.refs_2_, ...), custom_call_target="tpu_custom_call" | custom-call | flops 20000000 | bytes 12288000 | tf_op jit(solution)/shard_map/pallas_call | solution.py:646
  361.4 2.8 shard_map.181
  (11 shorter events, 0.0 us)
Async XLA Ops:
  304.7 14.7 %collective-permute-start = (bf16[1,400,640]{2,1,0:T(8,128)(2,1)}, bf16[1,400,640]{2,1,0:T(8,128)(2,1)}, u32[]{:S(2)}, u32[]{:S(2)}) collective-permute-start(bf16[1,400,640]{2,1,0:T(8,128)(2,1)} %get-tuple-element.30), channel_id=1, source_target_pairs={{0,2},{1,3},{2,4},{3,5},{4,6},{5,7},{6,0},{7,1},{8,10},{9,11},{10,... | collective-permute-start | bytes 1536008 | tf_op jit(solution)/shard_map/ppermute | solution.py:605
  305.1 14.3 %collective-permute-start.3 = (bf16[1,400,640]{2,1,0:T(8,128)(2,1)}, bf16[1,400,640]{2,1,0:T(8,128)(2,1)}, u32[]{:S(2)}, u32[]{:S(2)}) collective-permute-start(bf16[1,400,640]{2,1,0:T(8,128)(2,1)} %get-tuple-element.31), channel_id=1, source_target_pairs={{0,6},{1,7},{2,0},{3,1},{4,2},{5,3},{6,4},{7,5},{8,14},{9,15},{10,... | collective-permute-start | bytes 1536008 | tf_op jit(solution)/shard_map/ppermute | solution.py:608
  307.5 22.9 %collective-permute-start.9 = (bf16[1,400,640]{2,1,0:T(8,128)(2,1)}, bf16[1,400,640]{2,1,0:T(8,128)(2,1)}, u32[]{:S(2)}, u32[]{:S(2)}) collective-permute-start(bf16[1,400,640]{2,1,0:T(8,128)(2,1)} %get-tuple-element.31), channel_id=1, source_target_pairs={{0,2},{1,3},{2,4},{3,5},{4,6},{5,7},{6,0},{7,1},{8,10},{9,11},{10,... | collective-permute-start | bytes 1536008 | tf_op jit(solution)/shard_map/ppermute | solution.py:605
  307.5 34.5 %collective-permute-start.11 = (bf16[1,400,640]{2,1,0:T(8,128)(2,1)}, bf16[1,400,640]{2,1,0:T(8,128)(2,1)}, u32[]{:S(2)}, u32[]{:S(2)}) collective-permute-start(bf16[1,400,640]{2,1,0:T(8,128)(2,1)} %get-tuple-element.30), channel_id=1, source_target_pairs={{0,6},{1,7},{2,0},{3,1},{4,2},{5,3},{6,4},{7,5},{8,14},{9,15},{10,... | collective-permute-start | bytes 1536008 | tf_op jit(solution)/shard_map/ppermute | solution.py:608
  310.2 34.6 %collective-permute-start.6 = (bf16[2,400,640]{2,1,0:T(8,128)(2,1)}, bf16[2,400,640]{2,1,0:T(8,128)(2,1)}, u32[]{:S(2)}, u32[]{:S(2)}) collective-permute-start(bf16[2,400,640]{2,1,0:T(8,128)(2,1)} %get-tuple-element.32.refs_0_), channel_id=1, source_target_pairs={{0,1},{1,0},{2,3},{3,2},{4,5},{5,4},{6,7},{7,6},{8,9},{9,8},{10,11... | collective-permute-start | bytes 3072008 | tf_op jit(solution)/shard_map/ppermute | solution.py:611
  319.4 24.3 %collective-permute-start.1 = (bf16[1,400,640]{2,1,0:T(8,128)(2,1)}, bf16[1,400,640]{2,1,0:T(8,128)(2,1)}, u32[]{:S(2)}, u32[]{:S(2)}) collective-permute-start(bf16[1,400,640]{2,1,0:T(8,128)(2,1)} %collective-permute-done.refs_2_), channel_id=1, source_target_pairs={{0,2},{1,3},{2,4},{3,5},{4,6},{5,7},{6,0},{7,1},{8,10},{9,11},{10,... | collective-permute-start | bytes 1536008 | tf_op jit(solution)/shard_map/ppermute | solution.py:605
  319.4 25.4 %collective-permute-start.7 = (bf16[1,400,640]{2,1,0:T(8,128)(2,1)}, bf16[1,400,640]{2,1,0:T(8,128)(2,1)}, u32[]{:S(2)}, u32[]{:S(2)}) collective-permute-start(bf16[1,400,640]{2,1,0:T(8,128)(2,1)} %collective-permute-done.refs_2_), channel_id=1, source_target_pairs={{0,1},{1,0},{2,3},{3,2},{4,5},{5,4},{6,7},{7,6},{8,9},{9,8},{10,11... | collective-permute-start | bytes 1536008 | tf_op jit(solution)/shard_map/ppermute | solution.py:611
  330.4 13.4 %collective-permute-start.4 = (bf16[1,400,640]{2,1,0:T(8,128)(2,1)}, bf16[1,400,640]{2,1,0:T(8,128)(2,1)}, u32[]{:S(2)}, u32[]{:S(2)}) collective-permute-start(bf16[1,400,640]{2,1,0:T(8,128)(2,1)} %collective-permute-done.3.refs_4_), channel_id=1, source_target_pairs={{0,6},{1,7},{2,0},{3,1},{4,2},{5,3},{6,4},{7,5},{8,14},{9,15},{10,... | collective-permute-start | bytes 1536008 | tf_op jit(solution)/shard_map/ppermute | solution.py:608
  342.0 13.0 %collective-permute-start.8 = (bf16[1,400,640]{2,1,0:T(8,128)(2,1)}, bf16[1,400,640]{2,1,0:T(8,128)(2,1)}, u32[]{:S(2)}, u32[]{:S(2)}) collective-permute-start(bf16[1,400,640]{2,1,0:T(8,128)(2,1)} %collective-permute-done.3.refs_4_), channel_id=1, source_target_pairs={{0,1},{1,0},{2,3},{3,2},{4,5},{5,4},{6,7},{7,6},{8,9},{9,8},{10,11... | collective-permute-start | bytes 1536008 | tf_op jit(solution)/shard_map/ppermute | solution.py:611
  343.7 11.3 %collective-permute-start.10 = (bf16[1,400,640]{2,1,0:T(8,128)(2,1)}, bf16[1,400,640]{2,1,0:T(8,128)(2,1)}, u32[]{:S(2)}, u32[]{:S(2)}) collective-permute-start(bf16[1,400,640]{2,1,0:T(8,128)(2,1)} %collective-permute-done.9.refs_6_), channel_id=1, source_target_pairs={{0,1},{1,0},{2,3},{3,2},{4,5},{5,4},{6,7},{7,6},{8,9},{9,8},{10,11... | collective-permute-start | bytes 1536008 | tf_op jit(solution)/shard_map/ppermute | solution.py:611
  343.8 11.2 %collective-permute-start.12 = (bf16[1,400,640]{2,1,0:T(8,128)(2,1)}, bf16[1,400,640]{2,1,0:T(8,128)(2,1)}, u32[]{:S(2)}, u32[]{:S(2)}) collective-permute-start(bf16[1,400,640]{2,1,0:T(8,128)(2,1)} %collective-permute-done.11.refs_8_), channel_id=1, source_target_pairs={{0,1},{1,0},{2,3},{3,2},{4,5},{5,4},{6,7},{7,6},{8,9},{9,8},{10,11... | collective-permute-start | bytes 1536008 | tf_op jit(solution)/shard_map/ppermute | solution.py:611
  344.8 16.6 %collective-permute-start.2 = (bf16[1,400,640]{2,1,0:T(8,128)(2,1)}, bf16[1,400,640]{2,1,0:T(8,128)(2,1)}, u32[]{:S(2)}, u32[]{:S(2)}) collective-permute-start(bf16[1,400,640]{2,1,0:T(8,128)(2,1)} %collective-permute-done.1.refs_0_), channel_id=1, source_target_pairs={{0,1},{1,0},{2,3},{3,2},{4,5},{5,4},{6,7},{7,6},{8,9},{9,8},{10,11... | collective-permute-start | bytes 1536008 | tf_op jit(solution)/shard_map/ppermute | solution.py:611
  344.8 16.6 %collective-permute-start.5 = (bf16[1,400,640]{2,1,0:T(8,128)(2,1)}, bf16[1,400,640]{2,1,0:T(8,128)(2,1)}, u32[]{:S(2)}, u32[]{:S(2)}) collective-permute-start(bf16[1,400,640]{2,1,0:T(8,128)(2,1)} %collective-permute-done.4.refs_2_), channel_id=1, source_target_pairs={{0,1},{1,0},{2,3},{3,2},{4,5},{5,4},{6,7},{7,6},{8,9},{9,8},{10,11... | collective-permute-start | bytes 1536008 | tf_op jit(solution)/shard_map/ppermute | solution.py:611
  355.0 1.2 copy-start
